TPU v7x, 32 devices: a whole 2x2x4 slice. The times are simulated.
32 devices in a mesh: gx: 4 (over z), gy: 2 (over x), gz: 4 (over y, core).
Axes of the slice: x: 2, y: 2, z: 4, core: 2. Of those that a mesh axis runs over, the one named last changes fastest.
Arguments:
- old_slots: bfloat16 [4, 2, 32, 4096], P('gx', 'gy', 'gz'), may hold values from -6 to 6
- old_ids: int32 [4, 2, 32], P('gx', 'gy', 'gz'), may hold values from -1 to 31, as said below
- old_owner: int32 [4, 2, 32], P('gx', 'gy'), may hold values from 0 to 3, as said below
- coefficient: float32 [64, 32, 512], P('gx', 'gy', 'gz'), may hold values from 0.2 to 5
Outputs:
- solution: float32 [64, 32, 512], P('gx', 'gy', 'gz')
Inputs may be any that keep to these rules, and one draw needn't show every extreme that they name: old_owner[a, c, b] is the index along gz of the device that held box b of box column (a, c) before the move; no device holds more than 8 boxes of a column and some device holds exactly 8; no device holds more than 2 of the 8 boxes with one value of b // 8, and that bound is reached. old_ids[a, c, g * 8 + q] is the box held in slot q of device g of box column (a, c), or -1 for an empty slot; it agrees with old_owner and each box stands in exactly one slot.
All inputs are finite; a program needn't handle non-finite values.
Results may differ from a plain program's by a relative error of at most 0.0003.
Values may be sent and summed in bfloat16 or wider, within the bound.
No kernel may reach another device: no remote copies, remote signals or barrier semaphores. Data moves between devices by JAX's collectives and lax.ppermute only.
A program may use at most 64 MiB of HBM per device.

v0:
```python
import jax
import jax.numpy as jnp
from jax import lax
from jax.sharding import PartitionSpec as P

BOX = 16
NB = 8
SEND = 2
SWEEPS = 2


def with_halo(cells, sides, width):
    for axis, dim in sides:
        count = lax.axis_size(axis)
        ends = count - 1
        head = lax.slice_in_dim(cells, 0, width, axis=dim)
        tail = lax.slice_in_dim(cells, cells.shape[dim] - width, cells.shape[dim], axis=dim)
        cells = jnp.concatenate(
            [
                lax.ppermute(tail, axis, [(i, (i + 1) % count) for i in range(ends)]),
                cells,
                lax.ppermute(head, axis, [((i + 1) % count, i) for i in range(ends)]),
            ],
            axis=dim,
        )
    return cells


def rims(values, depth):
    return with_halo(values, (("gx", 0), ("gy", 1), ("gz", 2)), depth)


def inner(padded):
    return padded[1:-1, 1:-1, 1:-1]


def operator_parts(padded):
    face_first = 0.5 * (padded[:-1, 1:-1, 1:-1] + padded[1:, 1:-1, 1:-1])
    face_second = 0.5 * (padded[1:-1, :-1, 1:-1] + padded[1:-1, 1:, 1:-1])
    face_third = 0.5 * (padded[1:-1, 1:-1, :-1] + padded[1:-1, 1:-1, 1:])
    diagonal = (
        face_first[:-1]
        + face_first[1:]
        + face_second[:, :-1]
        + face_second[:, 1:]
        + face_third[:, :, :-1]
        + face_third[:, :, 1:]
    )
    return (face_first, face_second, face_third, diagonal)


def neighbours(padded, stencil):
    face_first, face_second, face_third, diagonal = stencil
    summed = face_first[:-1] * padded[:-2, 1:-1, 1:-1] + face_first[1:] * padded[2:, 1:-1, 1:-1]
    summed = (
        summed
        + face_second[:, :-1] * padded[1:-1, :-2, 1:-1]
        + face_second[:, 1:] * padded[1:-1, 2:, 1:-1]
    )
    summed = (
        summed
        + face_third[:, :, :-1] * padded[1:-1, 1:-1, :-2]
        + face_third[:, :, 1:] * padded[1:-1, 1:-1, 2:]
    )
    return summed


def red_cells(shape, margin):
    index_first = lax.broadcasted_iota(jnp.int32, shape, 0)
    index_second = lax.broadcasted_iota(jnp.int32, shape, 1)
    index_third = lax.broadcasted_iota(jnp.int32, shape, 2)
    return (index_first + index_second + index_third + margin) % 2 == 0


def relax(padded, source, stencil, factor, chosen):
    fresh = (factor * source + neighbours(padded, stencil)) / stencil[3]
    return jnp.where(chosen, fresh, inner(padded))


def apply_operator(values, stencil, factor):
    return (stencil[3] * values - neighbours(rims(values, 1), stencil)) / factor


def sweep_thin(values, source, stencil, factor, red_mask, starting):
    if starting:
        values = jnp.where(red_mask, factor * source / stencil[3], 0.0)
    else:
        values = relax(rims(values, 1), source, stencil, factor, red_mask)
    return relax(rims(values, 1), source, stencil, factor, jnp.logical_not(red_mask))


def smooth_thin(values, source, stencil, factor, starting):
    red_mask = red_cells(source.shape, 0)
    for counter in range(SWEEPS):
        values = sweep_thin(values, source, stencil, factor, red_mask, starting and counter == 0)
    return values


def sweep_deep(
    values, source_rim, stencil_rim, stencil_block, factor, red_rim, black_block, starting
):
    if starting:
        coloured = jnp.where(red_rim, factor * source_rim / stencil_rim[3], 0.0)
    else:
        coloured = relax(rims(values, 2), source_rim, stencil_rim, factor, red_rim)
    return relax(coloured, inner(source_rim), stencil_block, factor, black_block)


def coarsen(values):
    extent_first, extent_second, extent_third = values.shape
    grouped = values.reshape(extent_first // 2, 2, extent_second // 2, 2, extent_third // 2, 2)
    return grouped.mean(axis=(1, 3, 5))


def refine(values):
    return jnp.repeat(jnp.repeat(jnp.repeat(values, 2, axis=0), 2, axis=1), 2, axis=2)


def dot_pair(first_term, second_term):
    return lax.psum((first_term, second_term), ("gx", "gy", "gz"))


def bottom_solve(rhs_low, stencil, factor):
    image_low = apply_operator(rhs_low, stencil, factor)
    norm_rhs, along_rhs = dot_pair(jnp.sum(rhs_low * rhs_low), jnp.sum(rhs_low * image_low))
    alpha_step = norm_rhs / along_rhs
    rest_low = rhs_low - alpha_step * image_low
    turned = apply_operator(rest_low, stencil, factor)
    turned_rest, turned_norm = dot_pair(jnp.sum(turned * rest_low), jnp.sum(turned * turned))
    omega_step = turned_rest / turned_norm
    return alpha_step * rhs_low + omega_step * rest_low


def move_boxes(old_slots, old_ids, old_owner):
    slot_rows = old_slots.reshape(old_slots.shape[2], old_slots.shape[3])
    slot_ids = old_ids.reshape(-1)
    owner_map = old_owner.reshape(-1)
    groups = lax.axis_size("gz")
    my_index = lax.axis_index("gz")
    capacity = slot_ids.shape[0]
    filled = slot_ids >= 0
    target = jnp.where(filled, slot_ids // NB, -1)
    earlier = (
        (target[None, :] == target[:, None])
        & (slot_ids[None, :] < slot_ids[:, None])
        & filled[None, :]
    )
    ranking = jnp.sum(earlier.astype(jnp.int32), axis=1)
    send_row = jnp.where(filled, target * SEND + ranking, -1)
    picker = lax.broadcasted_iota(jnp.int32, (groups * SEND, capacity), 0) == send_row[None, :]
    outgoing = jnp.dot(
        picker.astype(jnp.bfloat16), slot_rows, preferred_element_type=jnp.float32
    ).astype(jnp.bfloat16)
    incoming = lax.all_to_all(outgoing, "gz", split_axis=0, concat_axis=0, tiled=True).astype(
        jnp.float32
    )
    arriving = lax.dynamic_slice_in_dim(owner_map, my_index * NB, NB)
    later_index = lax.broadcasted_iota(jnp.int32, (NB, NB), 0)
    before = (arriving[None, :] == arriving[:, None]) & (
        lax.broadcasted_iota(jnp.int32, (NB, NB), 1) < later_index
    )
    order_within = jnp.sum(before.astype(jnp.int32), axis=1)
    chosen_boxes = jnp.take(incoming, arriving * SEND + order_within, axis=0)
    stacked = chosen_boxes.reshape(NB, BOX, BOX, BOX).transpose(1, 2, 0, 3)
    return stacked.reshape(BOX, BOX, NB * BOX)


def per_device(old_slots, old_ids, old_owner, coefficient):
    source_fine = move_boxes(old_slots, old_ids, old_owner)
    coefficient_rim = rims(coefficient, 2)
    inside = inner(coefficient_rim) > 0.0
    face_first, face_second, face_third, diagonal = operator_parts(coefficient_rim)
    stencil_rim = (face_first, face_second, face_third, jnp.where(inside, diagonal, 1.0))
    stencil_fine = (inner(face_first), inner(face_second), inner(face_third), inner(diagonal))
    source_rim = rims(source_fine, 1)
    red_rim = jnp.logical_and(red_cells(inside.shape, 1), inside)
    black_fine = jnp.logical_not(red_cells(source_fine.shape, 0))

    def smooth_fine(values, starting):
        for counter in range(SWEEPS):
            values = sweep_deep(
                values,
                source_rim,
                stencil_rim,
                stencil_fine,
                1.0,
                red_rim,
                black_fine,
                starting and counter == 0,
            )
        return values

    fine_values = smooth_fine(jnp.zeros_like(source_fine), True)
    residual_fine = source_fine - apply_operator(fine_values, stencil_fine, 1.0)
    coefficient_mid = coarsen(coefficient)
    stencil_mid = operator_parts(rims(coefficient_mid, 1))
    source_mid = coarsen(residual_fine)
    middle_values = smooth_thin(jnp.zeros_like(source_mid), source_mid, stencil_mid, 4.0, True)
    residual_mid = source_mid - apply_operator(middle_values, stencil_mid, 4.0)
    coefficient_low = coarsen(coefficient_mid)
    stencil_low = operator_parts(rims(coefficient_low, 1))
    bottom_values = bottom_solve(coarsen(residual_mid), stencil_low, 16.0)
    middle_values = smooth_thin(
        middle_values + refine(bottom_values), source_mid, stencil_mid, 4.0, False
    )
    return smooth_fine(fine_values + refine(middle_values), False)


def solution(mesh):
    in_specs = (
        P("gx", "gy", "gz", None),
        P("gx", "gy", "gz"),
        P("gx", "gy", None),
        P("gx", "gy", "gz"),
    )
    out_specs = P("gx", "gy", "gz")
    return jax.shard_map(
        per_device, mesh=mesh, in_specs=in_specs, out_specs=out_specs, check_vma=False
    )
```

profile of v0, /device:TPU:0, one launch (start us, length us, event | category | flops | bytes accessed | tf_op | source)
XLA Modules:
  0.0 546.6 jit_solution(12764030653669933789)
XLA Ops:
  2.1 5.6 %collective-permute-start = (f32[2,16,128]{2,1,0:T(8,128)S(1)}, f32[2,16,128]{2,1,0:T(8,128)S(1)}, u32[]{:S(2)}, u32[]{:S(2)}) collective-permute-start(f32[2,16,128]{2,1,0:T(8,128)S(1)} %get-tuple-element.52), channel_id=1, source_target_pairs={{0,8},{8,16},{16,24},{1,9},{9,17},{17,25},{2,10},{10,18},{18,26},{... | collective-permute-start | bytes 49160 | tf_op jit(solution)/shard_map/ppermute | solution.py:20
  14.7 10.6 %reshape.184 = f32[8,2,8,2,64,2]{5,4,3,2,1,0:T(8,128)} reshape(f32[16,16,128]{2,1,0:T(8,128)} %param.7) | data formatting | bytes 262144 | tf_op jit(solution)/shard_map/reshape | solution.py:111
  30.0 4.5 collective-permute-start.24
  41.1 4.2 collective-permute-done.3
  48.1 4.3 collective-permute-done.5
  54.5 4.5 collective-permute-start.6
  61.1 4.2 collective-permute-done.7
  91.7 4.1 collective-permute-start.14
  112.9 4.5 collective-permute-start.18
  118.8 6.2 %collective-permute-start.28 = (f32[10,10,1]{2,1,0:T(8,128)S(1)}, f32[10,10,1]{2,1,0:T(8,128)S(1)}, u32[]{:S(2)}, u32[]{:S(2)}) collective-permute-start(f32[10,10,1]{2,1,0:T(8,128)S(1)} %get-tuple-element.69), channel_id=1, source_target_pairs={{0,1},{1,2},{2,3},{4,5},{5,6},{6,7},{8,9},{9,10},{10,11},{12,13},{... | collective-permute-start | bytes 1208 | tf_op jit(solution)/shard_map/ppermute | solution.py:20
  129.4 4.2 collective-permute-done.21
  141.5 9.8 %reshape.183 = f32[8,2,8,2,64,2]{5,4,3,2,1,0:T(8,128)} reshape(f32[16,16,128]{2,1,0:T(8,128)S(1)} %fusion.55) | data formatting | bytes 262144 | tf_op jit(solution)/shard_map/reshape | solution.py:111
  155.5 4.5 collective-permute-start.30
  161.4 4.2 collective-permute-done.31
  168.5 4.2 collective-permute-done.33
  177.6 4.1 collective-permute-done.35
  185.6 4.2 collective-permute-done.37
  192.8 4.2 collective-permute-done.39
  200.5 4.2 collective-permute-done.41
  215.3 4.2 collective-permute-done.45
  227.3 4.3 collective-permute-start.48
  242.2 4.2 collective-permute-done.51
  249.5 5.9 %collective-permute-done.53 = f32[10,10,1]{2,1,0:T(8,128)S(1)} collective-permute-done((f32[10,10,1]{2,1,0:T(8,128)S(1)}, f32[10,10,1]{2,1,0:T(8,128)S(1)}, u32[]{:S(2)}, u32[]{:S(2)}) %collective-permute-start.53) | collective-permute-done | bytes 432 | tf_op jit(solution)/shard_map/ppermute | solution.py:22
  256.8 4.5 collective-permute-start.60
  262.7 4.7 collective-permute-start.58
  283.9 41.1 %all-reduce.1 = (f32[]{:T(128)}, f32[]{:T(128)}) all-reduce(f32[]{:T(128)} %get-tuple-element.8, f32[]{:T(128)} %get-tuple-element.7), channel_id=1, replica_groups=mesh['gx'=4,'gy'=2,'gz'=4] {'gx','gy','gz'}, use_global_device_ids=true, to_apply=%region_6.7 | all-reduce | flops 2 | bytes 16 | tf_op jit(solution)/shard_map/psum | solution.py:120
  329.5 4.2 collective-permute-done.67
  333.7 4.2 collective-permute-start.68
  339.2 4.2 collective-permute-done.69
  346.1 4.3 collective-permute-done.71
  351.1 39.8 %all-reduce = (f32[]{:T(128)}, f32[]{:T(128)}) all-reduce(f32[]{:T(128)} %get-tuple-element.6, f32[]{:T(128)} %get-tuple-element.5), channel_id=1, replica_groups=mesh['gx'=4,'gy'=2,'gz'=4] {'gx','gy','gz'}, use_global_device_ids=true, to_apply=%region_11.12 | all-reduce | flops 2 | bytes 16 | tf_op jit(solution)/shard_map/psum | solution.py:120
  396.5 4.2 collective-permute-done.73
  400.7 4.2 collective-permute-start.74
  406.2 4.2 collective-permute-done.75
  413.1 4.4 collective-permute-done.77
  421.6 4.2 collective-permute-done.79
  428.8 4.2 collective-permute-done.81
  446.1 4.2 collective-permute-done.85
  453.3 4.2 collective-permute-done.87
  461.0 4.2 collective-permute-done.89
  468.6 4.2 collective-permute-done.91
  475.8 4.2 collective-permute-done.93
  495.5 4.2 collective-permute-done.97
  502.8 4.2 collective-permute-done.99
  510.7 4.4 collective-permute-done.101
  521.7 4.2 collective-permute-done.103
  529.0 4.2 collective-permute-done.105
  538.4 4.3 collective-permute-done.107
  (362 shorter events, 248.0 us)
Async XLA Ops:
  0.8 35.4 %collective-permute-start.1 = (f32[2,16,128]{2,1,0:T(8,128)S(1)}, f32[2,16,128]{2,1,0:T(8,128)S(1)}, u32[]{:S(2)}, u32[]{:S(2)}) collective-permute-start(f32[2,16,128]{2,1,0:T(8,128)S(1)} %get-tuple-element.51), channel_id=1, source_target_pairs={{8,0},{16,8},{24,16},{9,1},{17,9},{25,17},{10,2},{18,10},{26,18},{... | collective-permute-start | bytes 49160 | tf_op jit(solution)/shard_map/ppermute | solution.py:22
  2.1 34.0 %collective-permute-start = (f32[2,16,128]{2,1,0:T(8,128)S(1)}, f32[2,16,128]{2,1,0:T(8,128)S(1)}, u32[]{:S(2)}, u32[]{:S(2)}) collective-permute-start(f32[2,16,128]{2,1,0:T(8,128)S(1)} %get-tuple-element.52), channel_id=1, source_target_pairs={{0,8},{8,16},{16,24},{1,9},{9,17},{17,25},{2,10},{10,18},{18,26},{... | collective-permute-start | bytes 49160 | tf_op jit(solution)/shard_map/ppermute | solution.py:20
  11.4 41.3 %all-to-all-start = ((bf16[4,2,4096]{2,1,0:T(2,128)(2,1)}), bf16[4,2,4096]{2,1,0:T(2,128)(2,1)S(1)}, u32[]{:S(2)}, u32[]{:S(2)}) async-start(bf16[4,2,4096]{2,1,0:T(2,128)(2,1)} %all_to_all.6), calls=%async_computation | async-start | bytes 131072 | tf_op jit(solution)/shard_map/all_to_all | solution.py:154
  30.0 57.4 %collective-permute-start.24 = (f32[1,8,64]{2,1,0:T(8,128)}, f32[1,8,64]{2,1,0:T(8,128)}, u32[]{:S(2)}, u32[]{:S(2)}) collective-permute-start(f32[1,8,64]{2,1,0:T(8,128)} %get-tuple-element.105), channel_id=1, source_target_pairs={{0,8},{8,16},{16,24},{1,9},{9,17},{17,25},{2,10},{10,18},{18,26},{... | collective-permute-start | bytes 6152 | tf_op jit(solution)/shard_map/ppermute | solution.py:20
  34.5 52.9 %collective-permute-start.25 = (f32[1,8,64]{2,1,0:T(8,128)}, f32[1,8,64]{2,1,0:T(8,128)}, u32[]{:S(2)}, u32[]{:S(2)}) collective-permute-start(f32[1,8,64]{2,1,0:T(8,128)} %get-tuple-element.106), channel_id=1, source_target_pairs={{8,0},{16,8},{24,16},{9,1},{17,9},{25,17},{10,2},{18,10},{26,18},{... | collective-permute-start | bytes 6152 | tf_op jit(solution)/shard_map/ppermute | solution.py:22
  39.6 5.7 %collective-permute-start.3 = (f32[20,2,128]{2,1,0:T(2,128)S(1)}, f32[20,2,128]{2,1,0:T(2,128)S(1)}, u32[]{:S(2)}, u32[]{:S(2)}) collective-permute-start(f32[20,2,128]{2,1,0:T(2,128)S(1)} %get-tuple-element.38), channel_id=1, source_target_pairs={{4,0},{5,1},{6,2},{7,3},{12,8},{13,9},{14,10},{15,11},{20,16},{21,... | collective-permute-start | bytes 61448 | tf_op jit(solution)/shard_map/ppermute | solution.py:22
  46.8 5.6 %collective-permute-start.5 = (f32[20,20,2]{2,1,0:T(8,128)S(1)}, f32[20,20,2]{2,1,0:T(8,128)S(1)}, u32[]{:S(2)}, u32[]{:S(2)}) collective-permute-start(f32[20,20,2]{2,1,0:T(8,128)S(1)} %get-tuple-element.26), channel_id=1, source_target_pairs={{1,0},{2,1},{3,2},{5,4},{6,5},{7,6},{9,8},{10,9},{11,10},{13,12},{... | collective-permute-start | bytes 9608 | tf_op jit(solution)/shard_map/ppermute | solution.py:22
  54.5 6.5 %collective-permute-start.6 = (f32[1,16,128]{2,1,0:T(8,128)S(1)}, f32[1,16,128]{2,1,0:T(8,128)S(1)}, u32[]{:S(2)}, u32[]{:S(2)}) collective-permute-start(f32[1,16,128]{2,1,0:T(8,128)S(1)} %slice.1002), channel_id=1, source_target_pairs={{0,8},{8,16},{16,24},{1,9},{9,17},{17,25},{2,10},{10,18},{18,26},{... | collective-permute-start | bytes 24584 | tf_op jit(solution)/shard_map/ppermute | solution.py:20
  59.7 5.5 %collective-permute-start.7 = (f32[1,16,128]{2,1,0:T(8,128)S(1)}, f32[1,16,128]{2,1,0:T(8,128)S(1)}, u32[]{:S(2)}, u32[]{:S(2)}) collective-permute-start(f32[1,16,128]{2,1,0:T(8,128)S(1)} %slice.1004), channel_id=1, source_target_pairs={{8,0},{16,8},{24,16},{9,1},{17,9},{25,17},{10,2},{18,10},{26,18},{... | collective-permute-start | bytes 24584 | tf_op jit(solution)/shard_map/ppermute | solution.py:22
  66.9 5.6 %collective-permute-start.9 = (f32[18,1,128]{2,1,0:T(1,128)S(1)}, f32[18,1,128]{2,1,0:T(1,128)S(1)}, u32[]{:S(2)}, u32[]{:S(2)}) collective-permute-start(f32[18,1,128]{2,1,0:T(1,128)S(1)} %get-tuple-element.42), channel_id=1, source_target_pairs={{4,0},{5,1},{6,2},{7,3},{12,8},{13,9},{14,10},{15,11},{20,16},{21,... | collective-permute-start | bytes 27656 | tf_op jit(solution)/shard_map/ppermute | solution.py:22
  76.3 5.6 %collective-permute-start.11 = (f32[18,18,1]{2,1,0:T(8,128)S(1)}, f32[18,18,1]{2,1,0:T(8,128)S(1)}, u32[]{:S(2)}, u32[]{:S(2)}) collective-permute-start(f32[18,18,1]{2,1,0:T(8,128)S(1)} %get-tuple-element.30), channel_id=1, source_target_pairs={{1,0},{2,1},{3,2},{5,4},{6,5},{7,6},{9,8},{10,9},{11,10},{13,12},{... | collective-permute-start | bytes 3896 | tf_op jit(solution)/shard_map/ppermute | solution.py:22
  83.1 8.1 %collective-permute-start.12 = (f32[2,16,128]{2,1,0:T(8,128)S(1)}, f32[2,16,128]{2,1,0:T(8,128)S(1)}, u32[]{:S(2)}, u32[]{:S(2)}) collective-permute-start(f32[2,16,128]{2,1,0:T(8,128)S(1)} %get-tuple-element.49), channel_id=1, source_target_pairs={{0,8},{8,16},{16,24},{1,9},{9,17},{17,25},{2,10},{10,18},{18,26},{... | collective-permute-start | bytes 49160 | tf_op jit(solution)/shard_map/ppermute | solution.py:20
  86.1 5.6 %collective-permute-start.13 = (f32[2,16,128]{2,1,0:T(8,128)S(1)}, f32[2,16,128]{2,1,0:T(8,128)S(1)}, u32[]{:S(2)}, u32[]{:S(2)}) collective-permute-start(f32[2,16,128]{2,1,0:T(8,128)S(1)} %get-tuple-element.50), channel_id=1, source_target_pairs={{8,0},{16,8},{24,16},{9,1},{17,9},{25,17},{10,2},{18,10},{26,18},{... | collective-permute-start | bytes 49160 | tf_op jit(solution)/shard_map/ppermute | solution.py:22
  88.2 18.7 %collective-permute-start.26 = (f32[10,1,64]{2,1,0:T(1,128)S(1)}, f32[10,1,64]{2,1,0:T(1,128)S(1)}, u32[]{:S(2)}, u32[]{:S(2)}) collective-permute-start(f32[10,1,64]{2,1,0:T(1,128)S(1)} %get-tuple-element.87), channel_id=1, source_target_pairs={{0,4},{1,5},{2,6},{3,7},{8,12},{9,13},{10,14},{11,15},{16,20},{17,... | collective-permute-start | bytes 7688 | tf_op jit(solution)/shard_map/ppermute | solution.py:20
  89.9 17.1 %collective-permute-start.27 = (f32[10,1,64]{2,1,0:T(1,128)S(1)}, f32[10,1,64]{2,1,0:T(1,128)S(1)}, u32[]{:S(2)}, u32[]{:S(2)}) collective-permute-start(f32[10,1,64]{2,1,0:T(1,128)S(1)} %get-tuple-element.88), channel_id=1, source_target_pairs={{4,0},{5,1},{6,2},{7,3},{12,8},{13,9},{14,10},{15,11},{20,16},{21,... | collective-permute-start | bytes 7688 | tf_op jit(solution)/shard_map/ppermute | solution.py:22
  91.7 6.2 %collective-permute-start.14 = (f32[20,2,128]{2,1,0:T(2,128)S(1)}, f32[20,2,128]{2,1,0:T(2,128)S(1)}, u32[]{:S(2)}, u32[]{:S(2)}) collective-permute-start(f32[20,2,128]{2,1,0:T(2,128)S(1)} %get-tuple-element.35), channel_id=1, source_target_pairs={{0,4},{1,5},{2,6},{3,7},{8,12},{9,13},{10,14},{11,15},{16,20},{17,... | collective-permute-start | bytes 61448 | tf_op jit(solution)/shard_map/ppermute | solution.py:20
  95.8 5.7 %collective-permute-start.15 = (f32[20,2,128]{2,1,0:T(2,128)S(1)}, f32[20,2,128]{2,1,0:T(2,128)S(1)}, u32[]{:S(2)}, u32[]{:S(2)}) collective-permute-start(f32[20,2,128]{2,1,0:T(2,128)S(1)} %get-tuple-element.36), channel_id=1, source_target_pairs={{4,0},{5,1},{6,2},{7,3},{12,8},{13,9},{14,10},{15,11},{20,16},{21,... | collective-permute-start | bytes 61448 | tf_op jit(solution)/shard_map/ppermute | solution.py:22
  101.6 6.2 %collective-permute-start.16 = (f32[20,20,2]{2,1,0:T(8,128)S(1)}, f32[20,20,2]{2,1,0:T(8,128)S(1)}, u32[]{:S(2)}, u32[]{:S(2)}) collective-permute-start(f32[20,20,2]{2,1,0:T(8,128)S(1)} %get-tuple-element.23), channel_id=1, source_target_pairs={{0,1},{1,2},{2,3},{4,5},{5,6},{6,7},{8,9},{9,10},{10,11},{12,13},{... | collective-permute-start | bytes 9608 | tf_op jit(solution)/shard_map/ppermute | solution.py:20
  112.9 13.5 %collective-permute-start.18 = (f32[1,16,128]{2,1,0:T(8,128)S(1)}, f32[1,16,128]{2,1,0:T(8,128)S(1)}, u32[]{:S(2)}, u32[]{:S(2)}) collective-permute-start(f32[1,16,128]{2,1,0:T(8,128)S(1)} %get-tuple-element.47), channel_id=1, source_target_pairs={{0,8},{8,16},{16,24},{1,9},{9,17},{17,25},{2,10},{10,18},{18,26},{... | collective-permute-start | bytes 24584 | tf_op jit(solution)/shard_map/ppermute | solution.py:20
  117.5 8.9 %collective-permute-start.19 = (f32[1,16,128]{2,1,0:T(8,128)S(1)}, f32[1,16,128]{2,1,0:T(8,128)S(1)}, u32[]{:S(2)}, u32[]{:S(2)}) collective-permute-start(f32[1,16,128]{2,1,0:T(8,128)S(1)} %get-tuple-element.48), channel_id=1, source_target_pairs={{8,0},{16,8},{24,16},{9,1},{17,9},{25,17},{10,2},{18,10},{26,18},{... | collective-permute-start | bytes 24584 | tf_op jit(solution)/shard_map/ppermute | solution.py:22
  118.8 18.1 %collective-permute-start.28 = (f32[10,10,1]{2,1,0:T(8,128)S(1)}, f32[10,10,1]{2,1,0:T(8,128)S(1)}, u32[]{:S(2)}, u32[]{:S(2)}) collective-permute-start(f32[10,10,1]{2,1,0:T(8,128)S(1)} %get-tuple-element.69), channel_id=1, source_target_pairs={{0,1},{1,2},{2,3},{4,5},{5,6},{6,7},{8,9},{9,10},{10,11},{12,13},{... | collective-permute-start | bytes 1208 | tf_op jit(solution)/shard_map/ppermute | solution.py:20
  125.1 11.8 %collective-permute-start.29 = (f32[10,10,1]{2,1,0:T(8,128)S(1)}, f32[10,10,1]{2,1,0:T(8,128)S(1)}, u32[]{:S(2)}, u32[]{:S(2)}) collective-permute-start(f32[10,10,1]{2,1,0:T(8,128)S(1)} %get-tuple-element.70), channel_id=1, source_target_pairs={{1,0},{2,1},{3,2},{5,4},{6,5},{7,6},{9,8},{10,9},{11,10},{13,12},{... | collective-permute-start | bytes 1208 | tf_op jit(solution)/shard_map/ppermute | solution.py:22
  128.1 5.6 %collective-permute-start.21 = (f32[18,1,128]{2,1,0:T(1,128)S(1)}, f32[18,1,128]{2,1,0:T(1,128)S(1)}, u32[]{:S(2)}, u32[]{:S(2)}) collective-permute-start(f32[18,1,128]{2,1,0:T(1,128)S(1)} %get-tuple-element.40), channel_id=1, source_target_pairs={{4,0},{5,1},{6,2},{7,3},{12,8},{13,9},{14,10},{15,11},{20,16},{21,... | collective-permute-start | bytes 27656 | tf_op jit(solution)/shard_map/ppermute | solution.py:22
  135.4 5.6 %collective-permute-start.23 = (f32[18,18,1]{2,1,0:T(8,128)S(1)}, f32[18,18,1]{2,1,0:T(8,128)S(1)}, u32[]{:S(2)}, u32[]{:S(2)}) collective-permute-start(f32[18,18,1]{2,1,0:T(8,128)S(1)} %get-tuple-element.28), channel_id=1, source_target_pairs={{1,0},{2,1},{3,2},{5,4},{6,5},{7,6},{9,8},{10,9},{11,10},{13,12},{... | collective-permute-start | bytes 3896 | tf_op jit(solution)/shard_map/ppermute | solution.py:22
  155.5 5.9 %collective-permute-start.30 = (f32[1,8,64]{2,1,0:T(8,128)S(1)}, f32[1,8,64]{2,1,0:T(8,128)S(1)}, u32[]{:S(2)}, u32[]{:S(2)}) collective-permute-start(f32[1,8,64]{2,1,0:T(8,128)S(1)} %get-tuple-element.103), channel_id=1, source_target_pairs={{0,8},{8,16},{16,24},{1,9},{9,17},{17,25},{2,10},{10,18},{18,26},{... | collective-permute-start | bytes 6152 | tf_op jit(solution)/shard_map/ppermute | solution.py:20
  167.2 5.5 %collective-permute-start.33 = (f32[10,1,64]{2,1,0:T(1,128)S(1)}, f32[10,1,64]{2,1,0:T(1,128)S(1)}, u32[]{:S(2)}, u32[]{:S(2)}) collective-permute-start(f32[10,1,64]{2,1,0:T(1,128)S(1)} %get-tuple-element.86), channel_id=1, source_target_pairs={{4,0},{5,1},{6,2},{7,3},{12,8},{13,9},{14,10},{15,11},{20,16},{21,... | collective-permute-start | bytes 7688 | tf_op jit(solution)/shard_map/ppermute | solution.py:22
  191.5 5.5 %collective-permute-start.39 = (f32[10,1,64]{2,1,0:T(1,128)S(1)}, f32[10,1,64]{2,1,0:T(1,128)S(1)}, u32[]{:S(2)}, u32[]{:S(2)}) collective-permute-start(f32[10,1,64]{2,1,0:T(1,128)S(1)} %get-tuple-element.84), channel_id=1, source_target_pairs={{4,0},{5,1},{6,2},{7,3},{12,8},{13,9},{14,10},{15,11},{20,16},{21,... | collective-permute-start | bytes 7688 | tf_op jit(solution)/shard_map/ppermute | solution.py:22
  213.9 5.5 %collective-permute-start.45 = (f32[10,1,64]{2,1,0:T(1,128)S(1)}, f32[10,1,64]{2,1,0:T(1,128)S(1)}, u32[]{:S(2)}, u32[]{:S(2)}) collective-permute-start(f32[10,1,64]{2,1,0:T(1,128)S(1)} %get-tuple-element.82), channel_id=1, source_target_pairs={{4,0},{5,1},{6,2},{7,3},{12,8},{13,9},{14,10},{15,11},{20,16},{21,... | collective-permute-start | bytes 7688 | tf_op jit(solution)/shard_map/ppermute | solution.py:22
  219.6 7.4 %collective-permute-start.46 = (f32[10,10,1]{2,1,0:T(8,128)S(1)}, f32[10,10,1]{2,1,0:T(8,128)S(1)}, u32[]{:S(2)}, u32[]{:S(2)}) collective-permute-start(f32[10,10,1]{2,1,0:T(8,128)S(1)} %get-tuple-element.63), channel_id=1, source_target_pairs={{0,1},{1,2},{2,3},{4,5},{5,6},{6,7},{8,9},{9,10},{10,11},{12,13},{... | collective-permute-start | bytes 1208 | tf_op jit(solution)/shard_map/ppermute | solution.py:20
  223.0 10.0 %collective-permute-start.54 = (f32[1,4,32]{2,1,0:T(4,128)S(1)}, f32[1,4,32]{2,1,0:T(4,128)S(1)}, u32[]{:S(2)}, u32[]{:S(2)}) collective-permute-start(f32[1,4,32]{2,1,0:T(4,128)S(1)} %get-tuple-element.121), channel_id=1, source_target_pairs={{0,8},{8,16},{16,24},{1,9},{9,17},{17,25},{2,10},{10,18},{18,26},{... | collective-permute-start | bytes 1544 | tf_op jit(solution)/shard_map/ppermute | solution.py:20
  225.5 7.5 %collective-permute-start.55 = (f32[1,4,32]{2,1,0:T(4,128)S(1)}, f32[1,4,32]{2,1,0:T(4,128)S(1)}, u32[]{:S(2)}, u32[]{:S(2)}) collective-permute-start(f32[1,4,32]{2,1,0:T(4,128)S(1)} %get-tuple-element.122), channel_id=1, source_target_pairs={{8,0},{16,8},{24,16},{9,1},{17,9},{25,17},{10,2},{18,10},{26,18},{... | collective-permute-start | bytes 1544 | tf_op jit(solution)/shard_map/ppermute | solution.py:22
  227.3 9.0 %collective-permute-start.48 = (f32[1,8,64]{2,1,0:T(8,128)S(1)}, f32[1,8,64]{2,1,0:T(8,128)S(1)}, u32[]{:S(2)}, u32[]{:S(2)}) collective-permute-start(f32[1,8,64]{2,1,0:T(8,128)S(1)} %get-tuple-element.97), channel_id=1, source_target_pairs={{0,8},{8,16},{16,24},{1,9},{9,17},{17,25},{2,10},{10,18},{18,26},{... | collective-permute-start | bytes 6152 | tf_op jit(solution)/shard_map/ppermute | solution.py:20
  233.0 16.4 %collective-permute-start.56 = (f32[6,1,32]{2,1,0:T(1,128)S(1)}, f32[6,1,32]{2,1,0:T(1,128)S(1)}, u32[]{:S(2)}, u32[]{:S(2)}) collective-permute-start(f32[6,1,32]{2,1,0:T(1,128)S(1)} %get-tuple-element.115), channel_id=1, source_target_pairs={{0,4},{1,5},{2,6},{3,7},{8,12},{9,13},{10,14},{11,15},{16,20},{17,... | collective-permute-start | bytes 2312 | tf_op jit(solution)/shard_map/ppermute | solution.py:20
  235.0 14.5 %collective-permute-start.57 = (f32[6,1,32]{2,1,0:T(1,128)S(1)}, f32[6,1,32]{2,1,0:T(1,128)S(1)}, u32[]{:S(2)}, u32[]{:S(2)}) collective-permute-start(f32[6,1,32]{2,1,0:T(1,128)S(1)} %get-tuple-element.116), channel_id=1, source_target_pairs={{4,0},{5,1},{6,2},{7,3},{12,8},{13,9},{14,10},{15,11},{20,16},{21,... | collective-permute-start | bytes 2312 | tf_op jit(solution)/shard_map/ppermute | solution.py:22
  240.9 5.5 %collective-permute-start.51 = (f32[10,1,64]{2,1,0:T(1,128)S(1)}, f32[10,1,64]{2,1,0:T(1,128)S(1)}, u32[]{:S(2)}, u32[]{:S(2)}) collective-permute-start(f32[10,1,64]{2,1,0:T(1,128)S(1)} %get-tuple-element.80), channel_id=1, source_target_pairs={{4,0},{5,1},{6,2},{7,3},{12,8},{13,9},{14,10},{15,11},{20,16},{21,... | collective-permute-start | bytes 7688 | tf_op jit(solution)/shard_map/ppermute | solution.py:22
  248.2 7.2 %collective-permute-start.53 = (f32[10,10,1]{2,1,0:T(8,128)S(1)}, f32[10,10,1]{2,1,0:T(8,128)S(1)}, u32[]{:S(2)}, u32[]{:S(2)}) collective-permute-start(f32[10,10,1]{2,1,0:T(8,128)S(1)} %get-tuple-element.62), channel_id=1, source_target_pairs={{1,0},{2,1},{3,2},{5,4},{6,5},{7,6},{9,8},{10,9},{11,10},{13,12},{... | collective-permute-start | bytes 1208 | tf_op jit(solution)/shard_map/ppermute | solution.py:22
  256.8 11.9 %collective-permute-start.60 = (f32[1,4,32]{2,1,0:T(4,128)S(1)}, f32[1,4,32]{2,1,0:T(4,128)S(1)}, u32[]{:S(2)}, u32[]{:S(2)}) collective-permute-start(f32[1,4,32]{2,1,0:T(4,128)S(1)} %get-tuple-element.123), channel_id=1, source_target_pairs={{0,8},{8,16},{16,24},{1,9},{9,17},{17,25},{2,10},{10,18},{18,26},{... | collective-permute-start | bytes 1544 | tf_op jit(solution)/shard_map/ppermute | solution.py:20
  261.4 7.4 %collective-permute-start.61 = (f32[1,4,32]{2,1,0:T(4,128)S(1)}, f32[1,4,32]{2,1,0:T(4,128)S(1)}, u32[]{:S(2)}, u32[]{:S(2)}) collective-permute-start(f32[1,4,32]{2,1,0:T(4,128)S(1)} %get-tuple-element.124), channel_id=1, source_target_pairs={{8,0},{16,8},{24,16},{9,1},{17,9},{25,17},{10,2},{18,10},{26,18},{... | collective-permute-start | bytes 1544 | tf_op jit(solution)/shard_map/ppermute | solution.py:22
  262.7 16.2 %collective-permute-start.58 = (f32[6,6,1]{2,1,0:T(8,128)S(1)}, f32[6,6,1]{2,1,0:T(8,128)S(1)}, u32[]{:S(2)}, u32[]{:S(2)}) collective-permute-start(f32[6,6,1]{2,1,0:T(8,128)S(1)} %get-tuple-element.109), channel_id=1, source_target_pairs={{0,1},{1,2},{2,3},{4,5},{5,6},{6,7},{8,9},{9,10},{10,11},{12,13},{... | collective-permute-start | bytes 440 | tf_op jit(solution)/shard_map/ppermute | solution.py:20
  267.4 11.5 %collective-permute-start.59 = (f32[6,6,1]{2,1,0:T(8,128)S(1)}, f32[6,6,1]{2,1,0:T(8,128)S(1)}, u32[]{:S(2)}, u32[]{:S(2)}) collective-permute-start(f32[6,6,1]{2,1,0:T(8,128)S(1)} %get-tuple-element.110), channel_id=1, source_target_pairs={{1,0},{2,1},{3,2},{5,4},{6,5},{7,6},{9,8},{10,9},{11,10},{13,12},{... | collective-permute-start | bytes 440 | tf_op jit(solution)/shard_map/ppermute | solution.py:22
  344.8 5.6 %collective-permute-start.71 = (f32[6,6,1]{2,1,0:T(8,128)S(1)}, f32[6,6,1]{2,1,0:T(8,128)S(1)}, u32[]{:S(2)}, u32[]{:S(2)}) collective-permute-start(f32[6,6,1]{2,1,0:T(8,128)S(1)} %get-tuple-element.108), channel_id=1, source_target_pairs={{1,0},{2,1},{3,2},{5,4},{6,5},{7,6},{9,8},{10,9},{11,10},{13,12},{... | collective-permute-start | bytes 440 | tf_op jit(solution)/shard_map/ppermute | solution.py:22
  411.8 5.7 %collective-permute-start.77 = (f32[10,10,1]{2,1,0:T(8,128)S(1)}, f32[10,10,1]{2,1,0:T(8,128)S(1)}, u32[]{:S(2)}, u32[]{:S(2)}) collective-permute-start(f32[10,10,1]{2,1,0:T(8,128)S(1)} %get-tuple-element.60), channel_id=1, source_target_pairs={{1,0},{2,1},{3,2},{5,4},{6,5},{7,6},{9,8},{10,9},{11,10},{13,12},{... | collective-permute-start | bytes 1208 | tf_op jit(solution)/shard_map/ppermute | solution.py:22
  494.1 5.6 %collective-permute-start.97 = (f32[2,16,128]{2,1,0:T(8,128)S(1)}, f32[2,16,128]{2,1,0:T(8,128)S(1)}, u32[]{:S(2)}, u32[]{:S(2)}) collective-permute-start(f32[2,16,128]{2,1,0:T(8,128)S(1)} %get-tuple-element.46), channel_id=1, source_target_pairs={{8,0},{16,8},{24,16},{9,1},{17,9},{25,17},{10,2},{18,10},{26,18},{... | collective-permute-start | bytes 49160 | tf_op jit(solution)/shard_map/ppermute | solution.py:22
  501.4 5.7 %collective-permute-start.99 = (f32[20,2,128]{2,1,0:T(2,128)S(1)}, f32[20,2,128]{2,1,0:T(2,128)S(1)}, u32[]{:S(2)}, u32[]{:S(2)}) collective-permute-start(f32[20,2,128]{2,1,0:T(2,128)S(1)} %get-tuple-element.34), channel_id=1, source_target_pairs={{4,0},{5,1},{6,2},{7,3},{12,8},{13,9},{14,10},{15,11},{20,16},{21,... | collective-permute-start | bytes 61448 | tf_op jit(solution)/shard_map/ppermute | solution.py:22
  509.4 5.7 %collective-permute-start.101 = (f32[20,20,2]{2,1,0:T(8,128)S(1)}, f32[20,20,2]{2,1,0:T(8,128)S(1)}, u32[]{:S(2)}, u32[]{:S(2)}) collective-permute-start(f32[20,20,2]{2,1,0:T(8,128)S(1)} %get-tuple-element.22), channel_id=1, source_target_pairs={{1,0},{2,1},{3,2},{5,4},{6,5},{7,6},{9,8},{10,9},{11,10},{13,12},{... | collective-permute-start | bytes 9608 | tf_op jit(solution)/shard_map/ppermute | solution.py:22
  520.3 5.6 %collective-permute-start.103 = (f32[2,16,128]{2,1,0:T(8,128)S(1)}, f32[2,16,128]{2,1,0:T(8,128)S(1)}, u32[]{:S(2)}, u32[]{:S(2)}) collective-permute-start(f32[2,16,128]{2,1,0:T(8,128)S(1)} %get-tuple-element.44), channel_id=1, source_target_pairs={{8,0},{16,8},{24,16},{9,1},{17,9},{25,17},{10,2},{18,10},{26,18},{... | collective-permute-start | bytes 49160 | tf_op jit(solution)/shard_map/ppermute | solution.py:22
  527.6 5.7 %collective-permute-start.105 = (f32[20,2,128]{2,1,0:T(2,128)S(1)}, f32[20,2,128]{2,1,0:T(2,128)S(1)}, u32[]{:S(2)}, u32[]{:S(2)}) collective-permute-start(f32[20,2,128]{2,1,0:T(2,128)S(1)} %get-tuple-element.32), channel_id=1, source_target_pairs={{4,0},{5,1},{6,2},{7,3},{12,8},{13,9},{14,10},{15,11},{20,16},{21,... | collective-permute-start | bytes 61448 | tf_op jit(solution)/shard_map/ppermute | solution.py:22
  537.1 5.6 %collective-permute-start.107 = (f32[20,20,2]{2,1,0:T(8,128)S(1)}, f32[20,20,2]{2,1,0:T(8,128)S(1)}, u32[]{:S(2)}, u32[]{:S(2)}) collective-permute-start(f32[20,20,2]{2,1,0:T(8,128)S(1)} %get-tuple-element.20), channel_id=1, source_target_pairs={{1,0},{2,1},{3,2},{5,4},{6,5},{7,6},{9,8},{10,9},{11,10},{13,12},{... | collective-permute-start | bytes 9608 | tf_op jit(solution)/shard_map/ppermute | solution.py:22
  (78 other events, 1148.1 us)
where the time goes:
time: 554 us; the launch traced here: 547 us
  starting transfers between devices  221 us (40%)
  waiting for transfers between devices  175 us (32%)
  blocking collectives  80.9 us (15%)
  other arithmetic  32.8 us (6%)
  local copies, waits for them, and re-layouts  31.5 us (6%)
    ppermute x54, waiting for transfers between devices, with_halo(): lax.ppermute(head, axis, [((i + 1) % count, i) for i in range(ends)])  174 us
    ppermute x54, starting transfers between devices, with_halo(): lax.ppermute(tail, axis, [(i, (i + 1) % count) for i in range(ends)])  148 us
    psum x2, blocking collectives, dot_pair(): return lax.psum((first_term, second_term), ('gx', 'gy', 'gz'))  80.9 us
    ppermute x54, starting transfers between devices, with_halo(): lax.ppermute(head, axis, [((i + 1) % count, i) for i in range(ends)])  70.3 us
    reshape x3, local copies, waits for them, and re-layouts, coarsen(): values.reshape(extent_first // 2, 2, extent_second // 2, 2, extent_third...  21.5 us
  transfers between devices with their start and end apart: 109, of which 50 were waited for; matrix products, arithmetic and copies ran while one was open for 5% of the time, Pallas kernels for 0%

commit v1 on v0

v1 whole, which is shorter than its diff:
```python
import jax
import jax.numpy as jnp
from jax import lax
from jax.experimental import pallas as pl
from jax.experimental.pallas import tpu as pltpu
from jax.sharding import PartitionSpec as P

BOX = 16
HALO = 8
LANES = 128
HIGH = lax.Precision.HIGHEST
F32 = jnp.float32
BF16 = jnp.bfloat16


def iota(shape, dim):
    return lax.broadcasted_iota(jnp.int32, shape, dim)


def exact_dot(left, right):
    return lax.dot_general(
        left, right, (((1,), (0,)), ((), ())), precision=HIGH, preferred_element_type=F32
    )


def even_rows(shape, dims):
    total = iota(shape, dims[0])
    for dim in dims[1:]:
        total = total + iota(shape, dim)
    return total % 2 == 0


def call(kernel, outs, scratch=(), **more):
    return pl.pallas_call(
        kernel,
        out_shape=outs,
        scratch_shapes=list(scratch),
        compiler_params=pltpu.CompilerParams(vmem_limit_bytes=48 * 1024 * 1024),
        **more,
    )


def shape_f32(*dims):
    return jax.ShapeDtypeStruct(dims, F32)


class Geometry:
    def __init__(self, sizes, block):
        self.gx, self.gy, self.gz = sizes
        self.bx, self.by, self.bz = block
        self.swap = self.gy == 2
        self.wx = self.bx + 2 * HALO
        self.wy = self.by + (HALO if self.swap else 2 * HALO)

    def own_y(self):
        if self.swap:
            return pl.multiple_of(lax.axis_index("gy") * HALO, HALO)
        return HALO

    def halo_y(self):
        if self.swap:
            return (pl.multiple_of((1 - lax.axis_index("gy")) * self.by, HALO),)
        return (0, HALO + self.by)


def neighbours_of(axis, count, step):
    if step > 0:
        return [(i, i + 1) for i in range(count - 1)]
    return [(i + 1, i) for i in range(count - 1)]


def pack_coefficient(geo, own, before, after):
    bx, by, bz = geo.bx, geo.by, geo.bz
    half = bz // 2

    def kernel(own_ref, before_ref, after_ref, out_ref, *sends):
        rows = bx * by
        lane = iota((rows, bz), 1)
        mine = own_ref[...].reshape(rows, bz)
        near = jnp.where(
            lane < half, after_ref[...].reshape(rows, bz), before_ref[...].reshape(rows, bz)
        )
        source = iota((bz, LANES), 0)
        target = iota((bz, LANES), 1)

        def pick(shift):
            low = (source == 2 * target + shift).astype(F32)
            high = (source == 2 * target + shift - bz).astype(F32)
            return exact_dot(mine, low) + exact_dot(near, high)

        even = pick(0).reshape(bx, by, LANES)
        odd = pick(1).reshape(bx, by, LANES)
        first = even_rows((bx, by, LANES), (0, 1))
        out_ref[0] = jnp.where(first, even, odd)
        out_ref[1] = jnp.where(first, odd, even)
        emit_sends(geo, out_ref, sends)

    return call(kernel, [shape_f32(2, bx, by, LANES)] + send_shapes(geo))(own, before, after)


def send_shapes(geo):
    one = shape_f32(2, geo.bx, HALO, LANES)
    return [one] if geo.swap else [one, one]


def emit_sends(geo, out_ref, sends):
    top = geo.by - HALO
    if geo.swap:
        start = pl.multiple_of((1 - lax.axis_index("gy")) * top, HALO)
        sends[0][...] = out_ref[:, :, pl.ds(start, HALO), :]
    else:
        sends[0][...] = out_ref[:, :, 0:HALO, :]
        sends[1][...] = out_ref[:, :, top : top + HALO, :]


def pack_source(geo, slots, cells):
    bx, by = geo.bx, geo.by
    count = slots.shape[0]
    tiles = cells // LANES
    boxes = 2 * geo.bz // BOX
    own_boxes = geo.bz // BOX
    per_tile = LANES // BOX
    pair = BOX // 2

    def kernel(slot_ref, out_ref, *rest):
        sends, ordered = rest[:-1], rest[-1]
        ids = slot_ref[:, cells : cells + LANES].astype(F32)
        place = iota((count, LANES), 1)
        wanted = jnp.where(place < own_boxes + own_boxes // 2, place, place - boxes)
        wanted = (wanted + lax.axis_index("gz") * own_boxes).astype(F32)
        chosen = jnp.where((ids == wanted) & (ids >= 0.0) & (place < boxes), 1.0, 0.0)
        chosen = chosen.T[0:boxes].astype(BF16)
        for tile in range(tiles):
            ordered[tile] = jnp.dot(
                chosen,
                slot_ref[:, tile * LANES : (tile + 1) * LANES],
                preferred_element_type=F32,
            )
        rows = tiles * per_tile
        keep = iota((tiles, per_tile, LANES), 2) // BOX == iota((tiles, per_tile, LANES), 1)
        inside = iota((LANES, 2 * LANES), 0) % BOX
        target = iota((LANES, 2 * LANES), 1)
        slot_of = jnp.where(
            inside % 2 == 0, inside // 2, inside // 2 + LANES
        )
        total = jnp.zeros((rows, 2 * LANES), F32)
        for box in range(boxes):
            line = jnp.broadcast_to(ordered[:, box : box + 1, :], (tiles, per_tile, LANES))
            line = jnp.where(keep, line, 0.0).reshape(rows, LANES).astype(BF16)
            spread = (target == slot_of + box * pair).astype(F32).astype(BF16)
            total = total + jnp.dot(line, spread, preferred_element_type=F32)
        even = total[:, 0:LANES].reshape(bx, by, LANES)
        odd = total[:, LANES:].reshape(bx, by, LANES)
        first = even_rows((bx, by, LANES), (0, 1))
        out_ref[0] = jnp.where(first, even, odd)
        out_ref[1] = jnp.where(first, odd, even)
        emit_sends(geo, out_ref, sends)

    return call(
        kernel,
        [shape_f32(2, bx, by, LANES)] + send_shapes(geo),
        [pltpu.VMEM((tiles, boxes, LANES), F32)],
    )(slots)


def exchange_y(geo, sends):
    if geo.swap:
        return (lax.ppermute(sends[0], "gy", [(0, 1), (1, 0)]),)
    low, high = sends
    return (
        lax.ppermute(high, "gy", neighbours_of("gy", geo.gy, 1)),
        lax.ppermute(low, "gy", neighbours_of("gy", geo.gy, -1)),
    )


def widen_y(geo, own, halos):
    half = geo.bx // 2

    def kernel(own_ref, *rest):
        halo_refs, outs = rest[:-2], rest[-2:]
        for part, out in enumerate(outs):
            span = slice(part * half, (part + 1) * half)
            out[:, :, pl.ds(geo.own_y(), geo.by), :] = own_ref[:, span]
            for halo, start in zip(halo_refs, geo.halo_y()):
                out[:, :, pl.ds(start, HALO), :] = halo[:, span]

    slab = shape_f32(2, half, geo.wy, LANES)
    return call(kernel, [slab, slab])(own, *halos)


def exchange_x(geo, low, high):
    return (
        lax.ppermute(high, "gx", neighbours_of("gx", geo.gx, 1)),
        lax.ppermute(low, "gx", neighbours_of("gx", geo.gx, -1)),
    )


PAD = 8


def fine_sum(geo, ref, row, near_low):
    rows = slice(PAD, PAD + geo.wy)
    here = ref[row, rows, :]
    total = ref[row - 1, rows, :] + ref[row + 1, rows, :] + here
    total = total + ref[row, PAD - 1 : PAD - 1 + geo.wy, :]
    total = total + ref[row, PAD + 1 : PAD + 1 + geo.wy, :]
    low = pltpu.roll(here, 1, 1)
    high = pltpu.roll(here, LANES - 1, 1)
    return total + jnp.where(near_low, low, high)


def fine_rows(geo, body):
    even = iota((geo.wy, LANES), 0) % 2 == 0
    odd = jnp.logical_not(even)

    def step(index, carry):
        body(2 * index + 1, 2 * index, even)
        body(2 * index + 2, 2 * index + 1, odd)
        return carry

    lax.fori_loop(0, geo.wx // 2, step, 0)


def fine_half(geo, colour, coeff, weight, source, values, scaled, extra=None):
    other = 1 - colour

    def body(row, cell, low):
        near_low = low if colour == 0 else jnp.logical_not(low)
        rows = slice(PAD, PAD + geo.wy)
        mine = coeff[colour][row, rows, :]
        summed = mine * fine_sum(geo, values[other], row, near_low)
        summed = summed + fine_sum(geo, scaled[other], row, near_low)
        fresh = weight[colour][cell] * (source[colour][cell] + summed)
        values[colour][row, rows, :] = fresh
        scaled[colour][row, rows, :] = mine * fresh

    fine_rows(geo, body)


def clear_pads(geo, ref):
    blank_row = jnp.zeros((geo.wy + 2 * PAD, LANES), F32)
    ref[0] = blank_row
    ref[geo.wx + 1] = blank_row
    edge = jnp.zeros((geo.wx + 2, PAD, LANES), F32)
    ref[:, 0:PAD, :] = edge
    ref[:, PAD + geo.wy : PAD + geo.wy + PAD, :] = edge


def fine_scratch(geo):
    return pltpu.VMEM((geo.wx + 2, geo.wy + 2 * PAD, LANES), F32)


def fine_before(geo, coefficient, source):
    half = geo.bx // 2
    wx, wy = geo.wx, geo.wy
    cx, cy = geo.bx // 2, geo.by // 2

    def kernel(*refs):
        coeff_in, source_in = refs[0:4], refs[4:8]
        coarse_ref, out_black, out_coeff, out_weight, out_source = refs[8:13]
        kr, kb, vr, vb, wr, wb, diag, resid = refs[13:]
        coeff, values, scaled = (kr, kb), (vr, vb), (wr, wb)
        rows = slice(PAD, PAD + wy)
        for ref in (kr, kb, vr, vb, wr, wb):
            clear_pads(geo, ref)
        start = 0
        for slab, slab_source in zip(coeff_in, source_in):
            depth = slab.shape[1]
            for colour in (0, 1):
                scaled_slab = 0.5 * slab[colour]
                coeff[colour][1 + start : 1 + start + depth, rows, :] = scaled_slab
                out_coeff[colour, start : start + depth] = scaled_slab
                out_source[colour, start : start + depth] = slab_source[colour]
            start += depth
        weight = (out_weight.at[0], out_weight.at[1])
        source_at = (out_source.at[0], out_source.at[1])

        def first_red(row, cell, low):
            mine = kr[row, rows, :]
            total = 6.0 * mine + fine_sum(geo, kb, row, low)
            inverse = jnp.where(mine > 0.0, 1.0 / total, 0.0)
            diag[cell] = total
            out_weight[0, cell] = inverse
            fresh = inverse * out_source[0, cell]
            vr[row, rows, :] = fresh
            wr[row, rows, :] = mine * fresh

        fine_rows(geo, first_red)

        def first_black(row, cell, low):
            high = jnp.logical_not(low)
            mine = kb[row, rows, :]
            total = 6.0 * mine + fine_sum(geo, kr, row, high)
            inverse = jnp.where(mine > 0.0, 1.0 / total, 0.0)
            out_weight[1, cell] = inverse

        fine_rows(geo, first_black)
        fine_half(geo, 1, coeff, weight, source_at, values, scaled)
        fine_half(geo, 0, coeff, weight, source_at, values, scaled)
        fine_half(geo, 1, coeff, weight, source_at, values, scaled)

        def residual(row, cell, low):
            mine = kr[row, rows, :]
            summed = mine * fine_sum(geo, vb, row, low) + fine_sum(geo, wb, row, low)
            resid[cell] = out_source[0, cell] + summed - diag[cell] * vr[row, rows, :]
            out_black[cell] = vb[row, rows, :]

        fine_rows(geo, residual)

        own = geo.own_y()
        for cell in range(cx):
            at = HALO + 2 * cell
            pair = resid[at] + resid[at + 1]
            diag[at] = pair
            mine = kr[at + 1, rows, :] + kr[at + 2, rows, :]
            mine = mine + kb[at + 1, rows, :] + kb[at + 2, rows, :]
            diag[at + 1] = mine
            for which, scale in ((0, 0.125), (1, 0.25)):
                low = diag[at + which, pl.ds(own, cy, 2), :]
                high = diag[at + which, pl.ds(own + 1, cy, 2), :]
                coarse_ref[which, cell] = scale * (low + high)

    window = shape_f32(wx, wy, LANES)
    both = shape_f32(2, wx, wy, LANES)
    return call(
        kernel,
        [shape_f32(2, cx, cy, LANES), window, both, both, both],
        [fine_scratch(geo)] * 6 + [pltpu.VMEM((wx, wy, LANES), F32)] * 2,
    )(*coefficient, *source)


def mid_sum(my, ref, row):
    rows = slice(PAD, PAD + my)
    here = ref[row, rows, :]
    total = ref[row - 1, rows, :] + ref[row + 1, rows, :]
    total = total + ref[row, PAD - 1 : PAD - 1 + my, :]
    total = total + ref[row, PAD + 1 : PAD + 1 + my, :]
    return total + pltpu.roll(here, 1, 1) + pltpu.roll(here, LANES - 1, 1)


def mid_rows(mx, my, body):
    even = (iota((my, LANES), 0) + iota((my, LANES), 1)) % 2 == 0
    odd = jnp.logical_not(even)

    def step(index, carry):
        body(2 * index + 1, 2 * index, even)
        body(2 * index + 2, 2 * index + 1, odd)
        return carry

    lax.fori_loop(0, mx // 2, step, 0)


def mid_half(mx, my, colour, coeff, weight, source, values, scaled):
    rows = slice(PAD, PAD + my)

    def body(row, cell, red):
        chosen = red if colour == 0 else jnp.logical_not(red)
        mine = coeff[row, rows, :]
        summed = mine * mid_sum(my, values, row) + mid_sum(my, scaled, row)
        fresh = weight[cell] * (source[cell] + summed)
        fresh = jnp.where(chosen, fresh, values[row, rows, :])
        values[row, rows, :] = fresh
        scaled[row, rows, :] = mine * fresh

    mid_rows(mx, my, body)


def clear_mid(mx, my, ref):
    ref[0] = jnp.zeros((my + 2 * PAD, LANES), F32)
    ref[mx + 1] = jnp.zeros((my + 2 * PAD, LANES), F32)
    edge = jnp.zeros((mx + 2, PAD, LANES), F32)
    ref[:, 0:PAD, :] = edge
    ref[:, PAD + my : PAD + my + PAD, :] = edge


def mid_before(geo, gathered):
    depth, my = gathered.shape[2], gathered.shape[3]
    mx = geo.gx * depth
    lx, ly = mx // 2, my // 2
    share = geo.bz // 4
    groups = LANES // share

    def kernel(in_ref, low_ref, out_values, out_coeff, out_weight, out_source, *scratch):
        coeff, values, scaled, diag, pairs = scratch
        rows = slice(PAD, PAD + my)
        for ref in (coeff, values, scaled):
            clear_mid(mx, my, ref)
        for block in range(geo.gx):
            span = slice(block * depth, (block + 1) * depth)
            scaled_block = 0.5 * in_ref[block, 1]
            coeff[1 + block * depth : 1 + (block + 1) * depth, rows, :] = scaled_block
            out_coeff[span] = scaled_block
            out_source[span] = 4.0 * in_ref[block, 0]

        def first_red(row, cell, red):
            mine = coeff[row, rows, :]
            total = 6.0 * mine + mid_sum(my, coeff, row)
            inverse = jnp.where(mine > 0.0, 1.0 / total, 0.0)
            diag[cell] = total
            out_weight[cell] = inverse
            fresh = jnp.where(red, inverse * out_source[cell], 0.0)
            values[row, rows, :] = fresh
            scaled[row, rows, :] = mine * fresh

        mid_rows(mx, my, first_red)
        for colour in (1, 0, 1):
            mid_half(mx, my, colour, coeff, out_weight, out_source, values, scaled)

        def residual(row, cell, red):
            mine = coeff[row, rows, :]
            here = values[row, rows, :]
            summed = mine * mid_sum(my, values, row) + mid_sum(my, scaled, row)
            left = 0.25 * (out_source[cell] + summed - diag[cell] * here)
            pairs[cell] = jnp.where(red, left, 0.0)
            out_values[cell] = here

        mid_rows(mx, my, residual)

        source_lane = iota((LANES, LANES), 0)
        target_lane = iota((LANES, LANES), 1)
        for which in (0, 1):
            for cell in range(lx):
                if which == 0:
                    pair = pairs[2 * cell] + pairs[2 * cell + 1]
                else:
                    pair = out_coeff[2 * cell] + out_coeff[2 * cell + 1]
                diag[cell] = pair
            total = jnp.zeros((lx // groups * ly, LANES), F32)
            for group in range(groups):
                parts = []
                for cell in range(group, lx, groups):
                    low = diag[cell, pl.ds(0, ly, 2), :]
                    high = diag[cell, pl.ds(1, ly, 2), :]
                    parts.append(low + high)
                stacked = jnp.concatenate(parts, axis=0)
                fold = (target_lane == source_lane // 2 + group * share) & (
                    source_lane < 2 * share
                )
                total = total + exact_dot(stacked, jnp.where(fold, 0.125, 0.0))
            low_ref[which] = total.reshape(lx // groups, ly, LANES)

    full = shape_f32(mx, my, LANES)
    padded = pltpu.VMEM((mx + 2, my + 2 * PAD, LANES), F32)
    plain = pltpu.VMEM((mx, my, LANES), F32)
    return call(
        kernel,
        [shape_f32(2, lx // groups, ly, LANES), full, full, full, full],
        [padded] * 3 + [plain] * 2,
    )(gathered)


def low_shift(values, dim, step):
    size = values.shape[dim]
    if dim == 0:
        blank = jnp.zeros_like(values[0:1])
        if step < 0:
            return jnp.concatenate([blank, values[:-1]], axis=0)
        return jnp.concatenate([values[1:], blank], axis=0)
    turned = pltpu.roll(values, 1 if step < 0 else size - 1, dim)
    edge = 0 if step < 0 else size - 1
    return jnp.where(iota(values.shape, dim) == edge, 0.0, turned)


def low_sum(values):
    total = low_shift(values, 0, -1) + low_shift(values, 0, 1)
    for dim in (1, 2):
        total = total + low_shift(values, dim, -1) + low_shift(values, dim, 1)
    return total


def bottom_solve(rhs, half_coeff):
    diag = 6.0 * half_coeff + low_sum(half_coeff)

    def apply(values):
        summed = half_coeff * low_sum(values) + low_sum(half_coeff * values)
        return (diag * values - summed) * 0.0625

    image = apply(rhs)
    alpha = jnp.sum(rhs * rhs) / jnp.sum(rhs * image)
    rest = rhs - alpha * image
    turned = apply(rest)
    omega = jnp.sum(turned * rest) / jnp.sum(turned * turned)
    return alpha * rhs + omega * rest


def finish(geo, lows, mids, fines):
    mx, my = mids[0].shape[0], mids[0].shape[1]
    lx, ly = mx // 2, my // 2
    share = geo.bz // 4
    groups = LANES // share
    columns = geo.gz * share
    wx, wy = geo.wx, geo.wy
    cx, cy = geo.bx // 2, geo.by // 2
    reach = HALO // 2

    def kernel(*refs):
        low_ref = refs[0]
        mid_values, mid_coeff, mid_weight, mid_source = refs[1:5]
        fine_black, fine_coeff, fine_weight, fine_source = refs[5:9]
        out_ref = refs[9]
        low_full, spread, mc, mv, mw, up = refs[10:16]
        kr, kb, vr, vb, wr, wb = refs[16:]

        lane = iota((ly, LANES), 1) // share
        for which in (0, 1):
            for cell in range(lx):
                line, group = cell // groups, cell % groups
                for tile in range(columns // LANES):
                    total = jnp.zeros((ly, LANES), F32)
                    for part in range(groups):
                        piece = low_ref[tile * groups + part, which, line]
                        shift = ((part - group) * share) % LANES
                        if shift:
                            piece = pltpu.roll(piece, shift, 1)
                        total = jnp.where(lane == part, piece, total)
                    low_full[which, cell, :, tile * LANES : (tile + 1) * LANES] = total
        bottom = bottom_solve(low_full[0], low_full[1])

        target = iota((columns, LANES), 1)
        target = jnp.where(target < LANES // 2 + LANES // 4, target, target - LANES)
        wanted = (target + LANES) // 2 - LANES // 2 + lax.axis_index("gz") * share
        copy = (iota((columns, LANES), 0) == wanted).astype(F32)
        fetched = exact_dot(bottom.reshape(lx * ly, columns), copy).reshape(lx, ly, LANES)
        rows = slice(PAD, PAD + my)
        for ref in (mc, mv, mw):
            clear_mid(mx, my, ref)
        for cell in range(lx):
            spread[cell, pl.ds(0, ly, 2), :] = fetched[cell]
            spread[cell, pl.ds(1, ly, 2), :] = fetched[cell]
        for cell in range(mx):
            mine = mid_coeff[cell]
            fresh = mid_values[cell] + spread[cell // 2]
            mc[cell + 1, rows, :] = mine
            mv[cell + 1, rows, :] = fresh
            mw[cell + 1, rows, :] = mine * fresh
        for colour in (0, 1, 0, 1):
            mid_half(mx, my, colour, mc, mid_weight, mid_source, mv, mw)

        up[...] = jnp.zeros_like(up)
        first = lax.axis_index("gx") * cx - reach
        for cell in range(wx // 2):
            at = first + cell
            clipped = jnp.clip(at, 0, mx - 1)
            line = mv[clipped + 1, rows, :]
            line = jnp.where((at >= 0) & (at < mx), line, 0.0)
            up[cell, pl.ds(PAD, my, 2), :] = line
            up[cell, pl.ds(PAD + 1, my, 2), :] = line
        for ref in (kr, kb, vr, vb, wr, wb):
            clear_pads(geo, ref)
        begin = PAD + lax.axis_index("gy") * geo.by - geo.own_y()
        begin = pl.multiple_of(begin, HALO)
        inner = slice(PAD, PAD + wy)
        for cell in range(wx):
            red, black = fine_coeff[0, cell], fine_coeff[1, cell]
            kr[cell + 1, inner, :] = red
            kb[cell + 1, inner, :] = black
            lifted = jnp.where(black > 0.0, up[cell // 2, pl.ds(begin, wy), :], 0.0)
            fresh = fine_black[cell] + lifted
            vb[cell + 1, inner, :] = fresh
            wb[cell + 1, inner, :] = black * fresh
        coeff, values, scaled = (kr, kb), (vr, vb), (wr, wb)
        weight = (fine_weight.at[0], fine_weight.at[1])
        source = (fine_source.at[0], fine_source.at[1])
        for colour in (0, 1, 0, 1):
            fine_half(geo, colour, coeff, weight, source, values, scaled)

        own = pl.multiple_of(geo.own_y() + PAD, HALO)
        span = slice(HALO + 1, HALO + 1 + geo.bx)
        red = vr[span, pl.ds(own, geo.by), :]
        black = vb[span, pl.ds(own, geo.by), :]
        even_first = even_rows((geo.bx, geo.by, LANES), (0, 1))
        even = jnp.where(even_first, red, black).reshape(geo.bx * geo.by, LANES)
        odd = jnp.where(even_first, black, red).reshape(geo.bx * geo.by, LANES)
        from_lane = iota((LANES, geo.bz), 0)
        to_lane = iota((LANES, geo.bz), 1)
        result = exact_dot(even, (to_lane == 2 * from_lane).astype(F32))
        result = result + exact_dot(odd, (to_lane == 2 * from_lane + 1).astype(F32))
        out_ref[...] = result.reshape(geo.bx, geo.by, geo.bz)

    padded = pltpu.VMEM((mx + 2, my + 2 * PAD, LANES), F32)
    return call(
        kernel,
        shape_f32(geo.bx, geo.by, geo.bz),
        [
            pltpu.VMEM((2, lx, ly, columns), F32),
            pltpu.VMEM((lx, my, LANES), F32),
            padded,
            padded,
            padded,
            pltpu.VMEM((wx // 2, 2 * my + 2 * PAD, LANES), F32),
        ]
        + [fine_scratch(geo)] * 6,
    )(lows, *mids, *fines)


def gather_coarse(geo, coarse):
    if geo.swap:
        other = lax.ppermute(coarse, "gy", [(0, 1), (1, 0)])
        lower = lax.axis_index("gy") == 0
        rows = jnp.concatenate(
            [jnp.where(lower, coarse, other), jnp.where(lower, other, coarse)], axis=2
        )
    else:
        rows = lax.all_gather(coarse, "gy", axis=2, tiled=True)
    return lax.all_gather(rows, "gx", axis=0, tiled=False)


def per_device(geo, old_slots, old_ids, coefficient):
    before = lax.ppermute(coefficient, "gz", neighbours_of("gz", geo.gz, 1))
    after = lax.ppermute(coefficient, "gz", neighbours_of("gz", geo.gz, -1))
    capacity, cells = old_slots.shape[2], old_slots.shape[3]
    tags = jnp.broadcast_to(old_ids.reshape(capacity, 1), (capacity, LANES)).astype(BF16)
    tagged = jnp.concatenate([old_slots.reshape(capacity, cells), tags], axis=1)
    column = lax.all_gather(tagged, "gz", axis=0, tiled=True)

    own_k, *send_k = pack_coefficient(geo, coefficient, before, after)
    halo_k = exchange_y(geo, send_k)
    own_f, *send_f = pack_source(geo, column, cells)
    halo_f = exchange_y(geo, send_f)
    low_k, high_k = widen_y(geo, own_k, halo_k)
    left_k, right_k = exchange_x(geo, low_k, high_k)
    low_f, high_f = widen_y(geo, own_f, halo_f)
    left_f, right_f = exchange_x(geo, low_f, high_f)

    coarse, *fines = fine_before(
        geo, (left_k, low_k, high_k, right_k), (left_f, low_f, high_f, right_f)
    )
    packed, *mids = mid_before(geo, gather_coarse(geo, coarse))
    lows = lax.all_gather(packed, "gz", axis=0, tiled=False)
    return finish(geo, lows, mids, fines)


def solution(mesh):
    sizes = tuple(mesh.shape[name] for name in ("gx", "gy", "gz"))

    def body(old_slots, old_ids, old_owner, coefficient):
        del old_owner
        geo = Geometry(sizes, coefficient.shape)
        return per_device(geo, old_slots, old_ids, coefficient)

    in_specs = (
        P("gx", "gy", "gz", None),
        P("gx", "gy", "gz"),
        P("gx", "gy", None),
        P("gx", "gy", "gz"),
    )
    return jax.shard_map(
        body, mesh=mesh, in_specs=in_specs, out_specs=P("gx", "gy", "gz"), check_vma=False
    )
```

time: 554 us -> 96.5 us (0.17); the launches traced: 547 us -> 96.2 us
  starting transfers between devices: 221 us -> 18 us
  waiting for transfers between devices: 175 us -> 12.7 us
  blocking collectives: 80.9 us -> 30.2 us
  Pallas kernels: 0 us -> 33.5 us
  local copies, waits for them, and re-layouts: 31.5 us -> 0.08 us
  other arithmetic: 32.8 us -> 1.53 us
    ppermute x108 -> x9, starting transfers between devices: 218 us -> 18 us  [the longest x2 8.05 us: exchange_x(): lax.ppermute(high, 'gx', neighbours_of('gx', geo.gx, 1))]
    ppermute x108 -> x9, waiting for transfers between devices: 175 us -> 12.7 us  [the longest x2 4.74 us: exchange_x(): lax.ppermute(low, 'gx', neighbours_of('gx', geo.gx, -1))]
    psum x2 -> x0, blocking collectives: 80.9 us -> none  [dot_pair(): return lax.psum((first_term, second_term), ('gx', 'gy', 'gz'))]
    pallas_call x0 -> x7, Pallas kernels: none -> 33.5 us  [the longest x1 14.7 us: finish(): call(kernel, shape_f32(geo.bx, geo.by, geo.bz), [pltpu.VMEM((2, lx, ly, c...]
    all_gather x0 -> x3, blocking collectives: none -> 30.2 us  [the longest x1 15.7 us: gather_coarse(): return lax.all_gather(rows, 'gx', axis=0, tiled=False)]
    reshape x8 -> x0, local copies, waits for them, and re-layouts: 24.1 us -> none  [the longest x3 21.5 us: coarsen(): values.reshape(extent_first // 2, 2, extent_second // 2, 2, extent_third...]
    select_n x19 -> x1, other arithmetic: 11.8 us -> 0.01 us  [gather_coarse(): jnp.where(lower, coarse, other)]
    reduce_sum x8 -> x0, other arithmetic: 11 us -> none  [the longest x4 8.39 us: coarsen(): return grouped.mean(axis=(1, 3, 5))]
  transfers between devices with their start and end apart: 109 -> 9, of which waited for: 50 -> 5; matrix products, arithmetic and copies ran while one was open for 5% -> 2% of each run, Pallas kernels for 0% -> 2%
where the time goes in v1:
time: 96.5 us; the launch traced here: 96.2 us
  Pallas kernels  33.5 us (35%)
  blocking collectives  30.2 us (31%)
  starting transfers between devices  18 us (19%)
  waiting for transfers between devices  12.7 us (13%)
  other arithmetic  1.53 us (2%)
    all_gather x1, blocking collectives, gather_coarse(): return lax.all_gather(rows, 'gx', axis=0, tiled=False)  15.7 us
    pallas_call x1, Pallas kernels, finish(): call(kernel, shape_f32(geo.bx, geo.by, geo.bz), [pltpu.VMEM((2, lx, ly, c...  14.7 us
    pallas_call x1, Pallas kernels, fine_before(): call(kernel, [shape_f32(2, cx, cy, LANES), window, both, both, both], [fi...  9.46 us
    all_gather x1, blocking collectives, per_device(): column = lax.all_gather(tagged, 'gz', axis=0, tiled=True)  9.15 us
    ppermute x2, starting transfers between devices, exchange_x(): lax.ppermute(high, 'gx', neighbours_of('gx', geo.gx, 1))  8.05 us
    pallas_call x1, Pallas kernels, mid_before(): call(kernel, [shape_f32(2, lx // groups, ly, LANES), full, full, full, fu...  7.76 us
    all_gather x1, blocking collectives, per_device(): lows = lax.all_gather(packed, 'gz', axis=0, tiled=False)  5.41 us
    ppermute x2, waiting for transfers between devices, exchange_x(): lax.ppermute(low, 'gx', neighbours_of('gx', geo.gx, -1))  4.74 us
  transfers between devices with their start and end apart: 9, of which 5 were waited for; matrix products, arithmetic and copies ran while one was open for 2% of the time, Pallas kernels for 2%

profile of v1, /device:TPU:0, one launch (start us, length us, event | category | flops | bytes accessed | tf_op | source)
XLA Modules:
  0.0 96.2 jit_solution(5574074053727530226)
XLA Ops:
  0.0 2.4 %collective-permute-start = (f32[16,16,128]{2,1,0:T(8,128)}, f32[16,16,128]{2,1,0:T(8,128)S(1)}, u32[]{:S(2)}, u32[]{:S(2)}) collective-permute-start(f32[16,16,128]{2,1,0:T(8,128)} %own_ref.1), channel_id=1, source_target_pairs={{0,1},{1,2},{2,3},{4,5},{5,6},{6,7},{8,9},{9,10},{10,11},{12,13},{... | collective-permute-start | bytes 393224 | tf_op jit(solution)/shard_map/ppermute | solution.py:609
  2.4 1.3 %collective-permute-start.1 = (f32[16,16,128]{2,1,0:T(8,128)}, f32[16,16,128]{2,1,0:T(8,128)S(1)}, u32[]{:S(2)}, u32[]{:S(2)}) collective-permute-start(f32[16,16,128]{2,1,0:T(8,128)} %own_ref.1), channel_id=1, source_target_pairs={{1,0},{2,1},{3,2},{5,4},{6,5},{7,6},{9,8},{10,9},{11,10},{13,12},{... | collective-permute-start | bytes 393224 | tf_op jit(solution)/shard_map/ppermute | solution.py:610
  3.7 0.7 convert_bitcast_fusion
  4.4 0.1 broadcast_in_dim.2
  4.4 0.8 pad_maximum_fusion.1
  5.3 9.1 %all_gather.15.slot_ref = bf16[32,4224]{1,0:T(8,128)(2,1)S(1)} all-gather(bf16[8,4224]{1,0:T(8,128)(2,1)S(1)} %pad_maximum_fusion.1), channel_id=1, replica_groups=mesh['gx'=4,'gy'=2,'gz'=4] {'gz'}, dimensions={0}, use_global_device_ids=true | all-gather | bytes 337920 | tf_op jit(solution)/shard_map/all_gather | solution.py:614
  14.4 0.0 copy-start
  14.4 0.9 shard_map.39
  15.4 1.6 %collective-permute-start.5 = (f32[2,16,8,128]{3,2,1,0:T(8,128)S(1)}, f32[2,16,8,128]{3,2,1,0:T(8,128)S(1)}, u32[]{:S(2)}, u32[]{:S(2)}) collective-permute-start(f32[2,16,8,128]{3,2,1,0:T(8,128)S(1)} %get-tuple-element.28), channel_id=1, source_target_pairs={{0,4},{4,0},{1,5},{5,1},{2,6},{6,2},{3,7},{7,3},{8,12},{12,8},{9,1... | collective-permute-start | bytes 393224 | tf_op jit(solution)/shard_map/ppermute | solution.py:168
  16.9 0.0 collective-permute-done.before_ref
  16.9 0.0 collective-permute-done.1.after_ref
  16.9 0.0 copy-done
  16.9 0.6 shard_map.37
  17.5 0.6 collective-permute-start.2
  18.1 3.7 %collective-permute-done.5.rest_0_ = f32[2,16,8,128]{3,2,1,0:T(8,128)S(1)} collective-permute-done((f32[2,16,8,128]{3,2,1,0:T(8,128)S(1)}, f32[2,16,8,128]{3,2,1,0:T(8,128)S(1)}, u32[]{:S(2)}, u32[]{:S(2)}) %collective-permute-start.5) | collective-permute-done | bytes 131104 | tf_op jit(solution)/shard_map/ppermute | solution.py:168
  21.8 3.5 %collective-permute-start.6 = (f32[2,8,24,128]{3,2,1,0:T(8,128)S(1)}, f32[2,8,24,128]{3,2,1,0:T(8,128)S(1)}, u32[]{:S(2)}, u32[]{:S(2)}) collective-permute-start(f32[2,8,24,128]{3,2,1,0:T(8,128)S(1)} %get-tuple-element.29.refs_6_), channel_id=1, source_target_pairs={{0,8},{8,16},{16,24},{1,9},{9,17},{17,25},{2,10},{10,18},{18,26},{... | collective-permute-start | bytes 589832 | tf_op jit(solution)/shard_map/ppermute | solution.py:193
  25.3 1.3 %collective-permute-start.7 = (f32[2,8,24,128]{3,2,1,0:T(8,128)S(1)}, f32[2,8,24,128]{3,2,1,0:T(8,128)S(1)}, u32[]{:S(2)}, u32[]{:S(2)}) collective-permute-start(f32[2,8,24,128]{3,2,1,0:T(8,128)S(1)} %get-tuple-element.30.refs_5_), channel_id=1, source_target_pairs={{8,0},{16,8},{24,16},{9,1},{17,9},{25,17},{10,2},{18,10},{26,18},{... | collective-permute-start | bytes 589832 | tf_op jit(solution)/shard_map/ppermute | solution.py:194
  26.6 0.0 collective-permute-done.2.rest_0_
  26.7 4.6 %collective-permute-start.3 = (f32[2,8,24,128]{3,2,1,0:T(8,128)S(1)}, f32[2,8,24,128]{3,2,1,0:T(8,128)S(1)}, u32[]{:S(2)}, u32[]{:S(2)}) collective-permute-start(f32[2,8,24,128]{3,2,1,0:T(8,128)S(1)} %get-tuple-element.25.refs_2_), channel_id=1, source_target_pairs={{0,8},{8,16},{16,24},{1,9},{9,17},{17,25},{2,10},{10,18},{18,26},{... | collective-permute-start | bytes 589832 | tf_op jit(solution)/shard_map/ppermute | solution.py:193
  31.2 1.3 %collective-permute-start.4 = (f32[2,8,24,128]{3,2,1,0:T(8,128)S(1)}, f32[2,8,24,128]{3,2,1,0:T(8,128)S(1)}, u32[]{:S(2)}, u32[]{:S(2)}) collective-permute-start(f32[2,8,24,128]{3,2,1,0:T(8,128)S(1)} %get-tuple-element.26.refs_1_), channel_id=1, source_target_pairs={{8,0},{16,8},{24,16},{9,1},{17,9},{25,17},{10,2},{18,10},{26,18},{... | collective-permute-start | bytes 589832 | tf_op jit(solution)/shard_map/ppermute | solution.py:194
  32.5 0.0 collective-permute-done.6.refs_4_
  32.6 0.3 collective-permute-done.7.refs_7_
  32.9 1.5 %collective-permute-done.3.refs_0_ = f32[2,8,24,128]{3,2,1,0:T(8,128)S(1)} collective-permute-done((f32[2,8,24,128]{3,2,1,0:T(8,128)S(1)}, f32[2,8,24,128]{3,2,1,0:T(8,128)S(1)}, u32[]{:S(2)}, u32[]{:S(2)}) %collective-permute-start.3) | collective-permute-done | bytes 196640 | tf_op jit(solution)/shard_map/ppermute | solution.py:193
  34.4 4.4 %collective-permute-done.4.refs_3_ = f32[2,8,24,128]{3,2,1,0:T(8,128)S(1)} collective-permute-done((f32[2,8,24,128]{3,2,1,0:T(8,128)S(1)}, f32[2,8,24,128]{3,2,1,0:T(8,128)S(1)}, u32[]{:S(2)}, u32[]{:S(2)}) %collective-permute-start.4) | collective-permute-done | bytes 196640 | tf_op jit(solution)/shard_map/ppermute | solution.py:194
  38.8 9.5 %shard_map.41 = (f32[2,8,8,128]{3,2,1,0:T(8,128)S(1)}, f32[32,24,128]{2,1,0:T(8,128)S(1)}, f32[2,32,24,128]{3,2,1,0:T(8,128)S(1)}, f32[2,32,24,128]{3,2,1,0:T(8,128)S(1)}, f32[2,32,24,128]{3,2,1,0:T(8,128)S(1)}) custom-call(f32[2,8,24,128]{3,2,1,0:T(8,128)S(1)} %collective-permute-done.3.refs_0_, f32[2,8,24,128]{3,2,1,0:T(8,128)S(1)} %get-tuple-element.26.refs_1_, ...), custom_call_target="tpu_custom_call" | custom-call | tf_op jit(solution)/shard_map/pallas_call | solution.py:325
  48.3 1.6 %collective-permute-start.8 = (f32[2,8,8,128]{3,2,1,0:T(8,128)S(1)}, f32[2,8,8,128]{3,2,1,0:T(8,128)S(1)}, u32[]{:S(2)}, u32[]{:S(2)}) collective-permute-start(f32[2,8,8,128]{3,2,1,0:T(8,128)S(1)} %get-tuple-element.31), channel_id=1, source_target_pairs={{0,4},{4,0},{1,5},{5,1},{2,6},{6,2},{3,7},{7,3},{8,12},{12,8},{9,1... | collective-permute-start | bytes 196616 | tf_op jit(solution)/shard_map/ppermute | solution.py:598
  49.8 2.8 %collective-permute-done.8 = f32[2,8,8,128]{3,2,1,0:T(8,128)S(1)} collective-permute-done((f32[2,8,8,128]{3,2,1,0:T(8,128)S(1)}, f32[2,8,8,128]{3,2,1,0:T(8,128)S(1)}, u32[]{:S(2)}, u32[]{:S(2)}) %collective-permute-start.8) | collective-permute-done | bytes 65568 | tf_op jit(solution)/shard_map/ppermute | solution.py:598
  52.6 15.7 %all-gather = f32[8,8,16,128]{3,2,1,0:T(8,128)S(1)} all-gather(f32[2,8,16,128]{3,2,1,0:T(8,128)S(1)} %pad_maximum_fusion), channel_id=2, replica_groups=mesh['gx'=4,'gy'=2,'gz'=4] {'gx'}, dimensions={0}, use_global_device_ids=true | all-gather | bytes 655360 | tf_op jit(solution)/shard_map/all_gather | solution.py:605
  68.3 7.8 %shard_map.42 = (f32[2,4,8,128]{3,2,1,0:T(8,128)S(1)}, f32[32,16,128]{2,1,0:T(8,128)S(1)}, f32[32,16,128]{2,1,0:T(8,128)S(1)}, f32[32,16,128]{2,1,0:T(8,128)S(1)}, f32[32,16,128]{2,1,0:T(8,128)S(1)}) custom-call(f32[4,2,8,16,128]{4,3,2,1,0:T(8,128)S(1)} %bitcast.5), custom_call_target="tpu_custom_call" | custom-call | tf_op jit(solution)/shard_map/pallas_call | solution.py:445
  76.1 5.4 %all-gather.1 = f32[8,4,8,128]{3,2,1,0:T(8,128)S(1)} all-gather(f32[2,4,8,128]{3,2,1,0:T(8,128)S(1)} %get-tuple-element.32), channel_id=3, replica_groups=mesh['gx'=4,'gy'=2,'gz'=4] {'gz'}, dimensions={0}, use_global_device_ids=true | all-gather | bytes 163840 | tf_op jit(solution)/shard_map/all_gather | solution.py:629
  81.5 14.7 %shard_map.43 = f32[16,16,128]{2,1,0:T(8,128)} custom-call(f32[4,2,4,8,128]{4,3,2,1,0:T(8,128)S(1)} %bitcast.6, f32[32,16,128]{2,1,0:T(8,128)S(1)} %get-tuple-element.33.refs_1_, f32[32,16,128]{2,1,0:T(8,128)S(1)} %get-tuple-element.34.refs_2_, f32[32,16,128]{2,1,0:T(8,128)S(1)} %get-tuple-element.35.refs_3_, f32[32,16,128]{2,1,0:T(8,128)S(1)} %get-tuple-element.36.refs_4_, ...), custom_call_target="tpu_custom_call" | custom-call | tf_op jit(solution)/shard_map/pallas_call | solution.py:581
  (4 shorter events, 0.1 us)
Async XLA Ops:
  0.0 16.9 %collective-permute-start = (f32[16,16,128]{2,1,0:T(8,128)}, f32[16,16,128]{2,1,0:T(8,128)S(1)}, u32[]{:S(2)}, u32[]{:S(2)}) collective-permute-start(f32[16,16,128]{2,1,0:T(8,128)} %own_ref.1), channel_id=1, source_target_pairs={{0,1},{1,2},{2,3},{4,5},{5,6},{6,7},{8,9},{9,10},{10,11},{12,13},{... | collective-permute-start | bytes 393224 | tf_op jit(solution)/shard_map/ppermute | solution.py:609
  2.4 14.5 %collective-permute-start.1 = (f32[16,16,128]{2,1,0:T(8,128)}, f32[16,16,128]{2,1,0:T(8,128)S(1)}, u32[]{:S(2)}, u32[]{:S(2)}) collective-permute-start(f32[16,16,128]{2,1,0:T(8,128)} %own_ref.1), channel_id=1, source_target_pairs={{1,0},{2,1},{3,2},{5,4},{6,5},{7,6},{9,8},{10,9},{11,10},{13,12},{... | collective-permute-start | bytes 393224 | tf_op jit(solution)/shard_map/ppermute | solution.py:610
  14.4 2.5 %copy-start = (f32[16,16,128]{2,1,0:T(8,128)S(1)}, f32[16,16,128]{2,1,0:T(8,128)}, u32[]{:S(2)}) copy-start(f32[16,16,128]{2,1,0:T(8,128)} %own_ref.1) | copy-start | bytes 393220
  15.4 6.4 %collective-permute-start.5 = (f32[2,16,8,128]{3,2,1,0:T(8,128)S(1)}, f32[2,16,8,128]{3,2,1,0:T(8,128)S(1)}, u32[]{:S(2)}, u32[]{:S(2)}) collective-permute-start(f32[2,16,8,128]{3,2,1,0:T(8,128)S(1)} %get-tuple-element.28), channel_id=1, source_target_pairs={{0,4},{4,0},{1,5},{5,1},{2,6},{6,2},{3,7},{7,3},{8,12},{12,8},{9,1... | collective-permute-start | bytes 393224 | tf_op jit(solution)/shard_map/ppermute | solution.py:168
  17.5 9.1 %collective-permute-start.2 = (f32[2,16,8,128]{3,2,1,0:T(8,128)S(1)}, f32[2,16,8,128]{3,2,1,0:T(8,128)S(1)}, u32[]{:S(2)}, u32[]{:S(2)}) collective-permute-start(f32[2,16,8,128]{3,2,1,0:T(8,128)S(1)} %get-tuple-element.24), channel_id=1, source_target_pairs={{0,4},{4,0},{1,5},{5,1},{2,6},{6,2},{3,7},{7,3},{8,12},{12,8},{9,1... | collective-permute-start | bytes 393224 | tf_op jit(solution)/shard_map/ppermute | solution.py:168
  21.8 10.7 %collective-permute-start.6 = (f32[2,8,24,128]{3,2,1,0:T(8,128)S(1)}, f32[2,8,24,128]{3,2,1,0:T(8,128)S(1)}, u32[]{:S(2)}, u32[]{:S(2)}) collective-permute-start(f32[2,8,24,128]{3,2,1,0:T(8,128)S(1)} %get-tuple-element.29.refs_6_), channel_id=1, source_target_pairs={{0,8},{8,16},{16,24},{1,9},{9,17},{17,25},{2,10},{10,18},{18,26},{... | collective-permute-start | bytes 589832 | tf_op jit(solution)/shard_map/ppermute | solution.py:193
  25.3 7.6 %collective-permute-start.7 = (f32[2,8,24,128]{3,2,1,0:T(8,128)S(1)}, f32[2,8,24,128]{3,2,1,0:T(8,128)S(1)}, u32[]{:S(2)}, u32[]{:S(2)}) collective-permute-start(f32[2,8,24,128]{3,2,1,0:T(8,128)S(1)} %get-tuple-element.30.refs_5_), channel_id=1, source_target_pairs={{8,0},{16,8},{24,16},{9,1},{17,9},{25,17},{10,2},{18,10},{26,18},{... | collective-permute-start | bytes 589832 | tf_op jit(solution)/shard_map/ppermute | solution.py:194
  26.7 7.7 %collective-permute-start.3 = (f32[2,8,24,128]{3,2,1,0:T(8,128)S(1)}, f32[2,8,24,128]{3,2,1,0:T(8,128)S(1)}, u32[]{:S(2)}, u32[]{:S(2)}) collective-permute-start(f32[2,8,24,128]{3,2,1,0:T(8,128)S(1)} %get-tuple-element.25.refs_2_), channel_id=1, source_target_pairs={{0,8},{8,16},{16,24},{1,9},{9,17},{17,25},{2,10},{10,18},{18,26},{... | collective-permute-start | bytes 589832 | tf_op jit(solution)/shard_map/ppermute | solution.py:193
  31.2 7.6 %collective-permute-start.4 = (f32[2,8,24,128]{3,2,1,0:T(8,128)S(1)}, f32[2,8,24,128]{3,2,1,0:T(8,128)S(1)}, u32[]{:S(2)}, u32[]{:S(2)}) collective-permute-start(f32[2,8,24,128]{3,2,1,0:T(8,128)S(1)} %get-tuple-element.26.refs_1_), channel_id=1, source_target_pairs={{8,0},{16,8},{24,16},{9,1},{17,9},{25,17},{10,2},{18,10},{26,18},{... | collective-permute-start | bytes 589832 | tf_op jit(solution)/shard_map/ppermute | solution.py:194
  48.3 4.3 %collective-permute-start.8 = (f32[2,8,8,128]{3,2,1,0:T(8,128)S(1)}, f32[2,8,8,128]{3,2,1,0:T(8,128)S(1)}, u32[]{:S(2)}, u32[]{:S(2)}) collective-permute-start(f32[2,8,8,128]{3,2,1,0:T(8,128)S(1)} %get-tuple-element.31), channel_id=1, source_target_pairs={{0,4},{4,0},{1,5},{5,1},{2,6},{6,2},{3,7},{7,3},{8,12},{12,8},{9,1... | collective-permute-start | bytes 196616 | tf_op jit(solution)/shard_map/ppermute | solution.py:598

commit v2 on v1

--- a/solution.py
+++ b/solution.py
@@ -8,6 +8,7 @@
 BOX = 16
 HALO = 8
 LANES = 128
+UNROLL = 16
 HIGH = lax.Precision.HIGHEST
 F32 = jnp.float32
 BF16 = jnp.bfloat16
@@ -218,7 +219,7 @@
         body(2 * index + 2, 2 * index + 1, odd)
         return carry
 
-    lax.fori_loop(0, geo.wx // 2, step, 0)
+    lax.fori_loop(0, geo.wx // 2, step, 0, unroll=UNROLL)
 
 
 def fine_half(geo, colour, coeff, weight, source, values, scaled, extra=None):
@@ -347,7 +348,7 @@
         body(2 * index + 2, 2 * index + 1, odd)
         return carry
 
-    lax.fori_loop(0, mx // 2, step, 0)
+    lax.fori_loop(0, mx // 2, step, 0, unroll=UNROLL)
 
 
 def mid_half(mx, my, colour, coeff, weight, source, values, scaled):

time: 96.5 us -> 73.3 us (0.76)
  Pallas kernels: 33.5 us -> 10.3 us
    pallas_call x1, Pallas kernels: 14.7 us -> 4.88 us  [finish(): call(kernel, shape_f32(geo.bx, geo.by, geo.bz), [pltpu.VMEM((2, lx, ly, c...]
    pallas_call x1, Pallas kernels: 9.46 us -> 2.03 us  [fine_before(): call(kernel, [shape_f32(2, cx, cy, LANES), window, both, both, both], [fi...]
    pallas_call x1, Pallas kernels: 7.76 us -> 1.84 us  [mid_before(): call(kernel, [shape_f32(2, lx // groups, ly, LANES), full, full, full, fu...]
where the time goes in v2:
time: 73.3 us; the launch traced here: 73 us
  blocking collectives  30.2 us (41%)
  starting transfers between devices  18 us (25%)
  waiting for transfers between devices  12.7 us (17%)
  Pallas kernels  10.3 us (14%)
  other arithmetic  1.53 us (2%)
    all_gather x1, blocking collectives, gather_coarse(): return lax.all_gather(rows, 'gx', axis=0, tiled=False)  15.7 us
    all_gather x1, blocking collectives, per_device(): column = lax.all_gather(tagged, 'gz', axis=0, tiled=True)  9.15 us
    ppermute x2, starting transfers between devices, exchange_x(): lax.ppermute(high, 'gx', neighbours_of('gx', geo.gx, 1))  8.05 us
    all_gather x1, blocking collectives, per_device(): lows = lax.all_gather(packed, 'gz', axis=0, tiled=False)  5.41 us
    pallas_call x1, Pallas kernels, finish(): call(kernel, shape_f32(geo.bx, geo.by, geo.bz), [pltpu.VMEM((2, lx, ly, c...  4.88 us
    ppermute x2, waiting for transfers between devices, exchange_x(): lax.ppermute(low, 'gx', neighbours_of('gx', geo.gx, -1))  4.74 us
    ppermute x2, waiting for transfers between devices, exchange_y(): return (lax.ppermute(sends[0], 'gy', [(0, 1), (1, 0)]),)  3.67 us
    ppermute x1, waiting for transfers between devices, gather_coarse(): other = lax.ppermute(coarse, 'gy', [(0, 1), (1, 0)])  2.77 us
  transfers between devices with their start and end apart: 9, of which 5 were waited for; matrix products, arithmetic and copies ran while one was open for 2% of the time, Pallas kernels for 2%

profile of v2, /device:TPU:0, one launch (start us, length us, event | category | flops | bytes accessed | tf_op | source)
XLA Modules:
  0.0 73.0 jit_solution(17541618097441500789)
XLA Ops:
  0.0 2.4 %collective-permute-start = (f32[16,16,128]{2,1,0:T(8,128)}, f32[16,16,128]{2,1,0:T(8,128)S(1)}, u32[]{:S(2)}, u32[]{:S(2)}) collective-permute-start(f32[16,16,128]{2,1,0:T(8,128)} %own_ref.1), channel_id=1, source_target_pairs={{0,1},{1,2},{2,3},{4,5},{5,6},{6,7},{8,9},{9,10},{10,11},{12,13},{... | collective-permute-start | bytes 393224 | tf_op jit(solution)/shard_map/ppermute | solution.py:610
  2.4 1.3 %collective-permute-start.1 = (f32[16,16,128]{2,1,0:T(8,128)}, f32[16,16,128]{2,1,0:T(8,128)S(1)}, u32[]{:S(2)}, u32[]{:S(2)}) collective-permute-start(f32[16,16,128]{2,1,0:T(8,128)} %own_ref.1), channel_id=1, source_target_pairs={{1,0},{2,1},{3,2},{5,4},{6,5},{7,6},{9,8},{10,9},{11,10},{13,12},{... | collective-permute-start | bytes 393224 | tf_op jit(solution)/shard_map/ppermute | solution.py:611
  3.7 0.7 convert_bitcast_fusion
  4.4 0.1 broadcast_in_dim.2
  4.4 0.8 %pad_maximum_fusion.1 = bf16[8,4224]{1,0:T(8,128)(2,1)S(1)} fusion(bf16[8,128]{1,0:T(8,128)(2,1)S(1)} %broadcast_in_dim.2, bf16[8,4096]{1,0:T(8,128)(2,1)} %bitcast.7), kind=kLoop, calls=%fused_computation.1 | loop fusion | flops 135168 | bytes 135168 | tf_op jit(solution)/shard_map/concatenate | solution.py:614
  5.3 9.1 %all_gather.15.slot_ref = bf16[32,4224]{1,0:T(8,128)(2,1)S(1)} all-gather(bf16[8,4224]{1,0:T(8,128)(2,1)S(1)} %pad_maximum_fusion.1), channel_id=1, replica_groups=mesh['gx'=4,'gy'=2,'gz'=4] {'gz'}, dimensions={0}, use_global_device_ids=true | all-gather | bytes 337920 | tf_op jit(solution)/shard_map/all_gather | solution.py:615
  14.4 0.0 copy-start
  14.4 0.9 %shard_map.39 = (f32[2,16,16,128]{3,2,1,0:T(8,128)S(1)}, f32[2,16,8,128]{3,2,1,0:T(8,128)S(1)}) custom-call(bf16[32,4224]{1,0:T(8,128)(2,1)S(1)} %all_gather.15.slot_ref), custom_call_target="tpu_custom_call" | custom-call | tf_op jit(solution)/shard_map/pallas_call | solution.py:160
  15.4 1.6 %collective-permute-start.5 = (f32[2,16,8,128]{3,2,1,0:T(8,128)S(1)}, f32[2,16,8,128]{3,2,1,0:T(8,128)S(1)}, u32[]{:S(2)}, u32[]{:S(2)}) collective-permute-start(f32[2,16,8,128]{3,2,1,0:T(8,128)S(1)} %get-tuple-element.28), channel_id=1, source_target_pairs={{0,4},{4,0},{1,5},{5,1},{2,6},{6,2},{3,7},{7,3},{8,12},{12,8},{9,1... | collective-permute-start | bytes 393224 | tf_op jit(solution)/shard_map/ppermute | solution.py:169
  16.9 0.0 collective-permute-done.before_ref
  16.9 0.0 collective-permute-done.1.after_ref
  16.9 0.0 copy-done
  16.9 0.6 shard_map.37
  17.5 0.6 collective-permute-start.2
  18.1 3.7 %collective-permute-done.5.rest_0_ = f32[2,16,8,128]{3,2,1,0:T(8,128)S(1)} collective-permute-done((f32[2,16,8,128]{3,2,1,0:T(8,128)S(1)}, f32[2,16,8,128]{3,2,1,0:T(8,128)S(1)}, u32[]{:S(2)}, u32[]{:S(2)}) %collective-permute-start.5) | collective-permute-done | bytes 131104 | tf_op jit(solution)/shard_map/ppermute | solution.py:169
  21.8 3.5 %collective-permute-start.6 = (f32[2,8,24,128]{3,2,1,0:T(8,128)S(1)}, f32[2,8,24,128]{3,2,1,0:T(8,128)S(1)}, u32[]{:S(2)}, u32[]{:S(2)}) collective-permute-start(f32[2,8,24,128]{3,2,1,0:T(8,128)S(1)} %get-tuple-element.29.refs_6_), channel_id=1, source_target_pairs={{0,8},{8,16},{16,24},{1,9},{9,17},{17,25},{2,10},{10,18},{18,26},{... | collective-permute-start | bytes 589832 | tf_op jit(solution)/shard_map/ppermute | solution.py:194
  25.3 1.3 %collective-permute-start.7 = (f32[2,8,24,128]{3,2,1,0:T(8,128)S(1)}, f32[2,8,24,128]{3,2,1,0:T(8,128)S(1)}, u32[]{:S(2)}, u32[]{:S(2)}) collective-permute-start(f32[2,8,24,128]{3,2,1,0:T(8,128)S(1)} %get-tuple-element.30.refs_5_), channel_id=1, source_target_pairs={{8,0},{16,8},{24,16},{9,1},{17,9},{25,17},{10,2},{18,10},{26,18},{... | collective-permute-start | bytes 589832 | tf_op jit(solution)/shard_map/ppermute | solution.py:195
  26.6 0.0 collective-permute-done.2.rest_0_
  26.7 4.6 %collective-permute-start.3 = (f32[2,8,24,128]{3,2,1,0:T(8,128)S(1)}, f32[2,8,24,128]{3,2,1,0:T(8,128)S(1)}, u32[]{:S(2)}, u32[]{:S(2)}) collective-permute-start(f32[2,8,24,128]{3,2,1,0:T(8,128)S(1)} %get-tuple-element.25.refs_2_), channel_id=1, source_target_pairs={{0,8},{8,16},{16,24},{1,9},{9,17},{17,25},{2,10},{10,18},{18,26},{... | collective-permute-start | bytes 589832 | tf_op jit(solution)/shard_map/ppermute | solution.py:194
  31.2 1.3 %collective-permute-start.4 = (f32[2,8,24,128]{3,2,1,0:T(8,128)S(1)}, f32[2,8,24,128]{3,2,1,0:T(8,128)S(1)}, u32[]{:S(2)}, u32[]{:S(2)}) collective-permute-start(f32[2,8,24,128]{3,2,1,0:T(8,128)S(1)} %get-tuple-element.26.refs_1_), channel_id=1, source_target_pairs={{8,0},{16,8},{24,16},{9,1},{17,9},{25,17},{10,2},{18,10},{26,18},{... | collective-permute-start | bytes 589832 | tf_op jit(solution)/shard_map/ppermute | solution.py:195
  32.5 0.0 collective-permute-done.6.refs_4_
  32.6 0.3 collective-permute-done.7.refs_7_
  32.9 1.5 %collective-permute-done.3.refs_0_ = f32[2,8,24,128]{3,2,1,0:T(8,128)S(1)} collective-permute-done((f32[2,8,24,128]{3,2,1,0:T(8,128)S(1)}, f32[2,8,24,128]{3,2,1,0:T(8,128)S(1)}, u32[]{:S(2)}, u32[]{:S(2)}) %collective-permute-start.3) | collective-permute-done | bytes 196640 | tf_op jit(solution)/shard_map/ppermute | solution.py:194
  34.4 4.4 %collective-permute-done.4.refs_3_ = f32[2,8,24,128]{3,2,1,0:T(8,128)S(1)} collective-permute-done((f32[2,8,24,128]{3,2,1,0:T(8,128)S(1)}, f32[2,8,24,128]{3,2,1,0:T(8,128)S(1)}, u32[]{:S(2)}, u32[]{:S(2)}) %collective-permute-start.4) | collective-permute-done | bytes 196640 | tf_op jit(solution)/shard_map/ppermute | solution.py:195
  38.8 2.0 %shard_map.41 = (f32[2,8,8,128]{3,2,1,0:T(8,128)S(1)}, f32[32,24,128]{2,1,0:T(8,128)S(1)}, f32[2,32,24,128]{3,2,1,0:T(8,128)S(1)}, f32[2,32,24,128]{3,2,1,0:T(8,128)S(1)}, f32[2,32,24,128]{3,2,1,0:T(8,128)S(1)}) custom-call(f32[2,8,24,128]{3,2,1,0:T(8,128)S(1)} %collective-permute-done.3.refs_0_, f32[2,8,24,128]{3,2,1,0:T(8,128)S(1)} %get-tuple-element.26.refs_1_, ...), custom_call_target="tpu_custom_call" | custom-call | tf_op jit(solution)/shard_map/pallas_call | solution.py:326
  40.8 1.6 %collective-permute-start.8 = (f32[2,8,8,128]{3,2,1,0:T(8,128)S(1)}, f32[2,8,8,128]{3,2,1,0:T(8,128)S(1)}, u32[]{:S(2)}, u32[]{:S(2)}) collective-permute-start(f32[2,8,8,128]{3,2,1,0:T(8,128)S(1)} %get-tuple-element.31), channel_id=1, source_target_pairs={{0,4},{4,0},{1,5},{5,1},{2,6},{6,2},{3,7},{7,3},{8,12},{12,8},{9,1... | collective-permute-start | bytes 196616 | tf_op jit(solution)/shard_map/ppermute | solution.py:599
  42.4 2.8 %collective-permute-done.8 = f32[2,8,8,128]{3,2,1,0:T(8,128)S(1)} collective-permute-done((f32[2,8,8,128]{3,2,1,0:T(8,128)S(1)}, f32[2,8,8,128]{3,2,1,0:T(8,128)S(1)}, u32[]{:S(2)}, u32[]{:S(2)}) %collective-permute-start.8) | collective-permute-done | bytes 65568 | tf_op jit(solution)/shard_map/ppermute | solution.py:599
  45.2 15.7 %all-gather = f32[8,8,16,128]{3,2,1,0:T(8,128)S(1)} all-gather(f32[2,8,16,128]{3,2,1,0:T(8,128)S(1)} %pad_maximum_fusion), channel_id=2, replica_groups=mesh['gx'=4,'gy'=2,'gz'=4] {'gx'}, dimensions={0}, use_global_device_ids=true | all-gather | bytes 655360 | tf_op jit(solution)/shard_map/all_gather | solution.py:606
  60.9 1.8 %shard_map.42 = (f32[2,4,8,128]{3,2,1,0:T(8,128)S(1)}, f32[32,16,128]{2,1,0:T(8,128)S(1)}, f32[32,16,128]{2,1,0:T(8,128)S(1)}, f32[32,16,128]{2,1,0:T(8,128)S(1)}, f32[32,16,128]{2,1,0:T(8,128)S(1)}) custom-call(f32[4,2,8,16,128]{4,3,2,1,0:T(8,128)S(1)} %bitcast.5), custom_call_target="tpu_custom_call" | custom-call | tf_op jit(solution)/shard_map/pallas_call | solution.py:446
  62.7 5.4 %all-gather.1 = f32[8,4,8,128]{3,2,1,0:T(8,128)S(1)} all-gather(f32[2,4,8,128]{3,2,1,0:T(8,128)S(1)} %get-tuple-element.32), channel_id=3, replica_groups=mesh['gx'=4,'gy'=2,'gz'=4] {'gz'}, dimensions={0}, use_global_device_ids=true | all-gather | bytes 163840 | tf_op jit(solution)/shard_map/all_gather | solution.py:630
  68.1 4.9 %shard_map.43 = f32[16,16,128]{2,1,0:T(8,128)} custom-call(f32[4,2,4,8,128]{4,3,2,1,0:T(8,128)S(1)} %bitcast.6, f32[32,16,128]{2,1,0:T(8,128)S(1)} %get-tuple-element.33.refs_1_, f32[32,16,128]{2,1,0:T(8,128)S(1)} %get-tuple-element.34.refs_2_, f32[32,16,128]{2,1,0:T(8,128)S(1)} %get-tuple-element.35.refs_3_, f32[32,16,128]{2,1,0:T(8,128)S(1)} %get-tuple-element.36.refs_4_, ...), custom_call_target="tpu_custom_call" | custom-call | tf_op jit(solution)/shard_map/pallas_call | solution.py:582
  (4 shorter events, 0.1 us)
Async XLA Ops:
  0.0 16.9 %collective-permute-start = (f32[16,16,128]{2,1,0:T(8,128)}, f32[16,16,128]{2,1,0:T(8,128)S(1)}, u32[]{:S(2)}, u32[]{:S(2)}) collective-permute-start(f32[16,16,128]{2,1,0:T(8,128)} %own_ref.1), channel_id=1, source_target_pairs={{0,1},{1,2},{2,3},{4,5},{5,6},{6,7},{8,9},{9,10},{10,11},{12,13},{... | collective-permute-start | bytes 393224 | tf_op jit(solution)/shard_map/ppermute | solution.py:610
  2.4 14.5 %collective-permute-start.1 = (f32[16,16,128]{2,1,0:T(8,128)}, f32[16,16,128]{2,1,0:T(8,128)S(1)}, u32[]{:S(2)}, u32[]{:S(2)}) collective-permute-start(f32[16,16,128]{2,1,0:T(8,128)} %own_ref.1), channel_id=1, source_target_pairs={{1,0},{2,1},{3,2},{5,4},{6,5},{7,6},{9,8},{10,9},{11,10},{13,12},{... | collective-permute-start | bytes 393224 | tf_op jit(solution)/shard_map/ppermute | solution.py:611
  14.4 2.5 %copy-start = (f32[16,16,128]{2,1,0:T(8,128)S(1)}, f32[16,16,128]{2,1,0:T(8,128)}, u32[]{:S(2)}) copy-start(f32[16,16,128]{2,1,0:T(8,128)} %own_ref.1) | copy-start | bytes 393220
  15.4 6.4 %collective-permute-start.5 = (f32[2,16,8,128]{3,2,1,0:T(8,128)S(1)}, f32[2,16,8,128]{3,2,1,0:T(8,128)S(1)}, u32[]{:S(2)}, u32[]{:S(2)}) collective-permute-start(f32[2,16,8,128]{3,2,1,0:T(8,128)S(1)} %get-tuple-element.28), channel_id=1, source_target_pairs={{0,4},{4,0},{1,5},{5,1},{2,6},{6,2},{3,7},{7,3},{8,12},{12,8},{9,1... | collective-permute-start | bytes 393224 | tf_op jit(solution)/shard_map/ppermute | solution.py:169
  17.5 9.1 %collective-permute-start.2 = (f32[2,16,8,128]{3,2,1,0:T(8,128)S(1)}, f32[2,16,8,128]{3,2,1,0:T(8,128)S(1)}, u32[]{:S(2)}, u32[]{:S(2)}) collective-permute-start(f32[2,16,8,128]{3,2,1,0:T(8,128)S(1)} %get-tuple-element.24), channel_id=1, source_target_pairs={{0,4},{4,0},{1,5},{5,1},{2,6},{6,2},{3,7},{7,3},{8,12},{12,8},{9,1... | collective-permute-start | bytes 393224 | tf_op jit(solution)/shard_map/ppermute | solution.py:169
  21.8 10.7 %collective-permute-start.6 = (f32[2,8,24,128]{3,2,1,0:T(8,128)S(1)}, f32[2,8,24,128]{3,2,1,0:T(8,128)S(1)}, u32[]{:S(2)}, u32[]{:S(2)}) collective-permute-start(f32[2,8,24,128]{3,2,1,0:T(8,128)S(1)} %get-tuple-element.29.refs_6_), channel_id=1, source_target_pairs={{0,8},{8,16},{16,24},{1,9},{9,17},{17,25},{2,10},{10,18},{18,26},{... | collective-permute-start | bytes 589832 | tf_op jit(solution)/shard_map/ppermute | solution.py:194
  25.3 7.6 %collective-permute-start.7 = (f32[2,8,24,128]{3,2,1,0:T(8,128)S(1)}, f32[2,8,24,128]{3,2,1,0:T(8,128)S(1)}, u32[]{:S(2)}, u32[]{:S(2)}) collective-permute-start(f32[2,8,24,128]{3,2,1,0:T(8,128)S(1)} %get-tuple-element.30.refs_5_), channel_id=1, source_target_pairs={{8,0},{16,8},{24,16},{9,1},{17,9},{25,17},{10,2},{18,10},{26,18},{... | collective-permute-start | bytes 589832 | tf_op jit(solution)/shard_map/ppermute | solution.py:195
  26.7 7.7 %collective-permute-start.3 = (f32[2,8,24,128]{3,2,1,0:T(8,128)S(1)}, f32[2,8,24,128]{3,2,1,0:T(8,128)S(1)}, u32[]{:S(2)}, u32[]{:S(2)}) collective-permute-start(f32[2,8,24,128]{3,2,1,0:T(8,128)S(1)} %get-tuple-element.25.refs_2_), channel_id=1, source_target_pairs={{0,8},{8,16},{16,24},{1,9},{9,17},{17,25},{2,10},{10,18},{18,26},{... | collective-permute-start | bytes 589832 | tf_op jit(solution)/shard_map/ppermute | solution.py:194
  31.2 7.6 %collective-permute-start.4 = (f32[2,8,24,128]{3,2,1,0:T(8,128)S(1)}, f32[2,8,24,128]{3,2,1,0:T(8,128)S(1)}, u32[]{:S(2)}, u32[]{:S(2)}) collective-permute-start(f32[2,8,24,128]{3,2,1,0:T(8,128)S(1)} %get-tuple-element.26.refs_1_), channel_id=1, source_target_pairs={{8,0},{16,8},{24,16},{9,1},{17,9},{25,17},{10,2},{18,10},{26,18},{... | collective-permute-start | bytes 589832 | tf_op jit(solution)/shard_map/ppermute | solution.py:195
  40.8 4.3 %collective-permute-start.8 = (f32[2,8,8,128]{3,2,1,0:T(8,128)S(1)}, f32[2,8,8,128]{3,2,1,0:T(8,128)S(1)}, u32[]{:S(2)}, u32[]{:S(2)}) collective-permute-start(f32[2,8,8,128]{3,2,1,0:T(8,128)S(1)} %get-tuple-element.31), channel_id=1, source_target_pairs={{0,4},{4,0},{1,5},{5,1},{2,6},{6,2},{3,7},{7,3},{8,12},{12,8},{9,1... | collective-permute-start | bytes 196616 | tf_op jit(solution)/shard_map/ppermute | solution.py:599

commit v3 on v0

v3 whole, which is shorter than its diff:
```python
import jax
import jax.numpy as jnp
from jax import lax
from jax.experimental import pallas as pl
from jax.experimental.pallas import tpu as pltpu
from jax.sharding import PartitionSpec as P


BOX = 16
SOURCE_ROWS = 12
COEFF_ROWS = SOURCE_ROWS + 1
MID_ROWS = 6
FINE_ROWS = 4
Z_PAIRS = 16
LANES = 128
HIGH = lax.Precision.HIGHEST
F32 = jnp.float32
BF16 = jnp.bfloat16


def iota(shape, dim):
    return lax.broadcasted_iota(jnp.int32, shape, dim)


def exact_dot(left, right):
    return lax.dot_general(
        left, right, (((1,), (0,)), ((), ())), precision=HIGH, preferred_element_type=F32
    )


def even_rows(shape, dims):
    total = iota(shape, dims[0])
    for dim in dims[1:]:
        total = total + iota(shape, dim)
    return total % 2 == 0


def call(kernel, outs, scratch=(), room=8):
    return pl.pallas_call(
        kernel,
        out_shape=outs,
        scratch_shapes=list(scratch),
        compiler_params=pltpu.CompilerParams(vmem_limit_bytes=room * 1024 * 1024),
    )


def shape_f32(*dims):
    return jax.ShapeDtypeStruct(dims, F32)


class Geometry:
    def __init__(self, sizes, block):
        self.gx, self.gy, self.gz = sizes
        self.bx, self.by, self.bz = block
        self.swap = self.gy == 2
        self.wx = 3 * self.bx
        self.wy = (2 if self.swap else 3) * self.by
        self.cx, self.cy = self.bx // 2, self.by // 2
        self.mx, self.my = self.wx // 2, self.wy // 2
        self.devices = self.gx * self.gy * self.gz
        self.fy = self.by + (8 if self.swap else 16)

    def kept_y(self):
        if self.swap:
            start = pl.multiple_of(lax.axis_index("gy") * 8, 8)
            return start, start
        return self.by - 8, 8

    def own_y(self, rows):
        if self.swap:
            return pl.multiple_of(lax.axis_index("gy") * rows, 8)
        return rows


def neighbours_of(count, step):
    if step > 0:
        return [(i, i + 1) for i in range(count - 1)]
    return [(i + 1, i) for i in range(count - 1)]


def from_neighbours(axis, count, low, high):
    return (
        lax.ppermute(high, axis, neighbours_of(count, 1)),
        lax.ppermute(low, axis, neighbours_of(count, -1)),
    )


def pack_coefficient(geo, own):
    bx, by, bz = geo.bx, geo.by, geo.bz
    half = bz // 2

    def kernel(own_ref, out_ref):
        source = iota((bz, bz), 0)
        target = iota((bz, bz), 1)
        wanted = jnp.where(target < half, 2 * target, 2 * (target - half) + 1)
        split = exact_dot(own_ref[...].reshape(bx * by, bz), (source == wanted).astype(F32))
        turned = pltpu.roll(split, half, 1)
        first = even_rows((bx, by, bz), (0, 1))
        out_ref[...] = jnp.where(
            first, split.reshape(bx, by, bz), turned.reshape(bx, by, bz)
        )

    return call(kernel, shape_f32(bx, by, bz))(own)


def widen_coefficient(geo, own):
    if not geo.swap:
        low, high = from_neighbours("gy", geo.gy, own, own)
        center = jnp.concatenate([low, own, high], axis=1)
        return center, center[:COEFF_ROWS], center[geo.bx - COEFF_ROWS :]
    other = lax.ppermute(own, "gy", [(0, 1), (1, 0)])

    def kernel(own_ref, other_ref, center, low, high):
        mine = geo.own_y(geo.by)
        start = pl.multiple_of(geo.by - mine, 8)
        center[:, pl.ds(mine, geo.by), :] = own_ref[...]
        center[:, pl.ds(start, geo.by), :] = other_ref[...]
        low[...] = center[0:COEFF_ROWS]
        high[...] = center[geo.bx - COEFF_ROWS :]

    slab = shape_f32(COEFF_ROWS, geo.wy, geo.bz)
    return call(kernel, [shape_f32(geo.bx, geo.wy, geo.bz), slab, slab])(own, other)


def coefficient_rows(geo):
    rows = [(0, i) for i in range(COEFF_ROWS)]
    rows += [(1, i) for i in range(geo.bx)]
    return rows + [(2, i) for i in range(COEFF_ROWS)]


def pack_ends(geo, parts):
    rows = coefficient_rows(geo)
    lines = -(-len(rows) // 4)

    def kernel(left, center, right, last, first):
        refs = (left, center, right)
        group = iota((geo.wy, LANES), 1) % (LANES // 2) // Z_PAIRS
        for line in range(lines):
            ends = jnp.zeros((geo.wy, LANES), F32)
            starts = ends
            for place, (part, row) in enumerate(rows[4 * line : 4 * line + 4]):
                value = refs[part][row]
                shift = place * Z_PAIRS
                down = pltpu.roll(value, LANES - shift, 1) if shift else value
                up = pltpu.roll(value, shift, 1) if shift else value
                ends = jnp.where(group == 3 - place, down, ends)
                starts = jnp.where(group == place, up, starts)
            last[line] = ends
            first[line] = starts

    packed = shape_f32(lines, geo.wy, LANES)
    return call(kernel, [packed, packed])(*parts)


def pack_source(geo, slots, cells, columns):
    bx, by = geo.bx, geo.by
    count = slots.shape[0] // columns
    tiles = cells // LANES
    boxes = 2 * geo.bz // BOX
    own_boxes = geo.bz // BOX
    per_tile = LANES // BOX
    pair = BOX // 2

    def kernel(slot_ref, center, low, high, *ordered_refs):
        place = iota((count, LANES), 1)
        wanted = jnp.where(place < own_boxes + own_boxes // 2, place, place - boxes)
        wanted = (wanted + lax.axis_index("gz") * own_boxes).astype(F32)
        rows = tiles * per_tile
        keep = iota((tiles, per_tile, LANES), 2) // BOX == iota((tiles, per_tile, LANES), 1)
        inside = iota((LANES, 2 * LANES), 0) % BOX
        target = iota((LANES, 2 * LANES), 1)
        slot_of = jnp.where(inside % 2 == 0, inside // 2, inside // 2 + LANES)
        first = even_rows((bx, by, LANES), (0, 1))
        for column, ordered in enumerate(ordered_refs):
            here = slice(column * count, (column + 1) * count)
            ids = slot_ref[here, cells : cells + LANES].astype(F32)
            chosen = (ids == wanted) & (ids >= 0.0) & (place < boxes)
            chosen = jnp.where(chosen, 1.0, 0.0).T[0:boxes].astype(BF16)
            for tile in range(tiles):
                ordered[tile] = jnp.dot(
                    chosen,
                    slot_ref[here, tile * LANES : (tile + 1) * LANES],
                    preferred_element_type=F32,
                )
            total = jnp.zeros((rows, 2 * LANES), F32)
            for box in range(boxes):
                line = ordered[:, box : box + 1, :]
                line = jnp.broadcast_to(line, (tiles, per_tile, LANES))
                line = jnp.where(keep, line, 0.0).reshape(rows, LANES).astype(BF16)
                spread = (target == slot_of + box * pair).astype(F32).astype(BF16)
                total = total + jnp.dot(line, spread, preferred_element_type=F32)
            even = total[:, 0:LANES].reshape(bx, by, LANES)
            odd = total[:, LANES:].reshape(bx, by, LANES)
            span = slice(column * by, (column + 1) * by)
            center[0, :, span, :] = jnp.where(first, even, odd).astype(BF16)
            center[1, :, span, :] = jnp.where(first, odd, even).astype(BF16)
        low[...] = center[:, 0:SOURCE_ROWS]
        high[...] = center[:, bx - SOURCE_ROWS :]

    def shape(rows):
        return jax.ShapeDtypeStruct((2, rows, columns * by, LANES), BF16)

    return call(
        kernel,
        [shape(bx), shape(SOURCE_ROWS), shape(SOURCE_ROWS)],
        [pltpu.VMEM((tiles, boxes, LANES), F32)] * columns,
        room=12,
    )(slots)


def tag_slots(slots, ids):
    capacity, cells = slots.shape

    def kernel(slot_ref, id_ref, out_ref):
        out_ref[:, 0:cells] = slot_ref[...]
        tags = jnp.broadcast_to(id_ref[...], (capacity, LANES))
        out_ref[:, cells:] = tags.astype(F32).astype(BF16)

    shape = jax.ShapeDtypeStruct((capacity, cells + LANES), BF16)
    return call(kernel, shape)(slots, ids)


def gather_source(geo, old_slots, old_ids):
    capacity, cells = old_slots.shape[2], old_slots.shape[3]
    slots, ids = old_slots.reshape(capacity, cells), old_ids.reshape(capacity, 1)
    axes = ("gy", "gz") if geo.swap else ("gz",)
    column = lax.all_gather(tag_slots(slots, ids), axes, axis=0, tiled=True)
    if geo.swap:
        return pack_source(geo, column, cells, 2)
    own = pack_source(geo, column, cells, 1)[0]
    low, high = from_neighbours("gy", geo.gy, own, own)
    center = jnp.concatenate([low, own, high], axis=2)
    return center, center[:, :SOURCE_ROWS], center[:, geo.bx - SOURCE_ROWS :]


PAD = 8


def padded(rows, width):
    return pltpu.VMEM((rows + 2, width + 2 * PAD, LANES), F32)


def clear_pads(ref):
    rows, width = ref.shape[0] - 2, ref.shape[1] - 2 * PAD
    ref[0] = jnp.zeros((width + 2 * PAD, LANES), F32)
    ref[rows + 1] = jnp.zeros((width + 2 * PAD, LANES), F32)
    edge = jnp.zeros((rows + 2, PAD, LANES), F32)
    ref[:, 0:PAD, :] = edge
    ref[:, PAD + width :, :] = edge


def inner(ref, row):
    return ref[row + 1, PAD : ref.shape[1] - PAD, :]


def put(ref, row, value):
    ref[row + 1, PAD : ref.shape[1] - PAD, :] = value


def across(ref, row):
    width = ref.shape[1] - 2 * PAD
    total = inner(ref, row - 1) + inner(ref, row + 1)
    total = total + ref[row + 1, PAD - 1 : PAD - 1 + width, :]
    return total + ref[row + 1, PAD + 1 : PAD + 1 + width, :]


def fine_sum(ref, row, near_low):
    here = inner(ref, row)
    low = pltpu.roll(here, 1, 1)
    high = pltpu.roll(here, LANES - 1, 1)
    return across(ref, row) + here + jnp.where(near_low, low, high)


def mid_sum(ref, row):
    here = inner(ref, row)
    return across(ref, row) + pltpu.roll(here, 1, 1) + pltpu.roll(here, LANES - 1, 1)


def over_rows(span, mask, body):
    first, last = span
    flipped = jnp.logical_not(mask)

    def step(index, carry):
        body(first + 2 * index, mask)
        body(first + 2 * index + 1, flipped)
        return carry

    lax.fori_loop(0, (last - first) // 2, step, 0, unroll=(last - first) // 2)


def low_rows(width):
    return iota((width, LANES), 0) % 2 == 0


def red_lanes(width):
    return (iota((width, LANES), 0) + iota((width, LANES), 1)) % 2 == 0


def weights(coeff_row, total):
    return jnp.where(coeff_row > 0.0, 1.0 / total, 0.0)


def fine_half(span, colour, coeff, weight, source, values, scaled):
    other = 1 - colour

    def body(row, low):
        near_low = low if colour == 0 else jnp.logical_not(low)
        mine = inner(coeff[colour], row)
        summed = mine * fine_sum(values[other], row, near_low)
        summed = summed + fine_sum(scaled[other], row, near_low)
        fresh = weight[colour][row] * (source[colour][row] + summed)
        put(values[colour], row, fresh)
        put(scaled[colour], row, mine * fresh)

    over_rows(span, low_rows(coeff[0].shape[1] - 2 * PAD), body)


def mid_half(span, colour, coeff, weight, source, values, scaled):
    def body(row, red):
        chosen = red if colour == 0 else jnp.logical_not(red)
        mine = inner(coeff, row)
        summed = mine * mid_sum(values, row) + mid_sum(scaled, row)
        fresh = weight[row] * (source[row] + summed)
        fresh = jnp.where(chosen, fresh, inner(values, row))
        put(values, row, fresh)
        put(scaled, row, mine * fresh)

    over_rows(span, red_lanes(coeff.shape[1] - 2 * PAD), body)


def shrink(span, rows):
    first, last = span[0] + rows, span[1] - rows
    return first - first % 2, last + last % 2


def way_down(geo, coefficient, ends, source):
    bx, wx, wy, mx, my = geo.bx, geo.wx, geo.wy, geo.mx, geo.my
    cx, cy = geo.cx, geo.cy
    lx, ly = cx // 2, cy // 2
    rows = coefficient_rows(geo)
    top = bx - COEFF_ROWS
    share = geo.bz // 4
    kept = (bx - FINE_ROWS, 2 * bx + FINE_ROWS)
    depth = kept[1] - kept[0]

    def kernel(*refs):
        coeff_in, (before, after), source_in = refs[0:3], refs[3:5], refs[5:8]
        payload, sent_low, sent_high, center, mid_coeff, mid_weight = refs[8:14]
        out_black, out_coeff, out_weight, out_source = refs[14:18]
        kr, kb, vr, vb, wr, wb, weight_r, weight_b, source_r, source_b = refs[18:28]
        diag, resid, mc, mv, mw, mid_source, mid_diag = refs[28:]
        coeff, values, scaled = (kr, kb), (vr, vb), (wr, wb)
        weight, sources = (weight_r, weight_b), (source_r, source_b)
        for ref in (kr, kb, vr, vb, wr, wb, mc, mv, mw):
            clear_pads(ref)

        lane = iota((wy, LANES), 1)
        is_own, is_after = lane < LANES // 2, lane < LANES // 2 + Z_PAIRS
        is_before = lane >= LANES - Z_PAIRS
        for index, (part, row) in enumerate(rows):
            line, shift = index // 4, index % 4 * Z_PAIRS
            own, prior, later = coeff_in[part][row], before[line], after[line]
            for colour, own_turn, turn in ((0, 0, LANES // 2), (1, LANES // 2, 0)):
                lanes = pltpu.roll(own, own_turn, 1) if own_turn else own
                after_turn = (turn - shift) % LANES
                before_turn = (turn + shift) % LANES
                near = pltpu.roll(later, after_turn, 1) if after_turn else later
                past = pltpu.roll(prior, before_turn, 1) if before_turn else prior
                lanes = jnp.where(
                    is_own,
                    lanes,
                    jnp.where(is_after, near, jnp.where(is_before, past, 0.0)),
                )
                put(coeff[colour], top + index, 0.5 * lanes)
        edge = jnp.zeros((wy, LANES), F32)
        for colour in (0, 1):
            for row in (*range(top), *range(top + len(rows), wx)):
                put(coeff[colour], row, edge)
            sources[colour][bx - SOURCE_ROWS : bx] = source_in[0][colour].astype(F32)
            sources[colour][bx : 2 * bx] = source_in[1][colour].astype(F32)
            sources[colour][2 * bx : 2 * bx + SOURCE_ROWS] = source_in[2][colour].astype(F32)

        span = (bx - SOURCE_ROWS, 2 * bx + SOURCE_ROWS)
        lower = low_rows(wy)

        def first_red(row, low):
            mine = inner(kr, row)
            total = 6.0 * mine + fine_sum(kb, row, low)
            inverse = weights(mine, total)
            diag[row] = total
            weight_r[row] = inverse
            fresh = inverse * source_r[row]
            put(vr, row, fresh)
            put(wr, row, mine * fresh)

        over_rows(span, lower, first_red)

        def black_weight(row, low):
            mine = inner(kb, row)
            total = 6.0 * mine + fine_sum(kr, row, jnp.logical_not(low))
            weight_b[row] = weights(mine, total)

        over_rows(shrink(span, 1), lower, black_weight)
        fine_half(shrink(span, 1), 1, coeff, weight, sources, values, scaled)
        fine_half(shrink(span, 2), 0, coeff, weight, sources, values, scaled)
        fine_half(shrink(span, 3), 1, coeff, weight, sources, values, scaled)

        def residual(row, low):
            mine = inner(kr, row)
            summed = mine * fine_sum(vb, row, low) + fine_sum(wb, row, low)
            resid[row] = source_r[row] + summed - diag[row] * inner(vr, row)

        over_rows(shrink(span, 4), lower, residual)
        kept_at = geo.kept_y()[0]
        strip = pl.ds(kept_at, geo.fy)
        inner_strip = pl.ds(pl.multiple_of(kept_at + PAD, 8), geo.fy)
        for row in range(depth):
            at = kept[0] + row
            out_black[row] = vb[at + 1, inner_strip, :]
            for colour in (0, 1):
                out_coeff[colour, row] = coeff[colour][at + 1, inner_strip, :]
                out_weight[colour, row] = weight[colour][at, strip, :]
                out_source[colour, row] = sources[colour][at, strip, :].astype(BF16)

        mid_span = (cx - SOURCE_ROWS // 2, 2 * cx + SOURCE_ROWS // 2)
        mid_sourced = shrink(mid_span, 2)
        blank = jnp.zeros((my, LANES), F32)
        for row in range(mx):
            if not mid_span[0] <= row < mid_span[1]:
                put(mc, row, blank)
                put(mv, row, blank)
                put(mw, row, blank)
                continue
            at = 2 * row
            diag[at] = (inner(kr, at) + inner(kr, at + 1)) + (inner(kb, at) + inner(kb, at + 1))
            total = diag[at, pl.ds(0, my, 2), :] + diag[at, pl.ds(1, my, 2), :]
            put(mc, row, 0.125 * total)
            if mid_sourced[0] <= row < mid_sourced[1]:
                resid[at] = resid[at] + resid[at + 1]
                total = resid[at, pl.ds(0, my, 2), :] + resid[at, pl.ds(1, my, 2), :]
                mid_source[row] = 0.5 * total
            else:
                mid_source[row] = blank

        def mid_red(row, red):
            mine = inner(mc, row)
            total = 6.0 * mine + mid_sum(mc, row)
            inverse = weights(mine, total)
            mid_diag[row] = total
            mid_weight[row] = inverse
            fresh = jnp.where(red, inverse * mid_source[row], 0.0)
            put(mv, row, fresh)
            put(mw, row, mine * fresh)

        over_rows(mid_span, red_lanes(my), mid_red)
        for rows_off, colour in ((1, 1), (2, 0), (3, 1)):
            mid_half(
                shrink(mid_sourced, rows_off), colour, mc, mid_weight, mid_source, mv, mw
            )
        own = (cx, 2 * cx)

        def mid_residual(row, red):
            mine = inner(mc, row)
            summed = mine * mid_sum(mv, row) + mid_sum(mw, row)
            left = mid_source[row] + summed - mid_diag[row] * inner(mv, row)
            mid_diag[row] = jnp.where(red, 0.25 * left, 0.0)

        over_rows(own, red_lanes(my), mid_residual)
        for row in range(mx):
            mid_coeff[row] = inner(mc, row)
        for row in range(cx):
            center[0, row] = inner(mv, cx + row)
            center[1, row] = mid_source[cx + row]
        sent_low[...] = center[:, 0:MID_ROWS]
        sent_high[...] = center[:, cx - MID_ROWS :]

        start = geo.own_y(cy)
        parts = []
        for cell in range(lx):
            at = cx + 2 * cell
            mid_diag[at] = mid_diag[at] + mid_diag[at + 1]
            mid_diag[at + 1] = inner(mc, at) + inner(mc, at + 1)
            halves = []
            for row in (at, at + 1):
                first = mid_diag[row, pl.ds(start, ly, 2), :]
                halves.append(first + mid_diag[row, pl.ds(start + 1, ly, 2), :])
            parts.append(jnp.concatenate(halves, axis=0))
        from_lane = iota((LANES, LANES), 0)
        to_lane = iota((LANES, LANES), 1)
        total = jnp.zeros((2 * ly, LANES), F32)
        for cell in range(lx):
            fold = (to_lane == from_lane // 2 + cell * share) & (from_lane < 2 * share)
            total = total + exact_dot(parts[cell], jnp.where(fold, 0.125, 0.0))
        payload[...] = jnp.broadcast_to(total[None], payload.shape)

    slab = shape_f32(2, MID_ROWS, my, LANES)
    middle = shape_f32(mx, my, LANES)
    both = shape_f32(2, depth, geo.fy, LANES)
    source_kept = jax.ShapeDtypeStruct((2, depth, geo.fy, LANES), BF16)
    plain = pltpu.VMEM((wx, wy, LANES), F32)
    small = pltpu.VMEM((mx, my, LANES), F32)
    return call(
        kernel,
        [
            shape_f32(geo.devices, 2 * ly, LANES),
            slab,
            slab,
            shape_f32(2, cx, my, LANES),
            middle,
            middle,
            shape_f32(depth, geo.fy, LANES),
            both,
            both,
            source_kept,
        ],
        [padded(wx, wy)] * 6 + [plain] * 6 + [padded(mx, my)] * 3 + [small] * 2,
        room=20 if geo.swap else 40,
    )(*coefficient, *ends, *source)


def low_shift(values, dim, step):
    size = values.shape[dim]
    if dim == 0:
        blank = jnp.zeros_like(values[0:1])
        if step < 0:
            return jnp.concatenate([blank, values[:-1]], axis=0)
        return jnp.concatenate([values[1:], blank], axis=0)
    turned = pltpu.roll(values, 1 if step < 0 else size - 1, dim)
    edge = 0 if step < 0 else size - 1
    return jnp.where(iota(values.shape, dim) == edge, 0.0, turned)


def low_sum(values):
    total = low_shift(values, 0, -1) + low_shift(values, 0, 1)
    for dim in (1, 2):
        total = total + low_shift(values, dim, -1) + low_shift(values, dim, 1)
    return total


def bottom_solve(rhs, half_coeff):
    diag = 6.0 * half_coeff + low_sum(half_coeff)

    def apply(values):
        summed = half_coeff * low_sum(values) + low_sum(half_coeff * values)
        return (diag * values - summed) * 0.0625

    image = apply(rhs)
    alpha = jnp.sum(rhs * rhs) / jnp.sum(rhs * image)
    rest = rhs - alpha * image
    turned = apply(rest)
    omega = jnp.sum(turned * rest) / jnp.sum(turned * turned)
    return alpha * rhs + omega * rest


def lift_bottom(geo, lows):
    bz, mx, my = geo.bz, geo.mx, geo.my
    cx, cy = geo.cx, geo.cy
    block_x, block_y = cx // 2, cy // 2
    lx, ly = geo.gx * block_x, geo.gy * block_y
    share = bz // 4
    groups = LANES // share
    columns = geo.gz * share

    def kernel(low_ref, out_ref, low_full, spread):
        lane = iota((2 * block_y, LANES), 1) // share
        for ix in range(geo.gx):
            for iy in range(geo.gy):
                for group in range(block_x):
                    for tile in range(columns // LANES):
                        total = jnp.zeros((2 * block_y, LANES), F32)
                        for part in range(groups):
                            device = (ix * geo.gy + iy) * geo.gz + tile * groups + part
                            piece = low_ref[device]
                            shift = ((part - group) * share) % LANES
                            if shift:
                                piece = pltpu.roll(piece, shift, 1)
                            total = jnp.where(lane == part, piece, total)
                        at = slice(tile * LANES, (tile + 1) * LANES)
                        to = slice(iy * block_y, (iy + 1) * block_y)
                        low_full[0, ix * block_x + group, to, at] = total[0:block_y]
                        low_full[1, ix * block_x + group, to, at] = total[block_y:]
        bottom = bottom_solve(low_full[0], low_full[1])

        target = iota((columns, LANES), 1)
        target = jnp.where(target < LANES // 2 + LANES // 4, target, target - LANES)
        wanted = (target + LANES) // 2 - LANES // 2 + lax.axis_index("gz") * share
        copy = (iota((columns, LANES), 0) == wanted).astype(F32)
        fetched = exact_dot(bottom.reshape(lx * ly, columns), copy).reshape(lx, ly, LANES)
        edge = jnp.zeros((lx, PAD, LANES), F32)
        spread[:, 0:PAD, :] = edge
        spread[:, PAD + 2 * ly :, :] = edge
        for cell in range(lx):
            spread[cell, pl.ds(PAD, ly, 2), :] = fetched[cell]
            spread[cell, pl.ds(PAD + 1, ly, 2), :] = fetched[cell]
        begin = PAD + lax.axis_index("gy") * cy - geo.own_y(cy)
        begin = PAD if geo.swap else pl.multiple_of(begin, 8)
        first_x = lax.axis_index("gx") * block_x - block_x
        for cell in range(mx // 2):
            at = jnp.clip(first_x + cell, 0, lx - 1)
            out_ref[cell] = spread[at, pl.ds(begin, my), :]

    return call(
        kernel,
        shape_f32(mx // 2, my, LANES),
        [
            pltpu.VMEM((2, lx, ly, columns), F32),
            pltpu.VMEM((lx, 2 * ly + 2 * PAD, LANES), F32),
        ],
        room=8 if geo.swap else 24,
    )(lows)


def way_up(geo, lifted_low, mids, fines):
    bx, by, bz, wy, mx, my = geo.bx, geo.by, geo.bz, geo.wy, geo.mx, geo.my
    cx = geo.cx
    depth = bx + 2 * FINE_ROWS

    def kernel(*refs):
        low_ref, left, center, right, mid_coeff, mid_weight = refs[0:6]
        fine_black, fine_coeff, fine_weight, fine_source = refs[6:10]
        out_ref = refs[10]
        mc, mv, mw, mid_source, up, source_r, source_b = refs[11:18]
        kr, kb, vr, vb, wr, wb = refs[18:]
        for ref in (mc, mv, mw, kr, kb, vr, vb, wr, wb):
            clear_pads(ref)
        mid_span = (cx - MID_ROWS, 2 * cx + MID_ROWS)
        for row in range(mx):
            put(mc, row, mid_coeff[row])
            if not mid_span[0] <= row < mid_span[1]:
                put(mv, row, jnp.zeros((my, LANES), F32))
                put(mw, row, jnp.zeros((my, LANES), F32))
                continue
            if row < cx:
                part, place = left, row - mid_span[0]
            elif row < 2 * cx:
                part, place = center, row - cx
            else:
                part, place = right, row - 2 * cx
            mine = mid_coeff[row]
            fresh = part[0, place] + jnp.where(mine > 0.0, low_ref[row // 2], 0.0)
            mid_source[row] = part[1, place]
            put(mv, row, fresh)
            put(mw, row, mine * fresh)
        for rows_off, colour in ((1, 0), (2, 1), (3, 0), (4, 1)):
            mid_half(shrink(mid_span, rows_off), colour, mc, mid_weight, mid_source, mv, mw)

        first_mid = cx - FINE_ROWS // 2
        for cell in range(depth // 2):
            line = inner(mv, first_mid + cell)
            up[cell, pl.ds(0, my, 2), :] = line
            up[cell, pl.ds(1, my, 2), :] = line
        kept_at, own_at = geo.kept_y()
        for row in range(depth):
            red, black = fine_coeff[0, row], fine_coeff[1, row]
            put(kr, row, red)
            put(kb, row, black)
            source_r[row] = fine_source[0, row].astype(F32)
            source_b[row] = fine_source[1, row].astype(F32)
            lifted = up[row // 2, pl.ds(kept_at, geo.fy), :]
            fresh = fine_black[row] + jnp.where(black > 0.0, lifted, 0.0)
            put(vb, row, fresh)
            put(wb, row, black * fresh)
        coeff, values, scaled = (kr, kb), (vr, vb), (wr, wb)
        weight = (fine_weight.at[0], fine_weight.at[1])
        source = (source_r, source_b)
        for rows_off, colour in ((1, 0), (2, 1), (3, 0), (4, 1)):
            span = shrink((0, depth), rows_off)
            fine_half(span, colour, coeff, weight, source, values, scaled)

        own = pl.multiple_of(own_at + PAD, 8)
        span = slice(FINE_ROWS + 1, FINE_ROWS + 1 + bx)
        red = vr[span, pl.ds(own, by), :]
        black = vb[span, pl.ds(own, by), :]
        even_first = even_rows((bx, by, LANES), (0, 1))
        even = jnp.where(even_first, red, black).reshape(bx * by, LANES)
        odd = jnp.where(even_first, black, red).reshape(bx * by, LANES)
        from_lane = iota((LANES, bz), 0)
        to_lane = iota((LANES, bz), 1)
        result = exact_dot(even, (to_lane == 2 * from_lane).astype(F32))
        result = result + exact_dot(odd, (to_lane == 2 * from_lane + 1).astype(F32))
        out_ref[...] = result.reshape(bx, by, bz)

    return call(
        kernel,
        shape_f32(bx, by, bz),
        [
            padded(mx, my),
            padded(mx, my),
            padded(mx, my),
            pltpu.VMEM((mx, my, LANES), F32),
            pltpu.VMEM((depth // 2, wy, LANES), F32),
        ]
        + [pltpu.VMEM((depth, geo.fy, LANES), F32)] * 2
        + [padded(depth, geo.fy)] * 6,
        room=12 if geo.swap else 40,
    )(lifted_low, *mids, *fines)


def middle_neighbours(geo, center, low, high):
    if not geo.swap:
        own = center[:, :, geo.cy : 2 * geo.cy]
        before, after = from_neighbours("gy", geo.gy, own, own)
        center = jnp.concatenate([before, own, after], axis=2)
        low, high = center[:, :MID_ROWS], center[:, geo.cx - MID_ROWS :]
    left, right = from_neighbours("gx", geo.gx, low, high)
    return left, center, right


def per_device(geo, old_slots, old_ids, coefficient):
    center_k, low_k, high_k = widen_coefficient(geo, pack_coefficient(geo, coefficient))
    left_k, right_k = from_neighbours("gx", geo.gx, low_k, high_k)
    parts = (left_k, center_k, right_k)
    last, first = pack_ends(geo, parts)
    ends = from_neighbours("gz", geo.gz, first, last)

    center_f, low_f, high_f = gather_source(geo, old_slots, old_ids)
    left_f, right_f = from_neighbours("gx", geo.gx, low_f, high_f)

    payload, low_m, high_m, center_m, mid_coeff, mid_weight, *fines = way_down(
        geo, parts, ends, (left_f, center_f, right_f)
    )
    around = middle_neighbours(geo, center_m, low_m, high_m)
    lows = lax.all_to_all(payload, ("gx", "gy", "gz"), 0, 0, tiled=True)
    lifted = lift_bottom(geo, lows)
    return way_up(geo, lifted, (*around, mid_coeff, mid_weight), fines)


def solution(mesh):
    sizes = tuple(mesh.shape[name] for name in ("gx", "gy", "gz"))

    def body(old_slots, old_ids, old_owner, coefficient):
        del old_owner
        geo = Geometry(sizes, coefficient.shape)
        return per_device(geo, old_slots, old_ids, coefficient)

    in_specs = (
        P("gx", "gy", "gz", None),
        P("gx", "gy", "gz"),
        P("gx", "gy", None),
        P("gx", "gy", "gz"),
    )
    return jax.shard_map(
        body, mesh=mesh, in_specs=in_specs, out_specs=P("gx", "gy", "gz"), check_vma=False
    )
```

time: 554 us -> 65 us (0.12); the launches traced: 547 us -> 64.6 us
  starting transfers between devices: 221 us -> 30 us
  waiting for transfers between devices: 175 us -> 11.6 us
  blocking collectives: 80.9 us -> 9.91 us
  other arithmetic: 32.8 us -> 0 us
  local copies, waits for them, and re-layouts: 31.5 us -> 1 us
  Pallas kernels: 0 us -> 12 us
    ppermute x108 -> x9, starting transfers between devices: 218 us -> 22.2 us  [the longest x4 14 us: from_neighbours(): lax.ppermute(high, axis, neighbours_of(count, 1))]
    ppermute x108 -> x9, waiting for transfers between devices: 175 us -> 8.36 us  [the longest x4 4.85 us: from_neighbours(): lax.ppermute(low, axis, neighbours_of(count, -1))]
    psum x2 -> x0, blocking collectives: 80.9 us -> none  [dot_pair(): return lax.psum((first_term, second_term), ('gx', 'gy', 'gz'))]
    reshape x8 -> x1, local copies, waits for them, and re-layouts: 24.1 us -> 0.08 us  [gather_source(): old_ids.reshape(capacity, 1)]
    pallas_call x0 -> x8, Pallas kernels: none -> 12 us  [the longest x1 5.89 us: way_down(): call(kernel, [shape_f32(geo.devices, 2 * ly, LANES), slab, slab, shape_f3...]
    select_n x19 -> x0, other arithmetic: 11.8 us -> none  [the longest x14 9.6 us: relax(): return jnp.where(chosen, fresh, inner(padded))]
    reduce_sum x8 -> x0, other arithmetic: 11 us -> none  [the longest x4 8.39 us: coarsen(): return grouped.mean(axis=(1, 3, 5))]
    all_gather x0 -> x1, blocking collectives: none -> 9.91 us  [gather_source(): column = lax.all_gather(tag_slots(slots, ids), axes, axis=0, tiled=True)]
  transfers between devices with their start and end apart: 109 -> 10, of which waited for: 50 -> 4; matrix products, arithmetic and copies ran while one was open for 5% -> 0% of each run, Pallas kernels for 0% -> 5%
where the time goes in v3:
time: 65 us; the launch traced here: 64.6 us
  starting transfers between devices  30 us (46%)
  Pallas kernels  12 us (18%)
  waiting for transfers between devices  11.6 us (18%)
  blocking collectives  9.91 us (15%)
  local copies, waits for them, and re-layouts  1 us (2%)
    ppermute x4, starting transfers between devices, from_neighbours(): lax.ppermute(high, axis, neighbours_of(count, 1))  14 us
    all_gather x1, blocking collectives, gather_source(): column = lax.all_gather(tag_slots(slots, ids), axes, axis=0, tiled=True)  9.91 us
    all_to_all x1, starting transfers between devices, per_device(): lows = lax.all_to_all(payload, ('gx', 'gy', 'gz'), 0, 0, tiled=True)  7.84 us
    pallas_call x1, Pallas kernels, way_down(): call(kernel, [shape_f32(geo.devices, 2 * ly, LANES), slab, slab, shape_f3...  5.89 us
    ppermute x4, starting transfers between devices, from_neighbours(): lax.ppermute(low, axis, neighbours_of(count, -1))  5.17 us
    ppermute x4, waiting for transfers between devices, from_neighbours(): lax.ppermute(low, axis, neighbours_of(count, -1))  4.85 us
    ppermute x1, waiting for transfers between devices, widen_coefficient(): other = lax.ppermute(own, 'gy', [(0, 1), (1, 0)])  3.5 us
    all_to_all x1, waiting for transfers between devices, per_device(): lows = lax.all_to_all(payload, ('gx', 'gy', 'gz'), 0, 0, tiled=True)  3.22 us
  transfers between devices with their start and end apart: 10, of which 4 were waited for; matrix products, arithmetic and copies ran while one was open for 0% of the time, Pallas kernels for 5%

profile of v3, /device:TPU:0, one launch (start us, length us, event | category | flops | bytes accessed | tf_op | source)
XLA Modules:
  0.0 64.6 jit_solution(4657088375820069437)
XLA Ops:
  0.0 0.0 copy-start
  0.0 0.9 %copy-done = f32[16,16,128]{2,1,0:T(8,128)S(1)} copy-done((f32[16,16,128]{2,1,0:T(8,128)S(1)}, f32[16,16,128]{2,1,0:T(8,128)}, u32[]{:S(2)}) %copy-start) | copy-done | bytes 131096
  0.9 0.3 shard_map.37.own_ref
  1.2 0.0 copy-start.1
  1.3 3.0 %collective-permute-start = (f32[16,16,128]{2,1,0:T(8,128)S(1)}, f32[16,16,128]{2,1,0:T(8,128)S(1)}, u32[]{:S(2)}, u32[]{:S(2)}) collective-permute-start(f32[16,16,128]{2,1,0:T(8,128)S(1)} %shard_map.37.own_ref), channel_id=1, source_target_pairs={{0,4},{4,0},{1,5},{5,1},{2,6},{6,2},{3,7},{7,3},{8,12},{12,8},{9,1... | collective-permute-start | bytes 393224 | tf_op jit(solution)/shard_map/ppermute | solution.py:111
  4.3 3.5 %collective-permute-done.other_ref = f32[16,16,128]{2,1,0:T(8,128)S(1)} collective-permute-done((f32[16,16,128]{2,1,0:T(8,128)S(1)}, f32[16,16,128]{2,1,0:T(8,128)S(1)}, u32[]{:S(2)}, u32[]{:S(2)}) %collective-permute-start) | collective-permute-done | bytes 131104 | tf_op jit(solution)/shard_map/ppermute | solution.py:111
  7.8 0.1 shard_map.38
  7.9 3.7 %collective-permute-start.1 = (f32[13,32,128]{2,1,0:T(8,128)S(1)}, f32[13,32,128]{2,1,0:T(8,128)S(1)}, u32[]{:S(2)}, u32[]{:S(2)}) collective-permute-start(f32[13,32,128]{2,1,0:T(8,128)S(1)} %get-tuple-element.23), channel_id=1, source_target_pairs={{0,8},{8,16},{16,24},{1,9},{9,17},{17,25},{2,10},{10,18},{18,26},{... | collective-permute-start | bytes 638984 | tf_op jit(solution)/shard_map/ppermute | solution.py:83
  11.6 0.0 copy-start.2
  11.6 1.3 %collective-permute-start.2 = (f32[13,32,128]{2,1,0:T(8,128)S(1)}, f32[13,32,128]{2,1,0:T(8,128)S(1)}, u32[]{:S(2)}, u32[]{:S(2)}) collective-permute-start(f32[13,32,128]{2,1,0:T(8,128)S(1)} %get-tuple-element.25), channel_id=1, source_target_pairs={{8,0},{16,8},{24,16},{9,1},{17,9},{25,17},{10,2},{18,10},{26,18},{... | collective-permute-start | bytes 638984 | tf_op jit(solution)/shard_map/ppermute | solution.py:84
  12.9 0.0 copy-done.2
  12.9 0.1 copy.4.id_ref
  13.0 0.0 copy-done.1
  13.0 0.1 shard_map.40
  13.1 9.9 %all_gather.3.slot_ref = bf16[64,4224]{1,0:T(8,128)(2,1)S(1)} all-gather(bf16[8,4224]{1,0:T(8,128)(2,1)S(1)} %shard_map.40), channel_id=1, replica_groups=mesh['gx'=4,'gy'=2,'gz'=4] {'gy','gz'}, dimensions={0}, use_global_device_ids=true | all-gather | bytes 608256 | tf_op jit(solution)/shard_map/all_gather | solution.py:227
  23.0 1.6 %shard_map.41 = (bf16[2,16,32,128]{3,2,1,0:T(8,128)(2,1)S(1)}, bf16[2,12,32,128]{3,2,1,0:T(8,128)(2,1)S(1)}, bf16[2,12,32,128]{3,2,1,0:T(8,128)(2,1)S(1)}) custom-call(bf16[64,4224]{1,0:T(8,128)(2,1)S(1)} %all_gather.3.slot_ref), custom_call_target="tpu_custom_call" | custom-call | tf_op jit(solution)/shard_map/pallas_call | solution.py:203
  24.6 4.6 %collective-permute-start.5 = (bf16[2,12,32,128]{3,2,1,0:T(8,128)(2,1)S(1)}, bf16[2,12,32,128]{3,2,1,0:T(8,128)(2,1)S(1)}, u32[]{:S(2)}, u32[]{:S(2)}) collective-permute-start(bf16[2,12,32,128]{3,2,1,0:T(8,128)(2,1)S(1)} %get-tuple-element.28), channel_id=1, source_target_pairs={{0,8},{8,16},{16,24},{1,9},{9,17},{17,25},{2,10},{10,18},{18,26},{... | collective-permute-start | bytes 589832 | tf_op jit(solution)/shard_map/ppermute | solution.py:83
  29.2 1.3 %collective-permute-start.6 = (bf16[2,12,32,128]{3,2,1,0:T(8,128)(2,1)S(1)}, bf16[2,12,32,128]{3,2,1,0:T(8,128)(2,1)S(1)}, u32[]{:S(2)}, u32[]{:S(2)}) collective-permute-start(bf16[2,12,32,128]{3,2,1,0:T(8,128)(2,1)S(1)} %get-tuple-element.30), channel_id=1, source_target_pairs={{8,0},{16,8},{24,16},{9,1},{17,9},{25,17},{10,2},{18,10},{26,18},{... | collective-permute-start | bytes 589832 | tf_op jit(solution)/shard_map/ppermute | solution.py:84
  30.5 0.0 collective-permute-done.1.left.refs_0_
  30.5 0.0 collective-permute-done.2.right.refs_2_
  30.5 0.3 shard_map.39
  30.8 2.0 %collective-permute-start.3 = (f32[11,32,128]{2,1,0:T(8,128)S(1)}, f32[11,32,128]{2,1,0:T(8,128)S(1)}, u32[]{:S(2)}, u32[]{:S(2)}) collective-permute-start(f32[11,32,128]{2,1,0:T(8,128)S(1)} %get-tuple-element.26), channel_id=1, source_target_pairs={{0,1},{1,2},{2,3},{4,5},{5,6},{6,7},{8,9},{9,10},{10,11},{12,13},{... | collective-permute-start | bytes 540680 | tf_op jit(solution)/shard_map/ppermute | solution.py:83
  32.8 1.3 %collective-permute-start.4 = (f32[11,32,128]{2,1,0:T(8,128)S(1)}, f32[11,32,128]{2,1,0:T(8,128)S(1)}, u32[]{:S(2)}, u32[]{:S(2)}) collective-permute-start(f32[11,32,128]{2,1,0:T(8,128)S(1)} %get-tuple-element.27), channel_id=1, source_target_pairs={{1,0},{2,1},{3,2},{5,4},{6,5},{7,6},{9,8},{10,9},{11,10},{13,12},{... | collective-permute-start | bytes 540680 | tf_op jit(solution)/shard_map/ppermute | solution.py:84
  34.1 0.0 collective-permute-done.5.refs_5_
  34.1 3.8 %collective-permute-done.6.refs_7_ = bf16[2,12,32,128]{3,2,1,0:T(8,128)(2,1)S(1)} collective-permute-done((bf16[2,12,32,128]{3,2,1,0:T(8,128)(2,1)S(1)}, bf16[2,12,32,128]{3,2,1,0:T(8,128)(2,1)S(1)}, u32[]{:S(2)}, u32[]{:S(2)}) %collective-permute-start.6) | collective-permute-done | bytes 196640 | tf_op jit(solution)/shard_map/ppermute | solution.py:84
  37.9 0.0 collective-permute-done.3.refs_3_
  37.9 0.0 collective-permute-done.4.refs_4_
  37.9 5.9 %shard_map.42 = (f32[32,8,128]{2,1,0:T(8,128)}, f32[2,6,16,128]{3,2,1,0:T(8,128)S(1)}, f32[2,6,16,128]{3,2,1,0:T(8,128)S(1)}, f32[2,8,16,128]{3,2,1,0:T(8,128)S(...) custom-call(f32[13,32,128]{2,1,0:T(8,128)S(1)} %collective-permute-d, ...), custom_call_target="tpu_custom_call" | custom-call | tf_op jit(solution)/shard_map/pallas_call | solution.py:502
  43.8 7.8 %all-to-all-start = ((f32[32,8,128]{2,1,0:T(8,128)}), f32[32,8,128]{2,1,0:T(8,128)S(1)}, u32[]{:S(2)}, u32[]{:S(2)}) async-start(f32[32,8,128]{2,1,0:T(8,128)} %get-tuple-element.31), calls=%async_computation | async-start | bytes 262144 | tf_op jit(solution)/shard_map/all_to_all | solution.py:723
  51.7 3.7 %collective-permute-start.7 = (f32[2,6,16,128]{3,2,1,0:T(8,128)S(1)}, f32[2,6,16,128]{3,2,1,0:T(8,128)S(1)}, u32[]{:S(2)}, u32[]{:S(2)}) collective-permute-start(f32[2,6,16,128]{3,2,1,0:T(8,128)S(1)} %get-tuple-element.32), channel_id=1, source_target_pairs={{0,8},{8,16},{16,24},{1,9},{9,17},{17,25},{2,10},{10,18},{18,26},{... | collective-permute-start | bytes 294920 | tf_op jit(solution)/shard_map/ppermute | solution.py:83
  55.4 1.3 %collective-permute-start.8 = (f32[2,6,16,128]{3,2,1,0:T(8,128)S(1)}, f32[2,6,16,128]{3,2,1,0:T(8,128)S(1)}, u32[]{:S(2)}, u32[]{:S(2)}) collective-permute-start(f32[2,6,16,128]{3,2,1,0:T(8,128)S(1)} %get-tuple-element.34), channel_id=1, source_target_pairs={{8,0},{16,8},{24,16},{9,1},{17,9},{25,17},{10,2},{18,10},{26,18},{... | collective-permute-start | bytes 294920 | tf_op jit(solution)/shard_map/ppermute | solution.py:84
  56.7 3.2 %all-to-all-done.low_ref = f32[32,8,128]{2,1,0:T(8,128)S(1)} async-done(((f32[32,8,128]{2,1,0:T(8,128)}), f32[32,8,128]{2,1,0:T(8,128)S(1)}, u32[]{:S(2)}, u32[]{:S(2)}) %all-to-all-start) | async-done | bytes 131104 | tf_op jit(solution)/shard_map/all_to_all | solution.py:723
  59.9 0.9 %shard_map.43.refs_0_ = f32[12,16,128]{2,1,0:T(8,128)S(1)} custom-call(f32[32,8,128]{2,1,0:T(8,128)S(1)} %all-to-all-done.low_ref), custom_call_target="tpu_custom_call" | custom-call | tf_op jit(solution)/shard_map/pallas_call | solution.py:602
  60.8 0.0 collective-permute-done.7.refs_1_
  60.8 1.0 %collective-permute-done.8.refs_3_ = f32[2,6,16,128]{3,2,1,0:T(8,128)S(1)} collective-permute-done((f32[2,6,16,128]{3,2,1,0:T(8,128)S(1)}, f32[2,6,16,128]{3,2,1,0:T(8,128)S(1)}, u32[]{:S(2)}, u32[]{:S(2)}) %collective-permute-start.8) | collective-permute-done | bytes 98336 | tf_op jit(solution)/shard_map/ppermute | solution.py:84
  61.9 2.7 %shard_map.44 = f32[16,16,128]{2,1,0:T(8,128)} custom-call(f32[12,16,128]{2,1,0:T(8,128)S(1)} %shard_map.43.refs_0_, f32[2,6,16,128]{3,2,1,0:T(8,128)S(1)} %collective-permute-done.7.refs_1_, f32[2,8,16,128]{3,2,1,0:T(8,128)S(1)} %get-tuple-element.33.refs_2_, f32[2,6,16,128]{3,2,1,0:T(8,128)S(1)} %collective-permute-done.8.refs_3_, ...), custom_call_target="tpu_custom_call" | custom-call | tf_op jit(solution)/shard_map/pallas_call | solution.py:683
Async XLA Ops:
  0.0 0.9 %copy-start = (f32[16,16,128]{2,1,0:T(8,128)S(1)}, f32[16,16,128]{2,1,0:T(8,128)}, u32[]{:S(2)}) copy-start(f32[16,16,128]{2,1,0:T(8,128)} %own_ref.1) | copy-start | bytes 393220
  1.2 11.8 %copy-start.1 = (bf16[1,1,8,4096]{3,2,1,0:T(8,128)(2,1)S(1)}, bf16[1,1,8,4096]{3,2,1,0:T(8,128)(2,1)}, u32[]{:S(2)}) copy-start(bf16[1,1,8,4096]{3,2,1,0:T(8,128)(2,1)} %param.4) | copy-start | bytes 196612
  1.3 6.5 %collective-permute-start = (f32[16,16,128]{2,1,0:T(8,128)S(1)}, f32[16,16,128]{2,1,0:T(8,128)S(1)}, u32[]{:S(2)}, u32[]{:S(2)}) collective-permute-start(f32[16,16,128]{2,1,0:T(8,128)S(1)} %shard_map.37.own_ref), channel_id=1, source_target_pairs={{0,4},{4,0},{1,5},{5,1},{2,6},{6,2},{3,7},{7,3},{8,12},{12,8},{9,1... | collective-permute-start | bytes 393224 | tf_op jit(solution)/shard_map/ppermute | solution.py:111
  7.9 22.6 %collective-permute-start.1 = (f32[13,32,128]{2,1,0:T(8,128)S(1)}, f32[13,32,128]{2,1,0:T(8,128)S(1)}, u32[]{:S(2)}, u32[]{:S(2)}) collective-permute-start(f32[13,32,128]{2,1,0:T(8,128)S(1)} %get-tuple-element.23), channel_id=1, source_target_pairs={{0,8},{8,16},{16,24},{1,9},{9,17},{17,25},{2,10},{10,18},{18,26},{... | collective-permute-start | bytes 638984 | tf_op jit(solution)/shard_map/ppermute | solution.py:83
  11.6 1.3 %copy-start.2 = (s32[1,1,8]{2,1,0:T(1,128)S(1)}, s32[1,1,8]{2,1,0:T(1,128)}, u32[]{:S(2)}) copy-start(s32[1,1,8]{2,1,0:T(1,128)} %param.5) | copy-start | bytes 100
  11.6 18.9 %collective-permute-start.2 = (f32[13,32,128]{2,1,0:T(8,128)S(1)}, f32[13,32,128]{2,1,0:T(8,128)S(1)}, u32[]{:S(2)}, u32[]{:S(2)}) collective-permute-start(f32[13,32,128]{2,1,0:T(8,128)S(1)} %get-tuple-element.25), channel_id=1, source_target_pairs={{8,0},{16,8},{24,16},{9,1},{17,9},{25,17},{10,2},{18,10},{26,18},{... | collective-permute-start | bytes 638984 | tf_op jit(solution)/shard_map/ppermute | solution.py:84
  24.6 9.5 %collective-permute-start.5 = (bf16[2,12,32,128]{3,2,1,0:T(8,128)(2,1)S(1)}, bf16[2,12,32,128]{3,2,1,0:T(8,128)(2,1)S(1)}, u32[]{:S(2)}, u32[]{:S(2)}) collective-permute-start(bf16[2,12,32,128]{3,2,1,0:T(8,128)(2,1)S(1)} %get-tuple-element.28), channel_id=1, source_target_pairs={{0,8},{8,16},{16,24},{1,9},{9,17},{17,25},{2,10},{10,18},{18,26},{... | collective-permute-start | bytes 589832 | tf_op jit(solution)/shard_map/ppermute | solution.py:83
  29.2 8.8 %collective-permute-start.6 = (bf16[2,12,32,128]{3,2,1,0:T(8,128)(2,1)S(1)}, bf16[2,12,32,128]{3,2,1,0:T(8,128)(2,1)S(1)}, u32[]{:S(2)}, u32[]{:S(2)}) collective-permute-start(bf16[2,12,32,128]{3,2,1,0:T(8,128)(2,1)S(1)} %get-tuple-element.30), channel_id=1, source_target_pairs={{8,0},{16,8},{24,16},{9,1},{17,9},{25,17},{10,2},{18,10},{26,18},{... | collective-permute-start | bytes 589832 | tf_op jit(solution)/shard_map/ppermute | solution.py:84
  30.8 7.1 %collective-permute-start.3 = (f32[11,32,128]{2,1,0:T(8,128)S(1)}, f32[11,32,128]{2,1,0:T(8,128)S(1)}, u32[]{:S(2)}, u32[]{:S(2)}) collective-permute-start(f32[11,32,128]{2,1,0:T(8,128)S(1)} %get-tuple-element.26), channel_id=1, source_target_pairs={{0,1},{1,2},{2,3},{4,5},{5,6},{6,7},{8,9},{9,10},{10,11},{12,13},{... | collective-permute-start | bytes 540680 | tf_op jit(solution)/shard_map/ppermute | solution.py:83
  32.8 5.1 %collective-permute-start.4 = (f32[11,32,128]{2,1,0:T(8,128)S(1)}, f32[11,32,128]{2,1,0:T(8,128)S(1)}, u32[]{:S(2)}, u32[]{:S(2)}) collective-permute-start(f32[11,32,128]{2,1,0:T(8,128)S(1)} %get-tuple-element.27), channel_id=1, source_target_pairs={{1,0},{2,1},{3,2},{5,4},{6,5},{7,6},{9,8},{10,9},{11,10},{13,12},{... | collective-permute-start | bytes 540680 | tf_op jit(solution)/shard_map/ppermute | solution.py:84
  43.8 16.1 %all-to-all-start = ((f32[32,8,128]{2,1,0:T(8,128)}), f32[32,8,128]{2,1,0:T(8,128)S(1)}, u32[]{:S(2)}, u32[]{:S(2)}) async-start(f32[32,8,128]{2,1,0:T(8,128)} %get-tuple-element.31), calls=%async_computation | async-start | bytes 262144 | tf_op jit(solution)/shard_map/all_to_all | solution.py:723
  51.7 9.2 %collective-permute-start.7 = (f32[2,6,16,128]{3,2,1,0:T(8,128)S(1)}, f32[2,6,16,128]{3,2,1,0:T(8,128)S(1)}, u32[]{:S(2)}, u32[]{:S(2)}) collective-permute-start(f32[2,6,16,128]{3,2,1,0:T(8,128)S(1)} %get-tuple-element.32), channel_id=1, source_target_pairs={{0,8},{8,16},{16,24},{1,9},{9,17},{17,25},{2,10},{10,18},{18,26},{... | collective-permute-start | bytes 294920 | tf_op jit(solution)/shard_map/ppermute | solution.py:83
  55.4 6.5 %collective-permute-start.8 = (f32[2,6,16,128]{3,2,1,0:T(8,128)S(1)}, f32[2,6,16,128]{3,2,1,0:T(8,128)S(1)}, u32[]{:S(2)}, u32[]{:S(2)}) collective-permute-start(f32[2,6,16,128]{3,2,1,0:T(8,128)S(1)} %get-tuple-element.34), channel_id=1, source_target_pairs={{8,0},{16,8},{24,16},{9,1},{17,9},{25,17},{10,2},{18,10},{26,18},{... | collective-permute-start | bytes 294920 | tf_op jit(solution)/shard_map/ppermute | solution.py:84

commit v4 on v3

--- a/solution.py
+++ b/solution.py
@@ -57,7 +57,10 @@
         self.wy = (2 if self.swap else 3) * self.by
         self.cx, self.cy = self.bx // 2, self.by // 2
         self.mx, self.my = self.wx // 2, self.wy // 2
-        self.devices = self.gx * self.gy * self.gz
+        self.low_axes = ("gx", "gz") if self.swap else ("gx", "gy", "gz")
+        self.low_blocks = 1 if self.swap else self.gy
+        self.low_peers = self.gx * self.low_blocks * self.gz
+        self.low_y = (self.my if self.swap else self.cy) // 2
         self.fy = self.by + (8 if self.swap else 16)
 
     def kept_y(self):
@@ -72,17 +75,32 @@
         return rows
 
 
-def neighbours_of(count, step):
-    if step > 0:
-        return [(i, i + 1) for i in range(count - 1)]
-    return [(i + 1, i) for i in range(count - 1)]
+def is_even(axis):
+    return lax.axis_index(axis) % 2 == 0
+
+
+def swaps(axis, count, first, second):
+    def pairs(start):
+        steps = [(i, i + 1) for i in range(start, count - 1, 2)]
+        return steps + [(j, i) for i, j in steps]
+
+    return (
+        lax.ppermute(first, axis, pairs(0)),
+        lax.ppermute(second, axis, pairs(1)),
+    )
 
 
 def from_neighbours(axis, count, low, high):
-    return (
-        lax.ppermute(high, axis, neighbours_of(count, 1)),
-        lax.ppermute(low, axis, neighbours_of(count, -1)),
+    even = is_even(axis)
+    first, second = swaps(
+        axis, count, jnp.where(even, high, low), jnp.where(even, low, high)
     )
+    return jnp.where(even, second, first), jnp.where(even, first, second)
+
+
+def send_starts(axis, rows, sent):
+    even = is_even(axis)
+    return jnp.where(even, rows - sent, 0), jnp.where(even, 0, rows - sent)
 
 
 def pack_coefficient(geo, own):
@@ -107,16 +125,17 @@
     if not geo.swap:
         low, high = from_neighbours("gy", geo.gy, own, own)
         center = jnp.concatenate([low, own, high], axis=1)
-        return center, center[:COEFF_ROWS], center[geo.bx - COEFF_ROWS :]
+        starts = send_starts("gx", geo.bx, COEFF_ROWS)
+        return center, *(lax.dynamic_slice_in_dim(center, i, COEFF_ROWS) for i in starts)
     other = lax.ppermute(own, "gy", [(0, 1), (1, 0)])
 
-    def kernel(own_ref, other_ref, center, low, high):
+    def kernel(own_ref, other_ref, center, *sends):
         mine = geo.own_y(geo.by)
         start = pl.multiple_of(geo.by - mine, 8)
         center[:, pl.ds(mine, geo.by), :] = own_ref[...]
         center[:, pl.ds(start, geo.by), :] = other_ref[...]
-        low[...] = center[0:COEFF_ROWS]
-        high[...] = center[geo.bx - COEFF_ROWS :]
+        for send, at in zip(sends, send_starts("gx", geo.bx, COEFF_ROWS)):
+            send[...] = center[pl.ds(at, COEFF_ROWS)]
 
     slab = shape_f32(COEFF_ROWS, geo.wy, geo.bz)
     return call(kernel, [shape_f32(geo.bx, geo.wy, geo.bz), slab, slab])(own, other)
@@ -128,25 +147,34 @@
     return rows + [(2, i) for i in range(COEFF_ROWS)]
 
 
+def window_row(parts, part, row):
+    center, first, second = parts
+    if part == 1:
+        return center[row]
+    flip = is_even("gx") if part == 0 else jnp.logical_not(is_even("gx"))
+    return jnp.where(flip, second[row], first[row])
+
+
 def pack_ends(geo, parts):
     rows = coefficient_rows(geo)
     lines = -(-len(rows) // 4)
 
-    def kernel(left, center, right, last, first):
-        refs = (left, center, right)
+    def kernel(*refs):
+        given, (sent_first, sent_second) = refs[0:3], refs[3:5]
+        even = is_even("gz")
         group = iota((geo.wy, LANES), 1) % (LANES // 2) // Z_PAIRS
         for line in range(lines):
             ends = jnp.zeros((geo.wy, LANES), F32)
             starts = ends
             for place, (part, row) in enumerate(rows[4 * line : 4 * line + 4]):
-                value = refs[part][row]
+                value = window_row(given, part, row)
                 shift = place * Z_PAIRS
                 down = pltpu.roll(value, LANES - shift, 1) if shift else value
                 up = pltpu.roll(value, shift, 1) if shift else value
                 ends = jnp.where(group == 3 - place, down, ends)
                 starts = jnp.where(group == place, up, starts)
-            last[line] = ends
-            first[line] = starts
+            sent_first[line] = jnp.where(even, ends, starts)
+            sent_second[line] = jnp.where(even, starts, ends)
 
     packed = shape_f32(lines, geo.wy, LANES)
     return call(kernel, [packed, packed])(*parts)
@@ -161,7 +189,7 @@
     per_tile = LANES // BOX
     pair = BOX // 2
 
-    def kernel(slot_ref, center, low, high, *ordered_refs):
+    def kernel(slot_ref, center, send_a, send_b, *ordered_refs):
         place = iota((count, LANES), 1)
         wanted = jnp.where(place < own_boxes + own_boxes // 2, place, place - boxes)
         wanted = (wanted + lax.axis_index("gz") * own_boxes).astype(F32)
@@ -194,8 +222,8 @@
             span = slice(column * by, (column + 1) * by)
             center[0, :, span, :] = jnp.where(first, even, odd).astype(BF16)
             center[1, :, span, :] = jnp.where(first, odd, even).astype(BF16)
-        low[...] = center[:, 0:SOURCE_ROWS]
-        high[...] = center[:, bx - SOURCE_ROWS :]
+        for send, at in zip((send_a, send_b), send_starts("gx", bx, SOURCE_ROWS)):
+            send[...] = center[:, pl.ds(at, SOURCE_ROWS)]
 
     def shape(rows):
         return jax.ShapeDtypeStruct((2, rows, columns * by, LANES), BF16)
@@ -230,7 +258,8 @@
     own = pack_source(geo, column, cells, 1)[0]
     low, high = from_neighbours("gy", geo.gy, own, own)
     center = jnp.concatenate([low, own, high], axis=2)
-    return center, center[:, :SOURCE_ROWS], center[:, geo.bx - SOURCE_ROWS :]
+    starts = send_starts("gx", geo.bx, SOURCE_ROWS)
+    return center, *(lax.dynamic_slice_in_dim(center, i, SOURCE_ROWS, 1) for i in starts)
 
 
 PAD = 8
@@ -336,7 +365,7 @@
 def way_down(geo, coefficient, ends, source):
     bx, wx, wy, mx, my = geo.bx, geo.wx, geo.wy, geo.mx, geo.my
     cx, cy = geo.cx, geo.cy
-    lx, ly = cx // 2, cy // 2
+    lx, ly = cx // 2, geo.low_y
     rows = coefficient_rows(geo)
     top = bx - COEFF_ROWS
     share = geo.bz // 4
@@ -344,8 +373,8 @@
     depth = kept[1] - kept[0]
 
     def kernel(*refs):
-        coeff_in, (before, after), source_in = refs[0:3], refs[3:5], refs[5:8]
-        payload, sent_low, sent_high, center, mid_coeff, mid_weight = refs[8:14]
+        coeff_in, (ends_a, ends_b), source_in = refs[0:3], refs[3:5], refs[5:8]
+        payload, send_a, send_b, center, mid_coeff, mid_weight = refs[8:14]
         out_black, out_coeff, out_weight, out_source = refs[14:18]
         kr, kb, vr, vb, wr, wb, weight_r, weight_b, source_r, source_b = refs[18:28]
         diag, resid, mc, mv, mw, mid_source, mid_diag = refs[28:]
@@ -357,9 +386,12 @@
         lane = iota((wy, LANES), 1)
         is_own, is_after = lane < LANES // 2, lane < LANES // 2 + Z_PAIRS
         is_before = lane >= LANES - Z_PAIRS
+        even_z = is_even("gz")
         for index, (part, row) in enumerate(rows):
             line, shift = index // 4, index % 4 * Z_PAIRS
-            own, prior, later = coeff_in[part][row], before[line], after[line]
+            own = window_row(coeff_in, part, row)
+            prior = jnp.where(even_z, ends_b[line], ends_a[line])
+            later = jnp.where(even_z, ends_a[line], ends_b[line])
             for colour, own_turn, turn in ((0, 0, LANES // 2), (1, LANES // 2, 0)):
                 lanes = pltpu.roll(own, own_turn, 1) if own_turn else own
                 after_turn = (turn - shift) % LANES
@@ -376,9 +408,15 @@
         for colour in (0, 1):
             for row in (*range(top), *range(top + len(rows), wx)):
                 put(coeff[colour], row, edge)
-            sources[colour][bx - SOURCE_ROWS : bx] = source_in[0][colour].astype(F32)
-            sources[colour][bx : 2 * bx] = source_in[1][colour].astype(F32)
-            sources[colour][2 * bx : 2 * bx + SOURCE_ROWS] = source_in[2][colour].astype(F32)
+            even_x = is_even("gx")
+            after_x, before_x = 2 * bx, bx - SOURCE_ROWS
+            first_at = jnp.where(even_x, after_x, before_x)
+            second_at = jnp.where(even_x, before_x, after_x)
+            span = pl.ds(first_at, SOURCE_ROWS)
+            sources[colour][bx : 2 * bx] = source_in[0][colour].astype(F32)
+            sources[colour][span] = source_in[1][colour].astype(F32)
+            span = pl.ds(second_at, SOURCE_ROWS)
+            sources[colour][span] = source_in[2][colour].astype(F32)
 
         span = (bx - SOURCE_ROWS, 2 * bx + SOURCE_ROWS)
         lower = low_rows(wy)
@@ -471,10 +509,10 @@
         for row in range(cx):
             center[0, row] = inner(mv, cx + row)
             center[1, row] = mid_source[cx + row]
-        sent_low[...] = center[:, 0:MID_ROWS]
-        sent_high[...] = center[:, cx - MID_ROWS :]
-
-        start = geo.own_y(cy)
+        for send, at in zip((send_a, send_b), send_starts("gx", cx, MID_ROWS)):
+            send[...] = center[:, pl.ds(at, MID_ROWS)]
+
+        start = 0 if geo.swap else cy
         parts = []
         for cell in range(lx):
             at = cx + 2 * cell
@@ -502,7 +540,7 @@
     return call(
         kernel,
         [
-            shape_f32(geo.devices, 2 * ly, LANES),
+            shape_f32(geo.low_peers, 2 * ly, LANES),
             slab,
             slab,
             shape_f32(2, cx, my, LANES),
@@ -555,8 +593,8 @@
 def lift_bottom(geo, lows):
     bz, mx, my = geo.bz, geo.mx, geo.my
     cx, cy = geo.cx, geo.cy
-    block_x, block_y = cx // 2, cy // 2
-    lx, ly = geo.gx * block_x, geo.gy * block_y
+    block_x, block_y = cx // 2, geo.low_y
+    lx, ly = geo.gx * block_x, geo.low_blocks * block_y
     share = bz // 4
     groups = LANES // share
     columns = geo.gz * share
@@ -564,12 +602,12 @@
     def kernel(low_ref, out_ref, low_full, spread):
         lane = iota((2 * block_y, LANES), 1) // share
         for ix in range(geo.gx):
-            for iy in range(geo.gy):
+            for iy in range(geo.low_blocks):
                 for group in range(block_x):
                     for tile in range(columns // LANES):
                         total = jnp.zeros((2 * block_y, LANES), F32)
                         for part in range(groups):
-                            device = (ix * geo.gy + iy) * geo.gz + tile * groups + part
+                            device = (ix * geo.low_blocks + iy) * geo.gz + tile * groups + part
                             piece = low_ref[device]
                             shift = ((part - group) * share) % LANES
                             if shift:
@@ -616,7 +654,7 @@
     depth = bx + 2 * FINE_ROWS
 
     def kernel(*refs):
-        low_ref, left, center, right, mid_coeff, mid_weight = refs[0:6]
+        low_ref, center, first, second, mid_coeff, mid_weight = refs[0:6]
         fine_black, fine_coeff, fine_weight, fine_source = refs[6:10]
         out_ref = refs[10]
         mc, mv, mw, mid_source, up, source_r, source_b = refs[11:18]
@@ -631,14 +669,17 @@
                 put(mw, row, jnp.zeros((my, LANES), F32))
                 continue
             if row < cx:
-                part, place = left, row - mid_span[0]
+                part, place = 0, row - mid_span[0]
             elif row < 2 * cx:
-                part, place = center, row - cx
+                part, place = 1, row - cx
             else:
-                part, place = right, row - 2 * cx
+                part, place = 2, row - 2 * cx
             mine = mid_coeff[row]
-            fresh = part[0, place] + jnp.where(mine > 0.0, low_ref[row // 2], 0.0)
-            mid_source[row] = part[1, place]
+            values = window_row((center.at[0], first.at[0], second.at[0]), part, place)
+            fresh = values + jnp.where(mine > 0.0, low_ref[row // 2], 0.0)
+            mid_source[row] = window_row(
+                (center.at[1], first.at[1], second.at[1]), part, place
+            )
             put(mv, row, fresh)
             put(mw, row, mine * fresh)
         for rows_off, colour in ((1, 0), (2, 1), (3, 0), (4, 1)):
@@ -696,31 +737,32 @@
     )(lifted_low, *mids, *fines)
 
 
-def middle_neighbours(geo, center, low, high):
+def middle_neighbours(geo, center, first, second):
     if not geo.swap:
         own = center[:, :, geo.cy : 2 * geo.cy]
         before, after = from_neighbours("gy", geo.gy, own, own)
         center = jnp.concatenate([before, own, after], axis=2)
-        low, high = center[:, :MID_ROWS], center[:, geo.cx - MID_ROWS :]
-    left, right = from_neighbours("gx", geo.gx, low, high)
-    return left, center, right
+        starts = send_starts("gx", geo.cx, MID_ROWS)
+        first, second = (
+            lax.dynamic_slice_in_dim(center, i, MID_ROWS, 1) for i in starts
+        )
+    return center, *swaps("gx", geo.gx, first, second)
 
 
 def per_device(geo, old_slots, old_ids, coefficient):
-    center_k, low_k, high_k = widen_coefficient(geo, pack_coefficient(geo, coefficient))
-    left_k, right_k = from_neighbours("gx", geo.gx, low_k, high_k)
-    parts = (left_k, center_k, right_k)
-    last, first = pack_ends(geo, parts)
-    ends = from_neighbours("gz", geo.gz, first, last)
-
-    center_f, low_f, high_f = gather_source(geo, old_slots, old_ids)
-    left_f, right_f = from_neighbours("gx", geo.gx, low_f, high_f)
-
-    payload, low_m, high_m, center_m, mid_coeff, mid_weight, *fines = way_down(
-        geo, parts, ends, (left_f, center_f, right_f)
+    center_k, *sent_k = widen_coefficient(geo, pack_coefficient(geo, coefficient))
+    parts = (center_k, *swaps("gx", geo.gx, *sent_k))
+    sent_z = pack_ends(geo, parts)
+    ends = swaps("gz", geo.gz, *sent_z)
+
+    center_f, *sent_f = gather_source(geo, old_slots, old_ids)
+    source = (center_f, *swaps("gx", geo.gx, *sent_f))
+
+    payload, first_m, second_m, center_m, mid_coeff, mid_weight, *fines = way_down(
+        geo, parts, ends, source
     )
-    around = middle_neighbours(geo, center_m, low_m, high_m)
-    lows = lax.all_to_all(payload, ("gx", "gy", "gz"), 0, 0, tiled=True)
+    around = middle_neighbours(geo, center_m, first_m, second_m)
+    lows = lax.all_to_all(payload, geo.low_axes, 0, 0, tiled=True)
     lifted = lift_bottom(geo, lows)
     return way_up(geo, lifted, (*around, mid_coeff, mid_weight), fines)
 

time: 65 us -> 58.1 us (0.89)
  starting transfers between devices: 30 us -> 21.7 us
  waiting for transfers between devices: 11.6 us -> 13 us
    ppermute x8, starting transfers between devices: 19.1 us -> 11.2 us  [the longest x4 8.4 us: swaps(): lax.ppermute(first, axis, pairs(0))]
    all_to_all x1, waiting for transfers between devices: 3.22 us -> 5.88 us  [per_device(): lows = lax.all_to_all(payload, geo.low_axes, 0, 0, tiled=True)]
    ppermute x8, waiting for transfers between devices: 4.86 us -> 3.59 us  [the longest x4 3.58 us: swaps(): lax.ppermute(first, axis, pairs(0))]
  transfers between devices with their start and end apart: 10 -> 10, of which waited for: 4 -> 3; matrix products, arithmetic and copies ran while one was open for 0% -> 0% of each run, Pallas kernels for 5% -> 5%
where the time goes in v4:
time: 58.1 us; the launch traced here: 57.8 us
  starting transfers between devices  21.7 us (37%)
  waiting for transfers between devices  13 us (22%)
  Pallas kernels  12.1 us (21%)
  blocking collectives  9.91 us (17%)
  local copies, waits for them, and re-layouts  1 us (2%)
    all_gather x1, blocking collectives, gather_source(): column = lax.all_gather(tag_slots(slots, ids), axes, axis=0, tiled=True)  9.91 us
    ppermute x4, starting transfers between devices, swaps(): lax.ppermute(first, axis, pairs(0))  8.4 us
    all_to_all x1, starting transfers between devices, per_device(): lows = lax.all_to_all(payload, geo.low_axes, 0, 0, tiled=True)  7.55 us
    pallas_call x1, Pallas kernels, way_down(): call(kernel, [shape_f32(geo.low_peers, 2 * ly, LANES), slab, slab, shape_...  5.96 us
    all_to_all x1, waiting for transfers between devices, per_device(): lows = lax.all_to_all(payload, geo.low_axes, 0, 0, tiled=True)  5.88 us
    ppermute x4, waiting for transfers between devices, swaps(): lax.ppermute(first, axis, pairs(0))  3.58 us
    ppermute x1, waiting for transfers between devices, widen_coefficient(): other = lax.ppermute(own, 'gy', [(0, 1), (1, 0)])  3.5 us
    ppermute x1, starting transfers between devices, widen_coefficient(): other = lax.ppermute(own, 'gy', [(0, 1), (1, 0)])  3.03 us
  transfers between devices with their start and end apart: 10, of which 3 were waited for; matrix products, arithmetic and copies ran while one was open for 0% of the time, Pallas kernels for 5%

profile of v4, /device:TPU:0, one launch (start us, length us, event | category | flops | bytes accessed | tf_op | source)
XLA Modules:
  0.0 57.8 jit_solution(11067790623418635777)
XLA Ops:
  0.0 0.0 copy-start
  0.0 0.9 %copy-done = f32[16,16,128]{2,1,0:T(8,128)S(1)} copy-done((f32[16,16,128]{2,1,0:T(8,128)S(1)}, f32[16,16,128]{2,1,0:T(8,128)}, u32[]{:S(2)}) %copy-start) | copy-done | bytes 131096
  0.9 0.3 shard_map.37.own_ref
  1.2 0.0 copy-start.1
  1.3 3.0 %collective-permute-start = (f32[16,16,128]{2,1,0:T(8,128)S(1)}, f32[16,16,128]{2,1,0:T(8,128)S(1)}, u32[]{:S(2)}, u32[]{:S(2)}) collective-permute-start(f32[16,16,128]{2,1,0:T(8,128)S(1)} %shard_map.37.own_ref), channel_id=1, source_target_pairs={{0,4},{4,0},{1,5},{5,1},{2,6},{6,2},{3,7},{7,3},{8,12},{12,8},{9,1... | collective-permute-start | bytes 393224 | tf_op jit(solution)/shard_map/ppermute | solution.py:130
  4.3 3.5 %collective-permute-done.other_ref = f32[16,16,128]{2,1,0:T(8,128)S(1)} collective-permute-done((f32[16,16,128]{2,1,0:T(8,128)S(1)}, f32[16,16,128]{2,1,0:T(8,128)S(1)}, u32[]{:S(2)}, u32[]{:S(2)}) %collective-permute-start) | collective-permute-done | bytes 131104 | tf_op jit(solution)/shard_map/ppermute | solution.py:130
  7.8 0.1 shard_map.38
  7.8 1.9 %collective-permute-start.1 = (f32[13,32,128]{2,1,0:T(8,128)S(1)}, f32[13,32,128]{2,1,0:T(8,128)S(1)}, u32[]{:S(2)}, u32[]{:S(2)}) collective-permute-start(f32[13,32,128]{2,1,0:T(8,128)S(1)} %get-tuple-element.24), channel_id=1, source_target_pairs={{0,8},{16,24},{8,0},{24,16},{1,9},{17,25},{9,1},{25,17},{2,10},{18... | collective-permute-start | bytes 638984 | tf_op jit(solution)/shard_map/ppermute | solution.py:88
  9.7 0.0 copy-start.2
  9.7 0.8 %collective-permute-start.2 = (f32[13,32,128]{2,1,0:T(8,128)S(1)}, f32[13,32,128]{2,1,0:T(8,128)S(1)}, u32[]{:S(2)}, u32[]{:S(2)}) collective-permute-start(f32[13,32,128]{2,1,0:T(8,128)S(1)} %get-tuple-element.25), channel_id=1, source_target_pairs={{8,16},{16,8},{9,17},{17,9},{10,18},{18,10},{11,19},{19,11},{12,20... | collective-permute-start | bytes 638984 | tf_op jit(solution)/shard_map/ppermute | solution.py:89
  10.5 0.0 copy-done.2
  10.6 0.1 copy.4.id_ref
  10.6 0.0 copy-done.1
  10.6 0.1 shard_map.40
  10.7 9.9 %all_gather.3.slot_ref = bf16[64,4224]{1,0:T(8,128)(2,1)S(1)} all-gather(bf16[8,4224]{1,0:T(8,128)(2,1)S(1)} %shard_map.40), channel_id=1, replica_groups=mesh['gx'=4,'gy'=2,'gz'=4] {'gy','gz'}, dimensions={0}, use_global_device_ids=true | all-gather | bytes 608256 | tf_op jit(solution)/shard_map/all_gather | solution.py:255
  20.6 1.6 %shard_map.41 = (bf16[2,16,32,128]{3,2,1,0:T(8,128)(2,1)S(1)}, bf16[2,12,32,128]{3,2,1,0:T(8,128)(2,1)S(1)}, bf16[2,12,32,128]{3,2,1,0:T(8,128)(2,1)S(1)}) custom-call(bf16[64,4224]{1,0:T(8,128)(2,1)S(1)} %all_gather.3.slot_ref), custom_call_target="tpu_custom_call" | custom-call | tf_op jit(solution)/shard_map/pallas_call | solution.py:231
  22.3 4.4 %collective-permute-start.5 = (bf16[2,12,32,128]{3,2,1,0:T(8,128)(2,1)S(1)}, bf16[2,12,32,128]{3,2,1,0:T(8,128)(2,1)S(1)}, u32[]{:S(2)}, u32[]{:S(2)}) collective-permute-start(bf16[2,12,32,128]{3,2,1,0:T(8,128)(2,1)S(1)} %get-tuple-element.29), channel_id=1, source_target_pairs={{0,8},{16,24},{8,0},{24,16},{1,9},{17,25},{9,1},{25,17},{2,10},{18... | collective-permute-start | bytes 589832 | tf_op jit(solution)/shard_map/ppermute | solution.py:88
  26.7 0.7 %collective-permute-start.6 = (bf16[2,12,32,128]{3,2,1,0:T(8,128)(2,1)S(1)}, bf16[2,12,32,128]{3,2,1,0:T(8,128)(2,1)S(1)}, u32[]{:S(2)}, u32[]{:S(2)}) collective-permute-start(bf16[2,12,32,128]{3,2,1,0:T(8,128)(2,1)S(1)} %get-tuple-element.30), channel_id=1, source_target_pairs={{8,16},{16,8},{9,17},{17,9},{10,18},{18,10},{11,19},{19,11},{12,20... | collective-permute-start | bytes 589832 | tf_op jit(solution)/shard_map/ppermute | solution.py:89
  27.4 0.0 collective-permute-done.1.refs_1_
  27.4 0.0 collective-permute-done.2.refs_2_
  27.4 0.3 shard_map.39
  27.7 0.1 collective-permute-start.3
  27.9 0.7 %collective-permute-start.4 = (f32[11,32,128]{2,1,0:T(8,128)S(1)}, f32[11,32,128]{2,1,0:T(8,128)S(1)}, u32[]{:S(2)}, u32[]{:S(2)}) collective-permute-start(f32[11,32,128]{2,1,0:T(8,128)S(1)} %get-tuple-element.27), channel_id=1, source_target_pairs={{1,2},{2,1},{5,6},{6,5},{9,10},{10,9},{13,14},{14,13},{17,18},{18,... | collective-permute-start | bytes 540680 | tf_op jit(solution)/shard_map/ppermute | solution.py:89
  28.5 3.6 %collective-permute-done.5.refs_6_ = bf16[2,12,32,128]{3,2,1,0:T(8,128)(2,1)S(1)} collective-permute-done((bf16[2,12,32,128]{3,2,1,0:T(8,128)(2,1)S(1)}, bf16[2,12,32,128]{3,2,1,0:T(8,128)(2,1)S(1)}, u32[]{:S(2)}, u32[]{:S(2)}) %collective-permute-start.5) | collective-permute-done | bytes 196640 | tf_op jit(solution)/shard_map/ppermute | solution.py:88
  32.1 0.0 collective-permute-done.6.refs_7_
  32.1 0.0 collective-permute-done.3.refs_3_
  32.1 0.0 collective-permute-done.4.refs_4_
  32.1 6.0 %shard_map.42 = (f32[16,16,128]{2,1,0:T(8,128)}, f32[2,6,16,128]{3,2,1,0:T(8,128)S(1)}, f32[2,6,16,128]{3,2,1,0:T(8,128)S(1)}, f32[2,8,16,128]{3,2,1,0:T(8,128)S...) custom-call(f32[16,32,128]{2,1,0:T(8,128)S(1)} %get-tuple-element.23, ...), custom_call_target="tpu_custom_call" | custom-call | tf_op jit(solution)/shard_map/pallas_call | solution.py:540
  38.1 7.6 %all-to-all-start = ((f32[16,16,128]{2,1,0:T(8,128)}), f32[16,16,128]{2,1,0:T(8,128)S(1)}, u32[]{:S(2)}, u32[]{:S(2)}) async-start(f32[16,16,128]{2,1,0:T(8,128)} %get-tuple-element.31), calls=%async_computation | async-start | bytes 262144 | tf_op jit(solution)/shard_map/all_to_all | solution.py:765
  45.6 1.9 %collective-permute-start.7 = (f32[2,6,16,128]{3,2,1,0:T(8,128)S(1)}, f32[2,6,16,128]{3,2,1,0:T(8,128)S(1)}, u32[]{:S(2)}, u32[]{:S(2)}) collective-permute-start(f32[2,6,16,128]{3,2,1,0:T(8,128)S(1)} %get-tuple-element.33), channel_id=1, source_target_pairs={{0,8},{16,24},{8,0},{24,16},{1,9},{17,25},{9,1},{25,17},{2,10},{18... | collective-permute-start | bytes 294920 | tf_op jit(solution)/shard_map/ppermute | solution.py:88
  47.6 0.7 %collective-permute-start.8 = (f32[2,6,16,128]{3,2,1,0:T(8,128)S(1)}, f32[2,6,16,128]{3,2,1,0:T(8,128)S(1)}, u32[]{:S(2)}, u32[]{:S(2)}) collective-permute-start(f32[2,6,16,128]{3,2,1,0:T(8,128)S(1)} %get-tuple-element.34), channel_id=1, source_target_pairs={{8,16},{16,8},{9,17},{17,9},{10,18},{18,10},{11,19},{19,11},{12,20... | collective-permute-start | bytes 294920 | tf_op jit(solution)/shard_map/ppermute | solution.py:89
  48.2 5.9 %all-to-all-done.low_ref = f32[16,16,128]{2,1,0:T(8,128)S(1)} async-done(((f32[16,16,128]{2,1,0:T(8,128)}), f32[16,16,128]{2,1,0:T(8,128)S(1)}, u32[]{:S(2)}, u32[]{:S(2)}) %all-to-all-start) | async-done | bytes 131104 | tf_op jit(solution)/shard_map/all_to_all | solution.py:765
  54.1 0.9 %shard_map.43.refs_0_ = f32[12,16,128]{2,1,0:T(8,128)S(1)} custom-call(f32[16,16,128]{2,1,0:T(8,128)S(1)} %all-to-all-done.low_ref), custom_call_target="tpu_custom_call" | custom-call | tf_op jit(solution)/shard_map/pallas_call | solution.py:640
  55.1 0.0 collective-permute-done.7.refs_2_
  55.1 0.0 collective-permute-done.8.refs_3_
  55.1 2.8 %shard_map.44 = f32[16,16,128]{2,1,0:T(8,128)} custom-call(f32[12,16,128]{2,1,0:T(8,128)S(1)} %shard_map.43.refs_0_, f32[2,8,16,128]{3,2,1,0:T(8,128)S(1)} %get-tuple-element.32.refs_1_, f32[2,6,16,128]{3,2,1,0:T(8,128)S(1)} %collective-permute-done.7.refs_2_, f32[2,6,16,128]{3,2,1,0:T(8,128)S(1)} %collective-permute-done.8.refs_3_, ...), custom_call_target="tpu_custom_call" | custom-call | tf_op jit(solution)/shard_map/pallas_call | solution.py:724
Async XLA Ops:
  0.0 0.9 %copy-start = (f32[16,16,128]{2,1,0:T(8,128)S(1)}, f32[16,16,128]{2,1,0:T(8,128)}, u32[]{:S(2)}) copy-start(f32[16,16,128]{2,1,0:T(8,128)} %own_ref.1) | copy-start | bytes 393220
  1.2 9.4 %copy-start.1 = (bf16[1,1,8,4096]{3,2,1,0:T(8,128)(2,1)S(1)}, bf16[1,1,8,4096]{3,2,1,0:T(8,128)(2,1)}, u32[]{:S(2)}) copy-start(bf16[1,1,8,4096]{3,2,1,0:T(8,128)(2,1)} %param.4) | copy-start | bytes 196612
  1.3 6.5 %collective-permute-start = (f32[16,16,128]{2,1,0:T(8,128)S(1)}, f32[16,16,128]{2,1,0:T(8,128)S(1)}, u32[]{:S(2)}, u32[]{:S(2)}) collective-permute-start(f32[16,16,128]{2,1,0:T(8,128)S(1)} %shard_map.37.own_ref), channel_id=1, source_target_pairs={{0,4},{4,0},{1,5},{5,1},{2,6},{6,2},{3,7},{7,3},{8,12},{12,8},{9,1... | collective-permute-start | bytes 393224 | tf_op jit(solution)/shard_map/ppermute | solution.py:130
  7.8 19.5 %collective-permute-start.1 = (f32[13,32,128]{2,1,0:T(8,128)S(1)}, f32[13,32,128]{2,1,0:T(8,128)S(1)}, u32[]{:S(2)}, u32[]{:S(2)}) collective-permute-start(f32[13,32,128]{2,1,0:T(8,128)S(1)} %get-tuple-element.24), channel_id=1, source_target_pairs={{0,8},{16,24},{8,0},{24,16},{1,9},{17,25},{9,1},{25,17},{2,10},{18... | collective-permute-start | bytes 638984 | tf_op jit(solution)/shard_map/ppermute | solution.py:88
  9.7 0.8 %copy-start.2 = (s32[1,1,8]{2,1,0:T(1,128)S(1)}, s32[1,1,8]{2,1,0:T(1,128)}, u32[]{:S(2)}) copy-start(s32[1,1,8]{2,1,0:T(1,128)} %param.5) | copy-start | bytes 100
  9.7 17.6 %collective-permute-start.2 = (f32[13,32,128]{2,1,0:T(8,128)S(1)}, f32[13,32,128]{2,1,0:T(8,128)S(1)}, u32[]{:S(2)}, u32[]{:S(2)}) collective-permute-start(f32[13,32,128]{2,1,0:T(8,128)S(1)} %get-tuple-element.25), channel_id=1, source_target_pairs={{8,16},{16,8},{9,17},{17,9},{10,18},{18,10},{11,19},{19,11},{12,20... | collective-permute-start | bytes 638984 | tf_op jit(solution)/shard_map/ppermute | solution.py:89
  22.3 9.9 %collective-permute-start.5 = (bf16[2,12,32,128]{3,2,1,0:T(8,128)(2,1)S(1)}, bf16[2,12,32,128]{3,2,1,0:T(8,128)(2,1)S(1)}, u32[]{:S(2)}, u32[]{:S(2)}) collective-permute-start(bf16[2,12,32,128]{3,2,1,0:T(8,128)(2,1)S(1)} %get-tuple-element.29), channel_id=1, source_target_pairs={{0,8},{16,24},{8,0},{24,16},{1,9},{17,25},{9,1},{25,17},{2,10},{18... | collective-permute-start | bytes 589832 | tf_op jit(solution)/shard_map/ppermute | solution.py:88
  26.7 5.4 %collective-permute-start.6 = (bf16[2,12,32,128]{3,2,1,0:T(8,128)(2,1)S(1)}, bf16[2,12,32,128]{3,2,1,0:T(8,128)(2,1)S(1)}, u32[]{:S(2)}, u32[]{:S(2)}) collective-permute-start(bf16[2,12,32,128]{3,2,1,0:T(8,128)(2,1)S(1)} %get-tuple-element.30), channel_id=1, source_target_pairs={{8,16},{16,8},{9,17},{17,9},{10,18},{18,10},{11,19},{19,11},{12,20... | collective-permute-start | bytes 589832 | tf_op jit(solution)/shard_map/ppermute | solution.py:89
  27.7 4.4 %collective-permute-start.3 = (f32[11,32,128]{2,1,0:T(8,128)S(1)}, f32[11,32,128]{2,1,0:T(8,128)S(1)}, u32[]{:S(2)}, u32[]{:S(2)}) collective-permute-start(f32[11,32,128]{2,1,0:T(8,128)S(1)} %get-tuple-element.26), channel_id=1, source_target_pairs={{0,1},{2,3},{1,0},{3,2},{4,5},{6,7},{5,4},{7,6},{8,9},{10,11},{9,8... | collective-permute-start | bytes 540680 | tf_op jit(solution)/shard_map/ppermute | solution.py:88
  27.9 4.3 %collective-permute-start.4 = (f32[11,32,128]{2,1,0:T(8,128)S(1)}, f32[11,32,128]{2,1,0:T(8,128)S(1)}, u32[]{:S(2)}, u32[]{:S(2)}) collective-permute-start(f32[11,32,128]{2,1,0:T(8,128)S(1)} %get-tuple-element.27), channel_id=1, source_target_pairs={{1,2},{2,1},{5,6},{6,5},{9,10},{10,9},{13,14},{14,13},{17,18},{18,... | collective-permute-start | bytes 540680 | tf_op jit(solution)/shard_map/ppermute | solution.py:89
  38.1 16.0 %all-to-all-start = ((f32[16,16,128]{2,1,0:T(8,128)}), f32[16,16,128]{2,1,0:T(8,128)S(1)}, u32[]{:S(2)}, u32[]{:S(2)}) async-start(f32[16,16,128]{2,1,0:T(8,128)} %get-tuple-element.31), calls=%async_computation | async-start | bytes 262144 | tf_op jit(solution)/shard_map/all_to_all | solution.py:765
  45.6 9.4 %collective-permute-start.7 = (f32[2,6,16,128]{3,2,1,0:T(8,128)S(1)}, f32[2,6,16,128]{3,2,1,0:T(8,128)S(1)}, u32[]{:S(2)}, u32[]{:S(2)}) collective-permute-start(f32[2,6,16,128]{3,2,1,0:T(8,128)S(1)} %get-tuple-element.33), channel_id=1, source_target_pairs={{0,8},{16,24},{8,0},{24,16},{1,9},{17,25},{9,1},{25,17},{2,10},{18... | collective-permute-start | bytes 294920 | tf_op jit(solution)/shard_map/ppermute | solution.py:88
  47.6 7.5 %collective-permute-start.8 = (f32[2,6,16,128]{3,2,1,0:T(8,128)S(1)}, f32[2,6,16,128]{3,2,1,0:T(8,128)S(1)}, u32[]{:S(2)}, u32[]{:S(2)}) collective-permute-start(f32[2,6,16,128]{3,2,1,0:T(8,128)S(1)} %get-tuple-element.34), channel_id=1, source_target_pairs={{8,16},{16,8},{9,17},{17,9},{10,18},{18,10},{11,19},{19,11},{12,20... | collective-permute-start | bytes 294920 | tf_op jit(solution)/shard_map/ppermute | solution.py:89

commit v5 on v4

--- a/solution.py
+++ b/solution.py
@@ -16,6 +16,31 @@
 HIGH = lax.Precision.HIGHEST
 F32 = jnp.float32
 BF16 = jnp.bfloat16
+I16 = jnp.int16
+
+ROOT_LOW, ROOT_HIGH = 0.2**0.5, 5.0**0.5
+ROOT_MID = 0.5 * (ROOT_LOW + ROOT_HIGH)
+ROOT_STEP = 0.5 * (ROOT_HIGH - ROOT_LOW) / 32767.0
+
+
+def encode(values):
+    code = jnp.floor((jnp.sqrt(values) - ROOT_MID) * (1.0 / ROOT_STEP) + 0.5)
+    code = jnp.clip(code, -32767.0, 32767.0)
+    return jnp.where(code == 0.0, 1.0, code)
+
+
+def to_i16(code):
+    return code.astype(jnp.int32).astype(I16)
+
+
+def from_i16(code):
+    return code.astype(jnp.int32).astype(F32)
+
+
+def decode(code):
+    code = from_i16(code)
+    root = ROOT_MID + ROOT_STEP * code
+    return jnp.where(code == 0.0, 0.0, root * root)
 
 
 def iota(shape, dim):
@@ -107,18 +132,19 @@
     bx, by, bz = geo.bx, geo.by, geo.bz
     half = bz // 2
 
-    def kernel(own_ref, out_ref):
+    def kernel(own_ref, out_ref, coded_ref):
         source = iota((bz, bz), 0)
         target = iota((bz, bz), 1)
         wanted = jnp.where(target < half, 2 * target, 2 * (target - half) + 1)
         split = exact_dot(own_ref[...].reshape(bx * by, bz), (source == wanted).astype(F32))
         turned = pltpu.roll(split, half, 1)
         first = even_rows((bx, by, bz), (0, 1))
-        out_ref[...] = jnp.where(
-            first, split.reshape(bx, by, bz), turned.reshape(bx, by, bz)
-        )
-
-    return call(kernel, shape_f32(bx, by, bz))(own)
+        packed = jnp.where(first, split.reshape(bx, by, bz), turned.reshape(bx, by, bz))
+        out_ref[...] = packed
+        coded_ref[...] = to_i16(encode(packed))
+
+    coded = jax.ShapeDtypeStruct((bx, by, bz), I16)
+    return call(kernel, [shape_f32(bx, by, bz), coded])(own)
 
 
 def widen_coefficient(geo, own):
@@ -137,8 +163,9 @@
         for send, at in zip(sends, send_starts("gx", geo.bx, COEFF_ROWS)):
             send[...] = center[pl.ds(at, COEFF_ROWS)]
 
-    slab = shape_f32(COEFF_ROWS, geo.wy, geo.bz)
-    return call(kernel, [shape_f32(geo.bx, geo.wy, geo.bz), slab, slab])(own, other)
+    slab = jax.ShapeDtypeStruct((COEFF_ROWS, geo.wy, geo.bz), I16)
+    whole = jax.ShapeDtypeStruct((geo.bx, geo.wy, geo.bz), I16)
+    return call(kernel, [whole, slab, slab])(own, other)
 
 
 def coefficient_rows(geo):
@@ -147,12 +174,12 @@
     return rows + [(2, i) for i in range(COEFF_ROWS)]
 
 
-def window_row(parts, part, row):
+def window_row(parts, part, row, read=lambda value: value):
     center, first, second = parts
     if part == 1:
-        return center[row]
+        return read(center[row])
     flip = is_even("gx") if part == 0 else jnp.logical_not(is_even("gx"))
-    return jnp.where(flip, second[row], first[row])
+    return jnp.where(flip, read(second[row]), read(first[row]))
 
 
 def pack_ends(geo, parts):
@@ -162,21 +189,23 @@
     def kernel(*refs):
         given, (sent_first, sent_second) = refs[0:3], refs[3:5]
         even = is_even("gz")
-        group = iota((geo.wy, LANES), 1) % (LANES // 2) // Z_PAIRS
+        lane = iota((geo.wy, LANES), 1)
+        half = LANES // 2
+        group = lane % half // Z_PAIRS
         for line in range(lines):
             ends = jnp.zeros((geo.wy, LANES), F32)
             starts = ends
             for place, (part, row) in enumerate(rows[4 * line : 4 * line + 4]):
-                value = window_row(given, part, row)
+                value = window_row(given, part, row, from_i16)
                 shift = place * Z_PAIRS
-                down = pltpu.roll(value, LANES - shift, 1) if shift else value
-                up = pltpu.roll(value, shift, 1) if shift else value
-                ends = jnp.where(group == 3 - place, down, ends)
-                starts = jnp.where(group == place, up, starts)
-            sent_first[line] = jnp.where(even, ends, starts)
-            sent_second[line] = jnp.where(even, starts, ends)
-
-    packed = shape_f32(lines, geo.wy, LANES)
+                moved = pltpu.roll(value, shift, 1) if shift else value
+                last = (half - Z_PAIRS + shift) % half // Z_PAIRS
+                ends = jnp.where(group == last, moved, ends)
+                starts = jnp.where(group == place, moved, starts)
+            sent_first[line] = to_i16(jnp.where(even, ends, starts))
+            sent_second[line] = to_i16(jnp.where(even, starts, ends))
+
+    packed = jax.ShapeDtypeStruct((lines, geo.wy, LANES), I16)
     return call(kernel, [packed, packed])(*parts)
 
 
@@ -195,9 +224,10 @@
         wanted = (wanted + lax.axis_index("gz") * own_boxes).astype(F32)
         rows = tiles * per_tile
         keep = iota((tiles, per_tile, LANES), 2) // BOX == iota((tiles, per_tile, LANES), 1)
-        inside = iota((LANES, 2 * LANES), 0) % BOX
-        target = iota((LANES, 2 * LANES), 1)
-        slot_of = jnp.where(inside % 2 == 0, inside // 2, inside // 2 + LANES)
+        inside = iota((2 * LANES, 2 * LANES), 0)
+        target = iota((2 * LANES, 2 * LANES), 1)
+        slot_of = inside // LANES * pair + inside % BOX // 2
+        slot_of = slot_of + inside % 2 * LANES
         first = even_rows((bx, by, LANES), (0, 1))
         for column, ordered in enumerate(ordered_refs):
             here = slice(column * count, (column + 1) * count)
@@ -211,10 +241,14 @@
                     preferred_element_type=F32,
                 )
             total = jnp.zeros((rows, 2 * LANES), F32)
-            for box in range(boxes):
-                line = ordered[:, box : box + 1, :]
-                line = jnp.broadcast_to(line, (tiles, per_tile, LANES))
-                line = jnp.where(keep, line, 0.0).reshape(rows, LANES).astype(BF16)
+            for box in range(0, boxes, 2):
+                lines = []
+                for which in (box, box + 1):
+                    line = ordered[:, which : which + 1, :]
+                    line = jnp.broadcast_to(line, (tiles, per_tile, LANES))
+                    line = jnp.where(keep, line, 0.0).reshape(rows, LANES)
+                    lines.append(line.astype(BF16))
+                line = jnp.concatenate(lines, axis=1)
                 spread = (target == slot_of + box * pair).astype(F32).astype(BF16)
                 total = total + jnp.dot(line, spread, preferred_element_type=F32)
             even = total[:, 0:LANES].reshape(bx, by, LANES)
@@ -293,32 +327,37 @@
     return total + ref[row + 1, PAD + 1 : PAD + 1 + width, :]
 
 
-def fine_sum(ref, row, near_low):
-    here = inner(ref, row)
-    low = pltpu.roll(here, 1, 1)
-    high = pltpu.roll(here, LANES - 1, 1)
-    return across(ref, row) + here + jnp.where(near_low, low, high)
-
-
-def mid_sum(ref, row):
-    here = inner(ref, row)
-    return across(ref, row) + pltpu.roll(here, 1, 1) + pltpu.roll(here, LANES - 1, 1)
+def around(ref, row):
+    return across(ref, row) + inner(ref, row)
+
+
+def beside(first, second, colour):
+    even = iota(first.shape, 0) % 2 == 0
+    if colour == 1:
+        even = jnp.logical_not(even)
+    low = pltpu.roll(jnp.where(even, first, second), 1, 1)
+    high = pltpu.roll(jnp.where(even, second, first), LANES - 1, 1)
+    return jnp.where(even, low, high), jnp.where(even, high, low)
+
+
+def over_pairs(span, body):
+    first, last = span
+
+    def step(index, carry):
+        body(first + 2 * index)
+        return carry
+
+    lax.fori_loop(0, (last - first) // 2, step, 0, unroll=(last - first) // 2)
 
 
 def over_rows(span, mask, body):
-    first, last = span
     flipped = jnp.logical_not(mask)
 
-    def step(index, carry):
-        body(first + 2 * index, mask)
-        body(first + 2 * index + 1, flipped)
-        return carry
-
-    lax.fori_loop(0, (last - first) // 2, step, 0, unroll=(last - first) // 2)
-
-
-def low_rows(width):
-    return iota((width, LANES), 0) % 2 == 0
+    def both(row):
+        body(row, mask)
+        body(row + 1, flipped)
+
+    over_pairs(span, both)
 
 
 def red_lanes(width):
@@ -329,30 +368,46 @@
     return jnp.where(coeff_row > 0.0, 1.0 / total, 0.0)
 
 
-def fine_half(span, colour, coeff, weight, source, values, scaled):
+def fine_sums(row, colour, coeff, side, values, scaled):
     other = 1 - colour
-
-    def body(row, low):
-        near_low = low if colour == 0 else jnp.logical_not(low)
-        mine = inner(coeff[colour], row)
-        summed = mine * fine_sum(values[other], row, near_low)
-        summed = summed + fine_sum(scaled[other], row, near_low)
-        fresh = weight[colour][row] * (source[colour][row] + summed)
-        put(values[colour], row, fresh)
-        put(scaled[colour], row, mine * fresh)
-
-    over_rows(span, low_rows(coeff[0].shape[1] - 2 * PAD), body)
-
-
-def mid_half(span, colour, coeff, weight, source, values, scaled):
+    sixth = beside(inner(values[other], row), inner(values[other], row + 1), colour)
+    sums = []
+    for at, value in zip((row, row + 1), sixth):
+        total = inner(coeff[colour], at) * around(values[other], at)
+        sums.append(total + around(scaled[other], at) + side[colour][at] * value)
+    return sums
+
+
+def fine_half(span, colour, coeff, side, weight, source, values, scaled):
+    def body(row):
+        sums = fine_sums(row, colour, coeff, side, values, scaled)
+        for at, summed in zip((row, row + 1), sums):
+            fresh = weight[colour][at] * (source[colour][at] + summed)
+            put(values[colour], at, fresh)
+            put(scaled[colour], at, inner(coeff[colour], at) * fresh)
+
+    over_pairs(span, body)
+
+
+def mid_sides(ref, row):
+    here = inner(ref, row)
+    return pltpu.roll(here, 1, 1), pltpu.roll(here, LANES - 1, 1)
+
+
+def mid_sums(row, coeff, side, values, scaled):
+    below, above = mid_sides(values, row)
+    total = inner(coeff, row) * across(values, row) + across(scaled, row)
+    return total + side[0][row] * below + side[1][row] * above
+
+
+def mid_half(span, colour, coeff, side, weight, source, values, scaled):
     def body(row, red):
         chosen = red if colour == 0 else jnp.logical_not(red)
-        mine = inner(coeff, row)
-        summed = mine * mid_sum(values, row) + mid_sum(scaled, row)
+        summed = mid_sums(row, coeff, side, values, scaled)
         fresh = weight[row] * (source[row] + summed)
         fresh = jnp.where(chosen, fresh, inner(values, row))
         put(values, row, fresh)
-        put(scaled, row, mine * fresh)
+        put(scaled, row, inner(coeff, row) * fresh)
 
     over_rows(span, red_lanes(coeff.shape[1] - 2 * PAD), body)
 
@@ -362,7 +417,7 @@
     return first - first % 2, last + last % 2
 
 
-def way_down(geo, coefficient, ends, source):
+def way_down(geo, own_coefficient, coefficient, ends, source):
     bx, wx, wy, mx, my = geo.bx, geo.wx, geo.wy, geo.mx, geo.my
     cx, cy = geo.cx, geo.cy
     lx, ly = cx // 2, geo.low_y
@@ -373,37 +428,42 @@
     depth = kept[1] - kept[0]
 
     def kernel(*refs):
+        own_exact, refs = refs[0], refs[1:]
         coeff_in, (ends_a, ends_b), source_in = refs[0:3], refs[3:5], refs[5:8]
         payload, send_a, send_b, center, mid_coeff, mid_weight = refs[8:14]
         out_black, out_coeff, out_weight, out_source = refs[14:18]
         kr, kb, vr, vb, wr, wb, weight_r, weight_b, source_r, source_b = refs[18:28]
-        diag, resid, mc, mv, mw, mid_source, mid_diag = refs[28:]
+        diag, resid, side_r, side_b, mc, mv, mw = refs[28:35]
+        mid_source, mid_diag, mid_below, mid_above, center_exact = refs[35:]
+        side, mid_side = (side_r, side_b), (mid_below, mid_above)
         coeff, values, scaled = (kr, kb), (vr, vb), (wr, wb)
         weight, sources = (weight_r, weight_b), (source_r, source_b)
         for ref in (kr, kb, vr, vb, wr, wb, mc, mv, mw):
             clear_pads(ref)
 
         lane = iota((wy, LANES), 1)
-        is_own, is_after = lane < LANES // 2, lane < LANES // 2 + Z_PAIRS
-        is_before = lane >= LANES - Z_PAIRS
+        half = LANES // 2
+        is_own = lane < half
+        is_near = (lane % half < Z_PAIRS) | (lane % half >= half - Z_PAIRS)
         even_z = is_even("gz")
+        for row in range(bx):
+            center_exact[row] = decode(coeff_in[0][row])
+        center_exact[:, pl.ds(geo.own_y(geo.by), geo.by), :] = own_exact[...]
         for index, (part, row) in enumerate(rows):
-            line, shift = index // 4, index % 4 * Z_PAIRS
-            own = window_row(coeff_in, part, row)
-            prior = jnp.where(even_z, ends_b[line], ends_a[line])
-            later = jnp.where(even_z, ends_a[line], ends_b[line])
-            for colour, own_turn, turn in ((0, 0, LANES // 2), (1, LANES // 2, 0)):
-                lanes = pltpu.roll(own, own_turn, 1) if own_turn else own
-                after_turn = (turn - shift) % LANES
-                before_turn = (turn + shift) % LANES
-                near = pltpu.roll(later, after_turn, 1) if after_turn else later
-                past = pltpu.roll(prior, before_turn, 1) if before_turn else prior
-                lanes = jnp.where(
-                    is_own,
-                    lanes,
-                    jnp.where(is_after, near, jnp.where(is_before, past, 0.0)),
-                )
-                put(coeff[colour], top + index, 0.5 * lanes)
+            line, place = divmod(index, 4)
+            if part == 1:
+                own = center_exact[row]
+            else:
+                own = window_row(coeff_in, part, row, decode)
+            one, two = decode(ends_a[line]), decode(ends_b[line])
+            from_after = (lane % half // Z_PAIRS == place) == even_z
+            near = jnp.where(from_after, one, two)
+            if place:
+                near = pltpu.roll(near, LANES - place * Z_PAIRS, 1)
+            near = jnp.where(is_near, near, 0.0)
+            turned = pltpu.roll(jnp.where(is_own, near, own), half, 1)
+            put(kr, top + index, 0.5 * jnp.where(is_own, own, turned))
+            put(kb, top + index, 0.5 * jnp.where(is_own, turned, near))
         edge = jnp.zeros((wy, LANES), F32)
         for colour in (0, 1):
             for row in (*range(top), *range(top + len(rows), wx)):
@@ -419,36 +479,44 @@
             sources[colour][span] = source_in[2][colour].astype(F32)
 
         span = (bx - SOURCE_ROWS, 2 * bx + SOURCE_ROWS)
-        lower = low_rows(wy)
-
-        def first_red(row, low):
-            mine = inner(kr, row)
-            total = 6.0 * mine + fine_sum(kb, row, low)
-            inverse = weights(mine, total)
-            diag[row] = total
-            weight_r[row] = inverse
-            fresh = inverse * source_r[row]
-            put(vr, row, fresh)
-            put(wr, row, mine * fresh)
-
-        over_rows(span, lower, first_red)
-
-        def black_weight(row, low):
-            mine = inner(kb, row)
-            total = 6.0 * mine + fine_sum(kr, row, jnp.logical_not(low))
-            weight_b[row] = weights(mine, total)
-
-        over_rows(shrink(span, 1), lower, black_weight)
-        fine_half(shrink(span, 1), 1, coeff, weight, sources, values, scaled)
-        fine_half(shrink(span, 2), 0, coeff, weight, sources, values, scaled)
-        fine_half(shrink(span, 3), 1, coeff, weight, sources, values, scaled)
-
-        def residual(row, low):
-            mine = inner(kr, row)
-            summed = mine * fine_sum(vb, row, low) + fine_sum(wb, row, low)
-            resid[row] = source_r[row] + summed - diag[row] * inner(vr, row)
-
-        over_rows(shrink(span, 4), lower, residual)
+
+        def first_red(row):
+            sixth = beside(inner(kb, row), inner(kb, row + 1), 0)
+            for at, value in zip((row, row + 1), sixth):
+                mine = inner(kr, at)
+                total = 6.0 * mine + around(kb, at) + value
+                inverse = weights(mine, total)
+                side_r[at] = mine + value
+                diag[at] = total
+                weight_r[at] = inverse
+                fresh = inverse * source_r[at]
+                put(vr, at, fresh)
+                put(wr, at, mine * fresh)
+
+        over_pairs(span, first_red)
+
+        def first_black(row):
+            sixth = beside(inner(kr, row), inner(kr, row + 1), 1)
+            for at, value in zip((row, row + 1), sixth):
+                mine = inner(kb, at)
+                side_b[at] = mine + value
+                weight_b[at] = weights(mine, 6.0 * mine + around(kr, at) + value)
+            sums = fine_sums(row, 1, coeff, side, values, scaled)
+            for at, summed in zip((row, row + 1), sums):
+                fresh = weight_b[at] * (source_b[at] + summed)
+                put(vb, at, fresh)
+                put(wb, at, inner(kb, at) * fresh)
+
+        over_pairs(shrink(span, 1), first_black)
+        fine_half(shrink(span, 2), 0, coeff, side, weight, sources, values, scaled)
+        fine_half(shrink(span, 3), 1, coeff, side, weight, sources, values, scaled)
+
+        def residual(row):
+            sums = fine_sums(row, 0, coeff, side, values, scaled)
+            for at, summed in zip((row, row + 1), sums):
+                resid[at] = source_r[at] + summed - diag[at] * inner(vr, at)
+
+        over_pairs(shrink(span, 4), residual)
         kept_at = geo.kept_y()[0]
         strip = pl.ds(kept_at, geo.fy)
         inner_strip = pl.ds(pl.multiple_of(kept_at + PAD, 8), geo.fy)
@@ -482,7 +550,10 @@
 
         def mid_red(row, red):
             mine = inner(mc, row)
-            total = 6.0 * mine + mid_sum(mc, row)
+            below, above = mid_sides(mc, row)
+            mid_below[row] = mine + below
+            mid_above[row] = mine + above
+            total = 6.0 * mine + across(mc, row) + below + above
             inverse = weights(mine, total)
             mid_diag[row] = total
             mid_weight[row] = inverse
@@ -492,14 +563,12 @@
 
         over_rows(mid_span, red_lanes(my), mid_red)
         for rows_off, colour in ((1, 1), (2, 0), (3, 1)):
-            mid_half(
-                shrink(mid_sourced, rows_off), colour, mc, mid_weight, mid_source, mv, mw
-            )
+            part = shrink(mid_sourced, rows_off)
+            mid_half(part, colour, mc, mid_side, mid_weight, mid_source, mv, mw)
         own = (cx, 2 * cx)
 
         def mid_residual(row, red):
-            mine = inner(mc, row)
-            summed = mine * mid_sum(mv, row) + mid_sum(mw, row)
+            summed = mid_sums(row, mc, mid_side, mv, mw)
             left = mid_source[row] + summed - mid_diag[row] * inner(mv, row)
             mid_diag[row] = jnp.where(red, 0.25 * left, 0.0)
 
@@ -551,9 +620,10 @@
             both,
             source_kept,
         ],
-        [padded(wx, wy)] * 6 + [plain] * 6 + [padded(mx, my)] * 3 + [small] * 2,
+        [padded(wx, wy)] * 6 + [plain] * 8 + [padded(mx, my)] * 3 + [small] * 4
+        + [pltpu.VMEM((bx, wy, LANES), F32)],
         room=20 if geo.swap else 40,
-    )(*coefficient, *ends, *source)
+    )(own_coefficient, *coefficient, *ends, *source)
 
 
 def low_shift(values, dim, step):
@@ -657,8 +727,10 @@
         low_ref, center, first, second, mid_coeff, mid_weight = refs[0:6]
         fine_black, fine_coeff, fine_weight, fine_source = refs[6:10]
         out_ref = refs[10]
-        mc, mv, mw, mid_source, up, source_r, source_b = refs[11:18]
-        kr, kb, vr, vb, wr, wb = refs[18:]
+        mc, mv, mw, mid_source, mid_below, mid_above, up = refs[11:18]
+        source_r, source_b, side_r, side_b = refs[18:22]
+        kr, kb, vr, vb, wr, wb = refs[22:]
+        side, mid_side = (side_r, side_b), (mid_below, mid_above)
         for ref in (mc, mv, mw, kr, kb, vr, vb, wr, wb):
             clear_pads(ref)
         mid_span = (cx - MID_ROWS, 2 * cx + MID_ROWS)
@@ -682,8 +754,12 @@
             )
             put(mv, row, fresh)
             put(mw, row, mine * fresh)
+            below, above = mid_sides(mc, row)
+            mid_below[row] = mine + below
+            mid_above[row] = mine + above
         for rows_off, colour in ((1, 0), (2, 1), (3, 0), (4, 1)):
-            mid_half(shrink(mid_span, rows_off), colour, mc, mid_weight, mid_source, mv, mw)
+            part = shrink(mid_span, rows_off)
+            mid_half(part, colour, mc, mid_side, mid_weight, mid_source, mv, mw)
 
         first_mid = cx - FINE_ROWS // 2
         for cell in range(depth // 2):
@@ -701,12 +777,17 @@
             fresh = fine_black[row] + jnp.where(black > 0.0, lifted, 0.0)
             put(vb, row, fresh)
             put(wb, row, black * fresh)
+        for row in range(0, depth, 2):
+            for colour, mine, other in ((0, kr, kb), (1, kb, kr)):
+                sixth = beside(inner(other, row), inner(other, row + 1), colour)
+                side[colour][row] = inner(mine, row) + sixth[0]
+                side[colour][row + 1] = inner(mine, row + 1) + sixth[1]
         coeff, values, scaled = (kr, kb), (vr, vb), (wr, wb)
         weight = (fine_weight.at[0], fine_weight.at[1])
         source = (source_r, source_b)
         for rows_off, colour in ((1, 0), (2, 1), (3, 0), (4, 1)):
             span = shrink((0, depth), rows_off)
-            fine_half(span, colour, coeff, weight, source, values, scaled)
+            fine_half(span, colour, coeff, side, weight, source, values, scaled)
 
         own = pl.multiple_of(own_at + PAD, 8)
         span = slice(FINE_ROWS + 1, FINE_ROWS + 1 + bx)
@@ -729,9 +810,11 @@
             padded(mx, my),
             padded(mx, my),
             pltpu.VMEM((mx, my, LANES), F32),
+            pltpu.VMEM((mx, my, LANES), F32),
+            pltpu.VMEM((mx, my, LANES), F32),
             pltpu.VMEM((depth // 2, wy, LANES), F32),
         ]
-        + [pltpu.VMEM((depth, geo.fy, LANES), F32)] * 2
+        + [pltpu.VMEM((depth, geo.fy, LANES), F32)] * 4
         + [padded(depth, geo.fy)] * 6,
         room=12 if geo.swap else 40,
     )(lifted_low, *mids, *fines)
@@ -750,7 +833,8 @@
 
 
 def per_device(geo, old_slots, old_ids, coefficient):
-    center_k, *sent_k = widen_coefficient(geo, pack_coefficient(geo, coefficient))
+    own_k, coded_k = pack_coefficient(geo, coefficient)
+    center_k, *sent_k = widen_coefficient(geo, coded_k)
     parts = (center_k, *swaps("gx", geo.gx, *sent_k))
     sent_z = pack_ends(geo, parts)
     ends = swaps("gz", geo.gz, *sent_z)
@@ -759,7 +843,7 @@
     source = (center_f, *swaps("gx", geo.gx, *sent_f))
 
     payload, first_m, second_m, center_m, mid_coeff, mid_weight, *fines = way_down(
-        geo, parts, ends, source
+        geo, own_k, parts, ends, source
     )
     around = middle_neighbours(geo, center_m, first_m, second_m)
     lows = lax.all_to_all(payload, geo.low_axes, 0, 0, tiled=True)

time: 58.1 us -> 52.5 us (0.904)
  waiting for transfers between devices: 13 us -> 9.09 us
  Pallas kernels: 12.1 us -> 11 us
  starting transfers between devices: 21.7 us -> 21.1 us
    ppermute x1, waiting for transfers between devices: 3.5 us -> 0.01 us  [widen_coefficient(): other = lax.ppermute(own, 'gy', [(0, 1), (1, 0)])]
  transfers between devices with their start and end apart: 10 -> 10, of which waited for: 3 -> 2; matrix products, arithmetic and copies ran while one was open for 0% -> 0% of each run, Pallas kernels for 5% -> 4%
where the time goes in v5:
time: 52.5 us; the launch traced here: 52.1 us
  starting transfers between devices  21.1 us (40%)
  Pallas kernels  11 us (21%)
  blocking collectives  9.91 us (19%)
  waiting for transfers between devices  9.09 us (17%)
  local copies, waits for them, and re-layouts  0.99 us (2%)
    all_gather x1, blocking collectives, gather_source(): column = lax.all_gather(tag_slots(slots, ids), axes, axis=0, tiled=True)  9.91 us
    ppermute x4, starting transfers between devices, swaps(): lax.ppermute(first, axis, pairs(0))  8.09 us
    all_to_all x1, starting transfers between devices, per_device(): lows = lax.all_to_all(payload, geo.low_axes, 0, 0, tiled=True)  7.31 us
    all_to_all x1, waiting for transfers between devices, per_device(): lows = lax.all_to_all(payload, geo.low_axes, 0, 0, tiled=True)  5.88 us
    pallas_call x1, Pallas kernels, way_down(): call(kernel, [shape_f32(geo.low_peers, 2 * ly, LANES), slab, slab, shape_...  5.76 us
    ppermute x4, waiting for transfers between devices, swaps(): lax.ppermute(first, axis, pairs(0))  3.19 us
    ppermute x1, starting transfers between devices, widen_coefficient(): other = lax.ppermute(own, 'gy', [(0, 1), (1, 0)])  3.03 us
    ppermute x4, starting transfers between devices, swaps(): lax.ppermute(second, axis, pairs(1))  2.64 us
  transfers between devices with their start and end apart: 10, of which 2 were waited for; matrix products, arithmetic and copies ran while one was open for 0% of the time, Pallas kernels for 4%

profile of v5, /device:TPU:0, one launch (start us, length us, event | category | flops | bytes accessed | tf_op | source)
XLA Modules:
  0.0 52.1 jit_solution(1812249126422631924)
XLA Ops:
  0.0 0.0 copy-start
  0.0 0.9 %copy-done = f32[16,16,128]{2,1,0:T(8,128)S(1)} copy-done((f32[16,16,128]{2,1,0:T(8,128)S(1)}, f32[16,16,128]{2,1,0:T(8,128)}, u32[]{:S(2)}) %copy-start) | copy-done | bytes 131096
  0.9 0.0 copy-start.1
  0.9 0.4 shard_map.37
  1.3 0.0 copy-start.2
  1.3 3.0 %collective-permute-start = (s16[16,16,128]{2,1,0:T(8,128)(2,1)S(1)}, s16[16,16,128]{2,1,0:T(8,128)(2,1)S(1)}, u32[]{:S(2)}, u32[]{:S(2)}) collective-permute-start(s16[16,16,128]{2,1,0:T(8,128)(2,1)S(1)} %get-tuple-element.26.own_ref), channel_id=1, source_target_pairs={{0,4},{4,0},{1,5},{5,1},{2,6},{6,2},{3,7},{7,3},{8,12},{12,8},{9,1... | collective-permute-start | bytes 196616 | tf_op jit(solution)/shard_map/ppermute | solution.py:156
  4.3 0.0 copy-done.2
  4.3 0.1 copy.4.id_ref
  4.4 0.0 copy-done.1
  4.4 0.1 shard_map.40
  4.5 9.9 %all_gather.3.slot_ref = bf16[64,4224]{1,0:T(8,128)(2,1)S(1)} all-gather(bf16[8,4224]{1,0:T(8,128)(2,1)S(1)} %shard_map.40), channel_id=1, replica_groups=mesh['gx'=4,'gy'=2,'gz'=4] {'gy','gz'}, dimensions={0}, use_global_device_ids=true | all-gather | bytes 608256 | tf_op jit(solution)/shard_map/all_gather | solution.py:289
  14.4 1.1 %shard_map.41 = (bf16[2,16,32,128]{3,2,1,0:T(8,128)(2,1)S(1)}, bf16[2,12,32,128]{3,2,1,0:T(8,128)(2,1)S(1)}, bf16[2,12,32,128]{3,2,1,0:T(8,128)(2,1)S(1)}) custom-call(bf16[64,4224]{1,0:T(8,128)(2,1)S(1)} %all_gather.3.slot_ref), custom_call_target="tpu_custom_call" | custom-call | tf_op jit(solution)/shard_map/pallas_call | solution.py:265
  15.5 0.0 collective-permute-done.other_ref
  15.6 1.6 %collective-permute-start.1 = (s16[13,32,128]{2,1,0:T(8,128)(2,1)S(1)}, s16[13,32,128]{2,1,0:T(8,128)(2,1)S(1)}, u32[]{:S(2)}, u32[]{:S(2)}) collective-permute-start(s16[13,32,128]{2,1,0:T(8,128)(2,1)S(1)} %get-tuple-element.28), channel_id=1, source_target_pairs={{0,8},{16,24},{8,0},{24,16},{1,9},{17,25},{9,1},{25,17},{2,10},{18... | collective-permute-start | bytes 319496 | tf_op jit(solution)/shard_map/ppermute | solution.py:113
  17.2 0.7 %collective-permute-start.2 = (s16[13,32,128]{2,1,0:T(8,128)(2,1)S(1)}, s16[13,32,128]{2,1,0:T(8,128)(2,1)S(1)}, u32[]{:S(2)}, u32[]{:S(2)}) collective-permute-start(s16[13,32,128]{2,1,0:T(8,128)(2,1)S(1)} %get-tuple-element.29), channel_id=1, source_target_pairs={{8,16},{16,8},{9,17},{17,9},{10,18},{18,10},{11,19},{19,11},{12,20... | collective-permute-start | bytes 319496 | tf_op jit(solution)/shard_map/ppermute | solution.py:114
  17.9 4.5 %collective-permute-start.5 = (bf16[2,12,32,128]{3,2,1,0:T(8,128)(2,1)S(1)}, bf16[2,12,32,128]{3,2,1,0:T(8,128)(2,1)S(1)}, u32[]{:S(2)}, u32[]{:S(2)}) collective-permute-start(bf16[2,12,32,128]{3,2,1,0:T(8,128)(2,1)S(1)} %get-tuple-element.33), channel_id=1, source_target_pairs={{0,8},{16,24},{8,0},{24,16},{1,9},{17,25},{9,1},{25,17},{2,10},{18... | collective-permute-start | bytes 589832 | tf_op jit(solution)/shard_map/ppermute | solution.py:113
  22.3 0.7 %collective-permute-start.6 = (bf16[2,12,32,128]{3,2,1,0:T(8,128)(2,1)S(1)}, bf16[2,12,32,128]{3,2,1,0:T(8,128)(2,1)S(1)}, u32[]{:S(2)}, u32[]{:S(2)}) collective-permute-start(bf16[2,12,32,128]{3,2,1,0:T(8,128)(2,1)S(1)} %get-tuple-element.34), channel_id=1, source_target_pairs={{8,16},{16,8},{9,17},{17,9},{10,18},{18,10},{11,19},{19,11},{12,20... | collective-permute-start | bytes 589832 | tf_op jit(solution)/shard_map/ppermute | solution.py:114
  23.0 0.0 collective-permute-done.1.refs_1_.refs_2_
  23.0 0.0 collective-permute-done.2.refs_2_.refs_3_
  23.0 0.2 shard_map.39
  23.2 0.1 collective-permute-start.3
  23.3 0.7 %collective-permute-start.4 = (s16[11,32,128]{2,1,0:T(8,128)(2,1)S(1)}, s16[11,32,128]{2,1,0:T(8,128)(2,1)S(1)}, u32[]{:S(2)}, u32[]{:S(2)}) collective-permute-start(s16[11,32,128]{2,1,0:T(8,128)(2,1)S(1)} %get-tuple-element.31), channel_id=1, source_target_pairs={{1,2},{2,1},{5,6},{6,5},{9,10},{10,9},{13,14},{14,13},{17,18},{18,... | collective-permute-start | bytes 270344 | tf_op jit(solution)/shard_map/ppermute | solution.py:114
  24.0 3.2 %collective-permute-done.5.refs_7_ = bf16[2,12,32,128]{3,2,1,0:T(8,128)(2,1)S(1)} collective-permute-done((bf16[2,12,32,128]{3,2,1,0:T(8,128)(2,1)S(1)}, bf16[2,12,32,128]{3,2,1,0:T(8,128)(2,1)S(1)}, u32[]{:S(2)}, u32[]{:S(2)}) %collective-permute-start.5) | collective-permute-done | bytes 196640 | tf_op jit(solution)/shard_map/ppermute | solution.py:113
  27.2 0.0 collective-permute-done.6.refs_8_
  27.2 0.0 collective-permute-done.3.refs_4_
  27.2 0.0 collective-permute-done.4.refs_5_
  27.2 5.8 %shard_map.42 = (f32[16,16,128]{2,1,0:T(8,128)}, f32[2,6,16,128]{3,2,1,0:T(8,128)S(1)}, f32[2,6,16,128]{3,2,1,0:T(8,128)S(1)}, f32[2,8,16,128]{3,2,1,0:T(8,128)S...) custom-call(f32[16,16,128]{2,1,0:T(8,128)S(1)} %get-tuple-element.25, ...), custom_call_target="tpu_custom_call" | custom-call | tf_op jit(solution)/shard_map/pallas_call | solution.py:609
  33.0 7.3 %all-to-all-start = ((f32[16,16,128]{2,1,0:T(8,128)}), f32[16,16,128]{2,1,0:T(8,128)S(1)}, u32[]{:S(2)}, u32[]{:S(2)}) async-start(f32[16,16,128]{2,1,0:T(8,128)} %get-tuple-element.35), calls=%async_computation | async-start | bytes 262144 | tf_op jit(solution)/shard_map/all_to_all | solution.py:849
  40.3 1.9 %collective-permute-start.7 = (f32[2,6,16,128]{3,2,1,0:T(8,128)S(1)}, f32[2,6,16,128]{3,2,1,0:T(8,128)S(1)}, u32[]{:S(2)}, u32[]{:S(2)}) collective-permute-start(f32[2,6,16,128]{3,2,1,0:T(8,128)S(1)} %get-tuple-element.37), channel_id=1, source_target_pairs={{0,8},{16,24},{8,0},{24,16},{1,9},{17,25},{9,1},{25,17},{2,10},{18... | collective-permute-start | bytes 294920 | tf_op jit(solution)/shard_map/ppermute | solution.py:113
  42.2 0.7 %collective-permute-start.8 = (f32[2,6,16,128]{3,2,1,0:T(8,128)S(1)}, f32[2,6,16,128]{3,2,1,0:T(8,128)S(1)}, u32[]{:S(2)}, u32[]{:S(2)}) collective-permute-start(f32[2,6,16,128]{3,2,1,0:T(8,128)S(1)} %get-tuple-element.38), channel_id=1, source_target_pairs={{8,16},{16,8},{9,17},{17,9},{10,18},{18,10},{11,19},{19,11},{12,20... | collective-permute-start | bytes 294920 | tf_op jit(solution)/shard_map/ppermute | solution.py:114
  42.9 5.9 %all-to-all-done.low_ref = f32[16,16,128]{2,1,0:T(8,128)S(1)} async-done(((f32[16,16,128]{2,1,0:T(8,128)}), f32[16,16,128]{2,1,0:T(8,128)S(1)}, u32[]{:S(2)}, u32[]{:S(2)}) %all-to-all-start) | async-done | bytes 131104 | tf_op jit(solution)/shard_map/all_to_all | solution.py:849
  48.8 0.9 %shard_map.43.refs_0_ = f32[12,16,128]{2,1,0:T(8,128)S(1)} custom-call(f32[16,16,128]{2,1,0:T(8,128)S(1)} %all-to-all-done.low_ref), custom_call_target="tpu_custom_call" | custom-call | tf_op jit(solution)/shard_map/pallas_call | solution.py:710
  49.7 0.0 collective-permute-done.7.refs_2_
  49.7 0.0 collective-permute-done.8.refs_3_
  49.7 2.4 %shard_map.44 = f32[16,16,128]{2,1,0:T(8,128)} custom-call(f32[12,16,128]{2,1,0:T(8,128)S(1)} %shard_map.43.refs_0_, f32[2,8,16,128]{3,2,1,0:T(8,128)S(1)} %get-tuple-element.36.refs_1_, f32[2,6,16,128]{3,2,1,0:T(8,128)S(1)} %collective-permute-done.7.refs_2_, f32[2,6,16,128]{3,2,1,0:T(8,128)S(1)} %collective-permute-done.8.refs_3_, ...), custom_call_target="tpu_custom_call" | custom-call | tf_op jit(solution)/shard_map/pallas_call | solution.py:805
  (1 shorter events, 0.0 us)
Async XLA Ops:
  0.0 0.9 %copy-start = (f32[16,16,128]{2,1,0:T(8,128)S(1)}, f32[16,16,128]{2,1,0:T(8,128)}, u32[]{:S(2)}) copy-start(f32[16,16,128]{2,1,0:T(8,128)} %own_ref.1) | copy-start | bytes 393220
  0.9 3.5 %copy-start.1 = (bf16[1,1,8,4096]{3,2,1,0:T(8,128)(2,1)S(1)}, bf16[1,1,8,4096]{3,2,1,0:T(8,128)(2,1)}, u32[]{:S(2)}) copy-start(bf16[1,1,8,4096]{3,2,1,0:T(8,128)(2,1)} %param.4) | copy-start | bytes 196612
  1.3 3.0 %copy-start.2 = (s32[1,1,8]{2,1,0:T(1,128)S(1)}, s32[1,1,8]{2,1,0:T(1,128)}, u32[]{:S(2)}) copy-start(s32[1,1,8]{2,1,0:T(1,128)} %param.5) | copy-start | bytes 100
  1.3 14.2 %collective-permute-start = (s16[16,16,128]{2,1,0:T(8,128)(2,1)S(1)}, s16[16,16,128]{2,1,0:T(8,128)(2,1)S(1)}, u32[]{:S(2)}, u32[]{:S(2)}) collective-permute-start(s16[16,16,128]{2,1,0:T(8,128)(2,1)S(1)} %get-tuple-element.26.own_ref), channel_id=1, source_target_pairs={{0,4},{4,0},{1,5},{5,1},{2,6},{6,2},{3,7},{7,3},{8,12},{12,8},{9,1... | collective-permute-start | bytes 196616 | tf_op jit(solution)/shard_map/ppermute | solution.py:156
  15.6 7.4 %collective-permute-start.1 = (s16[13,32,128]{2,1,0:T(8,128)(2,1)S(1)}, s16[13,32,128]{2,1,0:T(8,128)(2,1)S(1)}, u32[]{:S(2)}, u32[]{:S(2)}) collective-permute-start(s16[13,32,128]{2,1,0:T(8,128)(2,1)S(1)} %get-tuple-element.28), channel_id=1, source_target_pairs={{0,8},{16,24},{8,0},{24,16},{1,9},{17,25},{9,1},{25,17},{2,10},{18... | collective-permute-start | bytes 319496 | tf_op jit(solution)/shard_map/ppermute | solution.py:113
  17.2 5.8 %collective-permute-start.2 = (s16[13,32,128]{2,1,0:T(8,128)(2,1)S(1)}, s16[13,32,128]{2,1,0:T(8,128)(2,1)S(1)}, u32[]{:S(2)}, u32[]{:S(2)}) collective-permute-start(s16[13,32,128]{2,1,0:T(8,128)(2,1)S(1)} %get-tuple-element.29), channel_id=1, source_target_pairs={{8,16},{16,8},{9,17},{17,9},{10,18},{18,10},{11,19},{19,11},{12,20... | collective-permute-start | bytes 319496 | tf_op jit(solution)/shard_map/ppermute | solution.py:114
  17.9 9.3 %collective-permute-start.5 = (bf16[2,12,32,128]{3,2,1,0:T(8,128)(2,1)S(1)}, bf16[2,12,32,128]{3,2,1,0:T(8,128)(2,1)S(1)}, u32[]{:S(2)}, u32[]{:S(2)}) collective-permute-start(bf16[2,12,32,128]{3,2,1,0:T(8,128)(2,1)S(1)} %get-tuple-element.33), channel_id=1, source_target_pairs={{0,8},{16,24},{8,0},{24,16},{1,9},{17,25},{9,1},{25,17},{2,10},{18... | collective-permute-start | bytes 589832 | tf_op jit(solution)/shard_map/ppermute | solution.py:113
  22.3 4.9 %collective-permute-start.6 = (bf16[2,12,32,128]{3,2,1,0:T(8,128)(2,1)S(1)}, bf16[2,12,32,128]{3,2,1,0:T(8,128)(2,1)S(1)}, u32[]{:S(2)}, u32[]{:S(2)}) collective-permute-start(bf16[2,12,32,128]{3,2,1,0:T(8,128)(2,1)S(1)} %get-tuple-element.34), channel_id=1, source_target_pairs={{8,16},{16,8},{9,17},{17,9},{10,18},{18,10},{11,19},{19,11},{12,20... | collective-permute-start | bytes 589832 | tf_op jit(solution)/shard_map/ppermute | solution.py:114
  23.2 3.9 %collective-permute-start.3 = (s16[11,32,128]{2,1,0:T(8,128)(2,1)S(1)}, s16[11,32,128]{2,1,0:T(8,128)(2,1)S(1)}, u32[]{:S(2)}, u32[]{:S(2)}) collective-permute-start(s16[11,32,128]{2,1,0:T(8,128)(2,1)S(1)} %get-tuple-element.30), channel_id=1, source_target_pairs={{0,1},{2,3},{1,0},{3,2},{4,5},{6,7},{5,4},{7,6},{8,9},{10,11},{9,8... | collective-permute-start | bytes 270344 | tf_op jit(solution)/shard_map/ppermute | solution.py:113
  23.3 3.9 %collective-permute-start.4 = (s16[11,32,128]{2,1,0:T(8,128)(2,1)S(1)}, s16[11,32,128]{2,1,0:T(8,128)(2,1)S(1)}, u32[]{:S(2)}, u32[]{:S(2)}) collective-permute-start(s16[11,32,128]{2,1,0:T(8,128)(2,1)S(1)} %get-tuple-element.31), channel_id=1, source_target_pairs={{1,2},{2,1},{5,6},{6,5},{9,10},{10,9},{13,14},{14,13},{17,18},{18,... | collective-permute-start | bytes 270344 | tf_op jit(solution)/shard_map/ppermute | solution.py:114
  33.0 15.8 %all-to-all-start = ((f32[16,16,128]{2,1,0:T(8,128)}), f32[16,16,128]{2,1,0:T(8,128)S(1)}, u32[]{:S(2)}, u32[]{:S(2)}) async-start(f32[16,16,128]{2,1,0:T(8,128)} %get-tuple-element.35), calls=%async_computation | async-start | bytes 262144 | tf_op jit(solution)/shard_map/all_to_all | solution.py:849
  40.3 9.4 %collective-permute-start.7 = (f32[2,6,16,128]{3,2,1,0:T(8,128)S(1)}, f32[2,6,16,128]{3,2,1,0:T(8,128)S(1)}, u32[]{:S(2)}, u32[]{:S(2)}) collective-permute-start(f32[2,6,16,128]{3,2,1,0:T(8,128)S(1)} %get-tuple-element.37), channel_id=1, source_target_pairs={{0,8},{16,24},{8,0},{24,16},{1,9},{17,25},{9,1},{25,17},{2,10},{18... | collective-permute-start | bytes 294920 | tf_op jit(solution)/shard_map/ppermute | solution.py:113
  42.2 7.5 %collective-permute-start.8 = (f32[2,6,16,128]{3,2,1,0:T(8,128)S(1)}, f32[2,6,16,128]{3,2,1,0:T(8,128)S(1)}, u32[]{:S(2)}, u32[]{:S(2)}) collective-permute-start(f32[2,6,16,128]{3,2,1,0:T(8,128)S(1)} %get-tuple-element.38), channel_id=1, source_target_pairs={{8,16},{16,8},{9,17},{17,9},{10,18},{18,10},{11,19},{19,11},{12,20... | collective-permute-start | bytes 294920 | tf_op jit(solution)/shard_map/ppermute | solution.py:114
